TPU v7x, 8 devices: a whole 2x2x1 slice. The times are simulated.
8 devices in a mesh: sp: 8 (over z, y, x, core).
Axes of the slice: x: 2, y: 2, z: 1, core: 2. Of those that a mesh axis runs over, the one named last changes fastest.
Arguments:
- hidden: bfloat16 [32, 512, 1024], P(None, 'sp')
- norm_gain: float32 [1024], replicated
- w_q: bfloat16 [1024, 2048], replicated
- w_k: bfloat16 [1024, 1024], replicated
- w_v: bfloat16 [1024, 1024], replicated
- q_gain: float32 [128], replicated
- k_gain: float32 [128], replicated
- w_o: bfloat16 [2048, 1024], replicated
- d_out: bfloat16 [32, 512, 1024], P(None, 'sp')
Outputs:
- output 1: bfloat16 [32, 512, 1024], P(None, 'sp')
- output 2: bfloat16 [32, 512, 1024], P(None, 'sp')
- output 3: float32 [1024, 2048], replicated
- output 4: float32 [1024, 1024], replicated
- output 5: float32 [1024, 1024], replicated
- output 6: float32 [2048, 1024], replicated
- output 7: float32 [1024], replicated
- output 8: float32 [128], replicated
- output 9: float32 [128], replicated
All inputs are finite; a program needn't handle non-finite values.
Results may differ from a plain program's by a relative error of at most 0.0177018.
Values are sent between devices in bfloat16 or wider.
A program may use at most 1 GiB of HBM per device.

v0:
```python
import math
import jax
import jax.numpy as jnp
from jax import lax
from jax.sharding import PartitionSpec as P

ROPE_BASE = 1000000.0
NORM_EPS = 1e-6


def rms_scale(values, gain):
    return values * lax.rsqrt(jnp.mean(values * values, axis=-1, keepdims=True) + NORM_EPS) * gain


def rope_tables(positions, head_dim):
    half_dim = head_dim // 2
    inv_freq = jnp.exp(jnp.arange(half_dim).astype(jnp.float32) * (-2.0 * math.log(ROPE_BASE) / head_dim))
    angles = positions[:, None] * inv_freq[None, :]
    return jnp.cos(angles), jnp.sin(angles)


def qk_post(raw, gain, cos_tab, sin_tab):
    normed = rms_scale(raw, gain)
    half_dim = raw.shape[-1] // 2
    first = normed[..., :half_dim]
    second = normed[..., half_dim:]
    cos_b = cos_tab[None, :, None, :]
    sin_b = sin_tab[None, :, None, :]
    return jnp.concatenate([first * cos_b - second * sin_b, second * cos_b + first * sin_b], axis=-1)


def core_forward(q_part, k_part, v_part):
    n_batch, n_pos, q_heads, head_dim = q_part.shape
    kv_heads = k_part.shape[2]
    q_grouped = q_part.reshape(n_batch, n_pos, kv_heads, q_heads // kv_heads, head_dim)
    scores = jnp.einsum('bqkgd,bskd->bkgqs', q_grouped, k_part, preferred_element_type=jnp.float32) * head_dim ** -0.5
    causal = lax.broadcasted_iota(jnp.int32, (n_pos, n_pos), 0) >= lax.broadcasted_iota(jnp.int32, (n_pos, n_pos), 1)
    scores = jnp.where(causal, scores, -1e30)
    attn_prob = jax.nn.softmax(scores, axis=-1)
    prob_bf = attn_prob.astype(jnp.bfloat16)
    out_heads = jnp.einsum('bkgqs,bskd->bqkgd', prob_bf, v_part, preferred_element_type=jnp.float32)
    return out_heads.astype(jnp.bfloat16).reshape(n_batch, n_pos, q_heads, head_dim), attn_prob, prob_bf


def core_backward(q_part, k_part, v_part, attn_prob, prob_bf, d_heads):
    n_batch, n_pos, q_heads, head_dim = q_part.shape
    kv_heads = k_part.shape[2]
    grouped_shape = (n_batch, n_pos, kv_heads, q_heads // kv_heads, head_dim)
    q_grouped = q_part.reshape(grouped_shape)
    d_grouped = d_heads.reshape(grouped_shape)
    d_prob = jnp.einsum('bqkgd,bskd->bkgqs', d_grouped, v_part, preferred_element_type=jnp.float32)
    d_scores = attn_prob * (d_prob - jnp.sum(attn_prob * d_prob, axis=-1, keepdims=True))
    d_scores = (d_scores * head_dim ** -0.5).astype(jnp.bfloat16)
    d_q = jnp.einsum('bkgqs,bskd->bqkgd', d_scores, k_part, preferred_element_type=jnp.float32)
    d_k = jnp.einsum('bkgqs,bqkgd->bskd', d_scores, q_grouped, preferred_element_type=jnp.float32)
    d_v = jnp.einsum('bkgqs,bqkgd->bskd', prob_bf, d_grouped, preferred_element_type=jnp.float32)
    return d_q.astype(jnp.bfloat16).reshape(n_batch, n_pos, q_heads, head_dim), d_k, d_v


def solution(mesh):
    n_dev = mesh.shape['sp']
    seq_spec = P(None, 'sp', None)
    replicated = P()

    def local_step(hidden, norm_gain, w_q, w_k, w_v, q_gain, k_gain, w_o, d_out):
        n_batch, seq_loc = hidden.shape[0], hidden.shape[1]
        head_dim = q_gain.shape[0]
        q_heads = w_q.shape[1] // head_dim
        kv_heads = w_k.shape[1] // head_dim
        copies = max(n_dev // kv_heads, 1)
        q_shape = (n_batch, seq_loc, q_heads, head_dim)
        kv_shape = (n_batch, seq_loc, kv_heads, head_dim)
        row_start = lax.axis_index('sp') * seq_loc
        positions = (row_start + jnp.arange(seq_loc)).astype(jnp.float32)
        cos_tab, sin_tab = rope_tables(positions, head_dim)
        hidden_f = hidden.astype(jnp.float32)
        normed_f, norm_back = jax.vjp(rms_scale, hidden_f, norm_gain)
        normed = normed_f.astype(jnp.bfloat16)
        q_raw = jnp.einsum('bsd,de->bse', normed, w_q, preferred_element_type=jnp.float32).astype(jnp.bfloat16)
        k_raw = jnp.einsum('bsd,de->bse', normed, w_k, preferred_element_type=jnp.float32).astype(jnp.bfloat16)
        v_raw = jnp.einsum('bsd,de->bse', normed, w_v, preferred_element_type=jnp.float32).astype(jnp.bfloat16)

        def post_both(q_in, k_in, q_scale, k_scale):
            return qk_post(q_in, q_scale, cos_tab, sin_tab), qk_post(k_in, k_scale, cos_tab, sin_tab)

        (q_rot, k_rot), post_back = jax.vjp(post_both, q_raw.astype(jnp.float32).reshape(q_shape), k_raw.astype(jnp.float32).reshape(kv_shape), q_gain, k_gain)
        k_rep = jnp.repeat(k_rot.astype(jnp.bfloat16), copies, axis=2)
        v_rep = jnp.repeat(v_raw.reshape(kv_shape), copies, axis=2)
        q_here = lax.all_to_all(q_rot.astype(jnp.bfloat16), 'sp', 2, 1, tiled=True)
        k_here = lax.all_to_all(k_rep, 'sp', 2, 1, tiled=True)
        v_here = lax.all_to_all(v_rep, 'sp', 2, 1, tiled=True)
        o_here, attn_prob, prob_bf = core_forward(q_here, k_here, v_here)
        attn = lax.all_to_all(o_here, 'sp', 1, 2, tiled=True).reshape(n_batch, seq_loc, q_heads * head_dim)
        y_out = (hidden_f + jnp.einsum('bse,ed->bsd', attn, w_o, preferred_element_type=jnp.float32)).astype(jnp.bfloat16)
        d_attn = jnp.einsum('bsd,ed->bse', d_out, w_o, preferred_element_type=jnp.float32).astype(jnp.bfloat16)
        d_wo = jnp.einsum('bse,bsd->ed', attn, d_out, preferred_element_type=jnp.float32)
        d_o_here = lax.all_to_all(d_attn.reshape(q_shape), 'sp', 2, 1, tiled=True)
        dq_here, dk_here, dv_here = core_backward(q_here, k_here, v_here, attn_prob, prob_bf, d_o_here)
        dq_loc = lax.all_to_all(dq_here, 'sp', 1, 2, tiled=True)
        dk_parts = lax.all_to_all(dk_here.astype(jnp.bfloat16), 'sp', 1, 2, tiled=True)
        dv_parts = lax.all_to_all(dv_here.astype(jnp.bfloat16), 'sp', 1, 2, tiled=True)
        split_shape = (n_batch, seq_loc, kv_heads, copies, head_dim)
        dk_sum = jnp.sum(dk_parts.reshape(split_shape).astype(jnp.float32), axis=3).astype(jnp.bfloat16)
        dv_sum = jnp.sum(dv_parts.reshape(split_shape).astype(jnp.float32), axis=3).astype(jnp.bfloat16)
        dq_raw_f, dk_raw_f, d_qgain, d_kgain = post_back((dq_loc.astype(jnp.float32), dk_sum.astype(jnp.float32)))
        dq_raw = dq_raw_f.astype(jnp.bfloat16).reshape(n_batch, seq_loc, q_heads * head_dim)
        dk_raw = dk_raw_f.astype(jnp.bfloat16).reshape(n_batch, seq_loc, kv_heads * head_dim)
        dv_raw = dv_sum.reshape(n_batch, seq_loc, kv_heads * head_dim)
        d_wq = jnp.einsum('bsd,bse->de', normed, dq_raw, preferred_element_type=jnp.float32)
        d_wk = jnp.einsum('bsd,bse->de', normed, dk_raw, preferred_element_type=jnp.float32)
        d_wv = jnp.einsum('bsd,bse->de', normed, dv_raw, preferred_element_type=jnp.float32)
        d_normed = (jnp.einsum('bse,de->bsd', dq_raw, w_q, preferred_element_type=jnp.float32) + jnp.einsum('bse,de->bsd', dk_raw, w_k, preferred_element_type=jnp.float32) + jnp.einsum('bse,de->bsd', dv_raw, w_v, preferred_element_type=jnp.float32))
        dx_f, d_ngain = norm_back(d_normed)
        d_hidden = (d_out.astype(jnp.float32) + dx_f).astype(jnp.bfloat16)
        return (y_out, d_hidden, lax.psum(d_wq, 'sp'), lax.psum(d_wk, 'sp'), lax.psum(d_wv, 'sp'), lax.psum(d_wo, 'sp'), lax.psum(d_ngain, 'sp'), lax.psum(d_qgain, 'sp'), lax.psum(d_kgain, 'sp'))

    return jax.shard_map(local_step, mesh=mesh, in_specs=(seq_spec, replicated, replicated, replicated, replicated, replicated, replicated, replicated, seq_spec), out_specs=(seq_spec, seq_spec, replicated, replicated, replicated, replicated, replicated, replicated, replicated), check_vma=False)
```

profile of v0, /device:TPU:0, one launch (start us, length us, event | category | flops | bytes accessed | tf_op | source)
XLA Modules:
  0.0 1268.9 jit_solution(10873981674641501719)
XLA Ops:
  129.5 15.0 %all-to-all-done = bf16[32,64,8,128]{3,1,0,2:T(8,128)(2,1)} async-done(((bf16[32,64,8,128]{3,1,0,2:T(8,128)(2,1)}), bf16[32,64,8,128]{3,1,0,2:T(8,128)(2,1)}, u32[]{:S(2)}, u32[]{:S(2)}) %all-to-all-start) | async-done | bytes 4194336 | tf_op jit(solution)/shard_map/all_to_all | solution.py:91
  148.3 14.0 %convert_bitcast_fusion.3 = bf16[32,8,16,8,128]{4,3,2,1,0:T(8,128)(2,1)} fusion(bf16[32,64,1024]{2,1,0:T(8,128)(2,1)} %param.17, bf16[2048,1024]{1,0:T(8,128)(2,1)} %param.16), kind=kOutput, calls=%fused_computation.72 | convolution fusion | flops 8594128896 | bytes 16777216 | tf_op jit(solution)/shard_map/bsd,ed->bse/dot_general | solution.py:95
  171.4 70.8 %all-to-all-done.2 = bf16[32,64,16,128]{3,1,0,2:T(8,128)(2,1)} async-done(((bf16[32,64,16,128]{3,1,0,2:T(8,128)(2,1)}), bf16[32,64,16,128]{3,1,0,2:T(8,128)(2,1)}, u32[]{:S(2)}, u32[]{:S(2)}) %all-to-all-start.2) | async-done | bytes 8388640 | tf_op jit(solution)/shard_map/all_to_all | solution.py:89
  267.4 72.9 %all-to-all-done.4 = bf16[32,64,16,128]{3,1,0,2:T(8,128)(2,1)} async-done(((bf16[32,64,16,128]{3,1,0,2:T(8,128)(2,1)}), bf16[32,64,16,128]{3,1,0,2:T(8,128)(2,1)}, u32[]{:S(2)}, u32[]{:S(2)}) %all-to-all-start.4) | async-done | bytes 8388640 | tf_op jit(solution)/shard_map/all_to_all | solution.py:97
  350.0 27.7 %fusion.6 = (f32[32,2,512]{2,1,0:T(2,128)S(1)}, f32[32,512,512,2]{2,1,3,0:T(8,128)}) fusion(pred[512,512]{0,1:T(8,128)(4,1)S(1)} %iota_compare_fusion, bf16[32,512,128,1]{2,1,3,0:T(8,128)(2,1)} %bitcast.274, bf16[32,512,2,128]{3,1,2,0:T(8,128)(2,1)} %bitcast.271), kind=kOutput, calls=%fused_computation.10 | convolution fusion | flops 4345266176 | bytes 80084992 | tf_op jit(solution)/shard_map/bqkgd,bskd->bkgqs/dot_general | solution.py:36
  377.7 21.7 %fusion.5 = f32[32,2,512]{2,1,0:T(2,128)S(1)} fusion(f32[32,512,512,2]{2,1,3,0:T(8,128)} %get-tuple-element.33, f32[32,2,512]{2,1,0:T(2,128)S(1)} %get-tuple-element.32, pred[512,512]{0,1:T(8,128)(4,1)S(1)} %iota_compare_fusion), kind=kLoop, calls=%fused_computation.9 | loop fusion | flops 67076096 | bytes 67633152 | tf_op jit(solution)/shard_map/reduce_sum | solution.py:39
  399.3 49.3 %fusion = (f32[32,2,512]{2,1,0:T(2,128)S(1)}, f32[32,512,512,2]{2,1,3,0:T(8,128)}) fusion(f32[32,2,512]{2,1,0:T(2,128)S(1)} %fusion.5, f32[32,2,512]{2,1,0:T(2,128)S(1)} %get-tuple-element.32, f32[32,512,512,2]{2,1,3,0:T(8,128)} %get-tuple-element.33, pred[512,512]{0,1:T(8,128)(4,1)S(1)} %iota_compare_fusion, bf16[32,512,128,1]{2,1,3,0:T(8,128)(2,1)} %bitcast.287, ...), kind=kOutput, calls=%fused_computation.3 | convolution fusion | flops 4395597824 | bytes 147456000 | tf_op jit(solution)/shard_map/bqkgd,bskd->bkgqs/dot_general | solution.py:51
  448.6 53.6 %fusion.7 = bf16[32,2,512,512]{2,3,1,0:T(8,128)(2,1)} fusion(f32[32,512,512,2]{2,1,3,0:T(8,128)} %get-tuple-element.35, f32[32,2,512]{2,1,0:T(2,128)S(1)} %get-tuple-element.34, f32[32,2,512]{2,1,0:T(2,128)S(1)} %fusion.5, f32[32,2,512]{2,1,0:T(2,128)S(1)} %get-tuple-element.32, f32[32,512,512,2]{2,1,3,0:T(8,128)} %get-tuple-element.33, ...), kind=kLoop, calls=%fused_computation.11 | loop fusion | flops 134217728 | bytes 168427520 | tf_op jit(solution)/shard_map/reshape.16
  502.2 19.8 %fusion.42 = bf16[32,512,1,128]{1,3,0,2:T(8,128)(2,1)} fusion(bf16[32,512,2,128]{3,1,2,0:T(8,128)(2,1)} %bitcast.272, bf16[32,2,512,512]{2,3,1,0:T(8,128)(2,1)} %fusion.7), kind=kOutput, calls=%fused_computation.82 | convolution fusion | flops 4297064448 | bytes 46137344 | tf_op jit(solution)/shard_map/bkgqs,bqkgd->bskd/dot_general | solution.py:55
  533.1 30.7 %fusion.43 = bf16[32,512,1,128]{1,3,0,2:T(8,128)(2,1)} fusion(bf16[32,512,2,128]{3,1,2,0:T(8,128)(2,1)} %bitcast.286, f32[32,2,512]{2,1,0:T(2,128)S(1)} %fusion.5, f32[32,2,512]{2,1,0:T(2,128)S(1)} %get-tuple-element.32, f32[32,512,512,2]{2,1,3,0:T(8,128)} %get-tuple-element.33, pred[512,512]{0,1:T(8,128)(4,1)S(1)} %iota_compare_fusion), kind=kOutput, calls=%fused_computation.83 | convolution fusion | flops 4380950528 | bytes 80216064 | tf_op jit(solution)/shard_map/bkgqs,bqkgd->bskd/dot_general | solution.py:56
  585.6 17.8 %convert_bitcast_fusion.2 = bf16[32,512,2,128]{1,3,2,0:T(8,128)(2,1)} fusion(bf16[32,512,128,1]{2,1,3,0:T(8,128)(2,1)} %bitcast.275, bf16[32,2,512,512]{2,3,1,0:T(8,128)(2,1)} %fusion.7), kind=kOutput, calls=%fused_computation.71 | convolution fusion | flops 4299161600 | bytes 46137344 | tf_op jit(solution)/shard_map/bkgqs,bskd->bqkgd/dot_general | solution.py:54
  603.4 21.2 %copy.204 = bf16[32,512,2,128]{3,2,0,1:T(2,128)(2,1)} copy(bf16[32,512,2,128]{1,3,2,0:T(8,128)(2,1)} %convert_bitcast_fusion.2) | data formatting | bytes 16777216 | tf_op jit(solution)/shard_map/reshape | solution.py:57
  638.3 29.5 %convert_bitcast_fusion.4 = bf16[32,512,2,128]{1,3,2,0:T(8,128)(2,1)} fusion(bf16[32,512,128,1]{2,1,3,0:T(8,128)(2,1)} %bitcast.288, f32[32,2,512]{2,1,0:T(2,128)S(1)} %fusion.5, f32[32,2,512]{2,1,0:T(2,128)S(1)} %get-tuple-element.32, f32[32,512,512,2]{2,1,3,0:T(8,128)} %get-tuple-element.33, pred[512,512]{0,1:T(8,128)(4,1)S(1)} %iota_compare_fusion), kind=kOutput, calls=%fused_computation.73 | convolution fusion | flops 4383047680 | bytes 80216064 | tf_op jit(solution)/shard_map/bkgqs,bskd->bqkgd/dot_general | solution.py:41
  667.9 21.6 %copy.197 = bf16[32,512,2,128]{3,2,0,1:T(2,128)(2,1)} copy(bf16[32,512,2,128]{1,3,2,0:T(8,128)(2,1)} %convert_bitcast_fusion.4) | data formatting | bytes 16777216 | tf_op jit(solution)/shard_map/reshape | solution.py:42
  762.7 16.5 %copy.205 = bf16[32,512,2,128]{3,1,2,0:T(8,128)(2,1)} copy(bf16[32,512,2,128]{3,2,0,1:T(2,128)(2,1)} %all-to-all-done.5) | data formatting | bytes 16777216 | tf_op jit(solution)/shard_map/all_to_all | solution.py:99
  802.7 25.0 %multiply_add_fusion.1 = (f32[32,64,16,64]{3,1,2,0:T(8,128)}, f32[32,64,16,64]{3,1,2,0:T(8,128)}) fusion(f32[32,64,16,128]{3,1,2,0:T(8,128)} %bitcast.267, f32[64,64]{1,0:T(8,128)S(1)} %copy-done.24, f32[64,64]{1,0:T(8,128)S(1)} %copy-done.22), kind=kLoop, calls=%fused_computation.29 | loop fusion | flops 14680064 | bytes 33587200 | tf_op jit(solution)/shard_map/transpose(jvp())/add_any | solution.py:29
  829.7 18.2 %multiply_reduce_fusion = (f32[128]{0:T(128)S(1)}, f32[32,64,16]{1,2,0:T(8,128)S(1)}) fusion(f32[32,64,16]{1,2,0:T(8,128)S(1)} %copy-done.10, f32[32,64,16,64]{3,1,2,0:T(8,128)} %get-tuple-element.23, f32[32,64,16,64]{3,1,2,0:T(8,128)} %get-tuple-element.22, f32[128]{0:T(128)S(1)} %copy-done.32, f32[32,64,2048]{2,1,0:T(8,128)S(1)} %bitcast.266), kind=kLoop, calls=%fused_computation.26 | loop fusion | flops 29327232 | bytes 33817600 | tf_op jit(solution)/shard_map/transpose(jvp())/reduce_sum | solution.py:12
  848.1 20.1 %fusion.27 = bf16[32,16,8,8,128]{4,3,2,1,0:T(8,128)(2,1)} fusion(f32[32,64,16]{1,2,0:T(8,128)S(1)} %multiply_multiply_fusion, f32[128]{0:T(128)S(1)} %copy-done.32, f32[32,64,16]{1,2,0:T(8,128)S(1)} %copy-done.10, f32[32,64,16,64]{3,1,2,0:T(8,128)} %get-tuple-element.23, f32[32,64,16,64]{3,1,2,0:T(8,128)} %get-tuple-element.22, f32[32,64,2048]{2,1,0:T(8,128)} %copy-done.1), kind=kLoop, calls=%fused_computation.50 | loop fusion | flops 29360128 | bytes 42205696
  882.1 16.5 %copy.198 = bf16[32,512,2,128]{3,1,2,0:T(8,128)(2,1)} copy(bf16[32,512,2,128]{3,2,0,1:T(2,128)(2,1)} %all-to-all-done.3) | data formatting | bytes 16777216 | tf_op jit(solution)/shard_map/all_to_all | solution.py:93
  898.6 16.2 %copy.199 = bf16[32,64,8,2,128]{4,3,2,1,0:T(2,128)(2,1)} copy(bf16[32,64,8,2,128]{4,1,2,3,0:T(8,128)(2,1)} %bitcast.278) | data formatting | bytes 16777216 | tf_op jit(solution)/shard_map/all_to_all | solution.py:93
  914.9 14.4 %reshape.272 = bf16[32,64,2048]{2,1,0:T(8,128)(2,1)} reshape(bf16[32,64,8,2,128]{4,3,2,1,0:T(2,128)(2,1)} %copy.199) | data formatting | bytes 16777216 | tf_op jit(solution)/shard_map/reshape | solution.py:93
  929.3 14.8 %convolution_bitcast_fusion = f32[2048,1024]{1,0:T(8,128)} fusion(bf16[32,64,2048]{2,1,0:T(8,128)(2,1)} %reshape.272, bf16[32,64,1024]{2,1,0:T(8,128)(2,1)} %param.17), kind=kOutput, calls=%fused_computation.81 | convolution fusion | flops 8589934592 | bytes 20971520 | tf_op jit(solution)/shard_map/bse,bsd->ed/dot_general | solution.py:96
  980.3 24.3 %all-reduce.4 = (f32[1024]{0:T(1024)}, f32[128]{0:T(128)}, f32[128]{0:T(128)}) all-reduce(f32[1024]{0:T(1024)S(1)} %get-tuple-element.13, f32[128]{0:T(128)S(1)} %get-tuple-element.9, f32[128]{0:T(128)S(1)} %copy-done.35), channel_id=1, replica_groups=mesh['sp'=8] {'sp'}, use_global_device_ids=true, to_apply=%region_14.15 | all-reduce | flops 1280 | bytes 10240 | tf_op jit(solution)/shard_map/psum | solution.py:115
  1027.1 215.2 %all-reduce.8.cloned.1.call-done = (f32[1024,2048]{1,0:T(8,128)}, f32[1024,1024]{1,0:T(8,128)}, f32[1024,1024]{1,0:T(8,128)}, f32[2048,1024]{1,0:T(8,128)}) async-done(((f32[1024,2048]{1,0:T(8,128)}, f32[1024,1024]{1,0:T(8,128)}, f32[1024,1024]{1,0:T(8,128)}, f32[2048,1024]{1,0:T(8,128)}), (f32[1024,2048]{1,0:T(8,128)}, f32[1024,1024]{1,0:T(8,128)}, f32[1024,1024]{1,0:T(8,128)}, ...) | async-done | bytes 25165840 | tf_op jit(solution)/shard_map/psum | solution.py:115
  (168 shorter events, 406.8 us)
Async XLA Ops:
  7.2 67.0 %copy-start = (bf16[1024,1024]{1,0:T(8,128)(2,1)S(1)}, bf16[1024,1024]{1,0:T(8,128)(2,1)}, u32[]{:S(2)}) copy-start(bf16[1024,1024]{1,0:T(8,128)(2,1)} %param.13) | copy-start | bytes 6291460
  11.0 63.2 %copy-start.27 = (f32[32,64]{1,0:T(8,128)}, f32[32,64]{1,0:T(8,128)S(1)}, u32[]{:S(2)}) copy-start(f32[32,64]{1,0:T(8,128)S(1)} %fusion.69) | copy-start | bytes 24580
  24.7 78.5 %copy-start.21 = (f32[64,64]{1,0:T(8,128)}, f32[64,64]{1,0:T(8,128)S(1)}, u32[]{:S(2)}) copy-start(f32[64,64]{1,0:T(8,128)S(1)} %get-tuple-element.30) | copy-start | bytes 49156
  24.7 78.5 %copy-start.23 = (f32[64,64]{1,0:T(8,128)}, f32[64,64]{1,0:T(8,128)S(1)}, u32[]{:S(2)}) copy-start(f32[64,64]{1,0:T(8,128)S(1)} %get-tuple-element.31) | copy-start | bytes 49156
  38.5 53.6 %all-to-all-start.1 = ((bf16[32,64,8,128]{3,1,0,2:T(8,128)(2,1)}), bf16[32,64,8,128]{3,1,0,2:T(8,128)(2,1)}, u32[]{:S(2)}, u32[]{:S(2)}) async-start(bf16[32,64,8,128]{3,1,0,2:T(8,128)(2,1)} %copy.189), calls=%async_computation.1 | async-start | bytes 8388608 | tf_op jit(solution)/shard_map/all_to_all | solution.py:90
  81.5 14.0 %copy-start.31 = (f32[128]{0:T(128)S(1)}, f32[128]{0:T(128)}, u32[]{:S(2)}) copy-start(f32[128]{0:T(128)} %param.14) | copy-start | bytes 1540
  92.0 52.5 %all-to-all-start = ((bf16[32,64,8,128]{3,1,0,2:T(8,128)(2,1)}), bf16[32,64,8,128]{3,1,0,2:T(8,128)(2,1)}, u32[]{:S(2)}, u32[]{:S(2)}) async-start(bf16[32,64,8,128]{3,1,0,2:T(8,128)(2,1)} %bitcast.281), calls=%async_computation | async-start | bytes 8388608 | tf_op jit(solution)/shard_map/all_to_all | solution.py:91
  144.6 97.7 %all-to-all-start.2 = ((bf16[32,64,16,128]{3,1,0,2:T(8,128)(2,1)}), bf16[32,64,16,128]{3,1,0,2:T(8,128)(2,1)}, u32[]{:S(2)}, u32[]{:S(2)}) async-start(bf16[32,64,16,128]{3,1,0,2:T(8,128)(2,1)} %copy.193), calls=%async_computation.2 | async-start | bytes 16777216 | tf_op jit(solution)/shard_map/all_to_all | solution.py:89
  242.2 98.1 %all-to-all-start.4 = ((bf16[32,64,16,128]{3,1,0,2:T(8,128)(2,1)}), bf16[32,64,16,128]{3,1,0,2:T(8,128)(2,1)}, u32[]{:S(2)}, u32[]{:S(2)}) async-start(bf16[32,64,16,128]{3,1,0,2:T(8,128)(2,1)} %bitcast.277), calls=%async_computation.4 | async-start | bytes 16777216 | tf_op jit(solution)/shard_map/all_to_all | solution.py:97
  529.8 52.3 %all-to-all-start.6 = ((bf16[32,512,1,128]{3,0,2,1:T(8,128)(2,1)}), bf16[32,512,1,128]{3,0,2,1:T(8,128)(2,1)}, u32[]{:S(2)}, u32[]{:S(2)}) async-start(bf16[32,512,1,128]{3,0,2,1:T(8,128)(2,1)} %copy.212), calls=%async_computation.6 | async-start | bytes 8388608 | tf_op jit(solution)/shard_map/all_to_all | solution.py:100
  582.1 52.5 %all-to-all-start.7 = ((bf16[32,512,1,128]{3,0,2,1:T(8,128)(2,1)}), bf16[32,512,1,128]{3,0,2,1:T(8,128)(2,1)}, u32[]{:S(2)}, u32[]{:S(2)}) async-start(bf16[32,512,1,128]{3,0,2,1:T(8,128)(2,1)} %copy.219), calls=%async_computation.7 | async-start | bytes 8388608 | tf_op jit(solution)/shard_map/all_to_all | solution.py:101
  634.6 124.1 %all-to-all-start.5 = ((bf16[32,512,2,128]{3,2,0,1:T(2,128)(2,1)}), bf16[32,512,2,128]{3,2,0,1:T(2,128)(2,1)}, u32[]{:S(2)}, u32[]{:S(2)}) async-start(bf16[32,512,2,128]{3,2,0,1:T(2,128)(2,1)} %copy.204), calls=%async_computation.5 | async-start | bytes 16777216 | tf_op jit(solution)/shard_map/all_to_all | solution.py:99
  758.7 123.5 %all-to-all-start.3 = ((bf16[32,512,2,128]{3,2,0,1:T(2,128)(2,1)}), bf16[32,512,2,128]{3,2,0,1:T(2,128)(2,1)}, u32[]{:S(2)}, u32[]{:S(2)}) async-start(bf16[32,512,2,128]{3,2,0,1:T(2,128)(2,1)} %copy.197), calls=%async_computation.3 | async-start | bytes 16777216 | tf_op jit(solution)/shard_map/all_to_all | solution.py:93
  762.4 479.9 %all-reduce.8.cloned.1.call-start = ((), (), s32[]{:S(2)}) async-start(), calls=%async_computation.8 | async-start | bytes 50331648 | tf_op jit(solution)/shard_map/psum | solution.py:115
  802.7 25.1 %slice-start = ((s8[16777216]{0:T(1024)(128)(4,1)}), s8[4194304]{0:T(1024)(128)(4,1)S(1)}, s32[]{:S(2)}) async-start(s8[16777216]{0:T(1024)(128)(4,1)} %bitcast.265), calls=%async_computation.9 | async-start | bytes 8388608
  802.7 25.1 %slice-start.1 = ((s8[16777216]{0:T(1024)(128)(4,1)}), s8[4194304]{0:T(1024)(128)(4,1)S(1)}, s32[]{:S(2)}) async-start(s8[16777216]{0:T(1024)(128)(4,1)} %bitcast.265), calls=%async_computation.10 | async-start | bytes 8388608
  802.7 25.2 %slice-start.2 = ((s8[16777216]{0:T(1024)(128)(4,1)}), s8[4194304]{0:T(1024)(128)(4,1)S(1)}, s32[]{:S(2)}) async-start(s8[16777216]{0:T(1024)(128)(4,1)} %bitcast.265), calls=%async_computation.11 | async-start | bytes 8388608
  802.7 27.0 %slice-start.3 = ((s8[16777216]{0:T(1024)(128)(4,1)}), s8[4194304]{0:T(1024)(128)(4,1)S(1)}, s32[]{:S(2)}) async-start(s8[16777216]{0:T(1024)(128)(4,1)} %bitcast.265), calls=%async_computation.12 | async-start | bytes 8388608
  802.7 27.0 %copy-start.10 = (f32[32,64,16]{1,2,0:T(8,128)S(1)}, f32[32,64,16]{1,2,0:T(8,128)}, u32[]{:S(2)}) copy-start(f32[32,64,16]{1,2,0:T(8,128)} %copy-done.9) | copy-start | bytes 393220
  802.7 27.0 %copy-start.32 = (f32[128]{0:T(128)S(1)}, f32[128]{0:T(128)}, u32[]{:S(2)}) copy-start(f32[128]{0:T(128)} %param.14) | copy-start | bytes 1540
  829.7 18.2 %copy-start.16 = (f32[32,64,16]{1,2,0:T(8,128)S(1)}, f32[32,64,16]{1,2,0:T(8,128)}, u32[]{:S(2)}) copy-start(f32[32,64,16]{1,2,0:T(8,128)} %copy-done.15) | copy-start | bytes 393220
  848.1 20.1 %copy-start.6 = (bf16[32,64,1024]{2,1,0:T(8,128)(2,1)S(1)}, bf16[32,64,1024]{2,1,0:T(8,128)(2,1)}, u32[]{:S(2)}) copy-start(bf16[32,64,1024]{2,1,0:T(8,128)(2,1)} %param.9) | copy-start | bytes 12582916
  954.9 13.5 %copy-start.12 = (bf16[32,64,1024]{2,1,0:T(8,128)(2,1)S(1)}, bf16[32,64,1024]{2,1,0:T(8,128)(2,1)}, u32[]{:S(2)}) copy-start(bf16[32,64,1024]{2,1,0:T(8,128)(2,1)} %convert_element_type.178) | copy-start | bytes 12582916
  968.5 36.1 %copy-start.26 = (f32[32,64]{1,0:T(8,128)S(1)}, f32[32,64]{1,0:T(8,128)}, u32[]{:S(2)}) copy-start(f32[32,64]{1,0:T(8,128)} %copy-done.25) | copy-start | bytes 24580
  (31 other events, 236.6 us)
Sparse Core Ops, SparseCore 0:
  944.2 297.9 all-reduce.7
where the time goes:
time: 1280 us; the launch traced here: 1270 us
  waiting for transfers between devices  402 us (31%)
  matrix products  308 us (24%)
  local copies, waits for them, and re-layouts  253 us (20%)
  other arithmetic  237 us (19%)
  starting transfers between devices  30.1 us (2%)
  blocking collectives  24.3 us (2%)
  between operations  15.2 us (1%)
    psum x1, waiting for transfers between devices, local_step(): lax.psum(d_wq, 'sp')  215 us
    all_to_all x1, waiting for transfers between devices, local_step(): d_o_here = lax.all_to_all(d_attn.reshape(q_shape), 'sp', 2, 1, tiled=True)  72.9 us
    all_to_all x1, waiting for transfers between devices, local_step(): q_here = lax.all_to_all(q_rot.astype(jnp.bfloat16), 'sp', 2, 1, tiled=True)  70.8 us
    another operation x3, other arithmetic  63.9 us
    dot_general x1, matrix products, core_backward(): jnp.einsum('bqkgd,bskd->bkgqs', d_grouped, v_part, preferred_element_type...  49.3 us
    unnamed x98, local copies, waits for them, and re-layouts  37.4 us
    all_to_all x2, local copies, waits for them, and re-layouts, local_step(): lax.all_to_all(o_here, 'sp', 1, 2, tiled=True)  32.7 us
    add_any x2, other arithmetic, qk_post(): second * sin_b  32.4 us
  transfers between devices with their start and end apart: 9, of which 7 were waited for; matrix products, arithmetic and copies ran while one was open for 39% of the time, Pallas kernels for 0%

commit v1 on v0

v1 whole, which is shorter than its diff:
```python
import math
import functools
import jax
import jax.numpy as jnp
from jax import lax
from jax.experimental import pallas as pl
from jax.experimental.pallas import tpu as pltpu
from jax.sharding import PartitionSpec as P

ROPE_BASE = 1000000.0
NORM_EPS = 1e-6
F32 = jnp.float32
BF16 = jnp.bfloat16
HD = 128
VMEM_LIMIT = 60 * 1024 * 1024


def rope_tables(n_pos):
    half = HD // 2
    inv_freq = jnp.exp(jnp.arange(half).astype(F32) * (-2.0 * math.log(ROPE_BASE) / HD))
    angles = jnp.arange(n_pos).astype(F32)[:, None] * inv_freq[None, :]
    cos, sin = jnp.cos(angles), jnp.sin(angles)
    return jnp.concatenate([cos, cos], axis=-1), jnp.concatenate([-sin, sin], axis=-1)


def qkv_kernel(x_ref, g_ref, wq_ref, wk_ref, wv_ref, gq_ref, gk_ref, cos_ref, sin_ref, h_ref, raw_ref, rot_ref):
    n_src, rows, tok, dim = x_ref.shape
    n = n_src * rows * tok
    x = x_ref[...].reshape(n, dim).astype(F32)
    r = lax.rsqrt(jnp.mean(x * x, axis=-1, keepdims=True) + NORM_EPS)
    h_ref[...] = (x * r * g_ref[...]).astype(BF16).reshape(h_ref.shape)
    cos = cos_ref[...].reshape(n_src, 1, tok, HD)
    sin = sin_ref[...].reshape(n_src, 1, tok, HD)

    def post(raw, gain):
        v = raw.astype(F32)
        v = v * lax.rsqrt(jnp.mean(v * v, axis=-1, keepdims=True) + NORM_EPS) * gain
        rolled = pltpu.roll(v, HD // 2, 1).reshape(n_src, rows, tok, HD)
        return (v.reshape(n_src, rows, tok, HD) * cos + rolled * sin).astype(BF16)

    gq, gk = gq_ref[...], gk_ref[...]
    shape = (n_src, rows, tok, HD)

    def body(j, _):
        hh = h_ref[...].reshape(n, dim)

        def proj(w_ref, width):
            cols = pl.ds(pl.multiple_of(j * width, width), width)
            return jnp.dot(hh, w_ref[:, cols], preferred_element_type=F32).astype(BF16)

        q, k, v = proj(wq_ref, 4 * HD), proj(wk_ref, 2 * HD), proj(wv_ref, 2 * HD)
        for i in range(2):
            heads = [q[:, 2 * i * HD:(2 * i + 1) * HD], q[:, (2 * i + 1) * HD:(2 * i + 2) * HD], k[:, i * HD:(i + 1) * HD]]
            for part, (val, gain) in enumerate(zip(heads, (gq, gq, gk))):
                raw_ref[:, :, :, pl.ds(pl.multiple_of((2 * j + i) * 3 * HD + part * HD, HD), HD)] = val.reshape(shape)
                rot_ref[:, :, :, pl.ds(pl.multiple_of((2 * j + i) * 4 * HD + part * HD, HD), HD)] = post(val, gain)
            rot_ref[:, :, :, pl.ds(pl.multiple_of((2 * j + i) * 4 * HD + 3 * HD, HD), HD)] = v[:, i * HD:(i + 1) * HD].reshape(shape)
        return 0

    lax.fori_loop(0, wk_ref.shape[1] // (2 * HD), body, 0, unroll=2)


QB = 256
NT = (((1,), (1,)), ((), ()))
EXP_SCALE = HD ** -0.5 * math.log2(math.e)


def softmax_t(k, q, qb):
    lo = qb * QB
    parts = [(lo, lax.dot_general(k[lo:lo + QB], q, NT, preferred_element_type=F32))]
    keys = lax.broadcasted_iota(jnp.int32, (QB, QB), 0)
    queries = lax.broadcasted_iota(jnp.int32, (QB, QB), 1)
    parts[0] = (lo, jnp.where(keys <= queries, parts[0][1], -1e30))
    if lo:
        parts.append((0, lax.dot_general(k[:lo], q, NT, preferred_element_type=F32)))
    top = functools.reduce(jnp.maximum, [jnp.max(s, axis=0, keepdims=True) for _, s in parts])
    exps = [(at, jnp.exp2((s - top) * EXP_SCALE)) for at, s in parts]
    inv = 1.0 / functools.reduce(jnp.add, [jnp.sum(e, axis=0, keepdims=True) for _, e in exps])
    return [(at, e * inv) for at, e in exps]


def attn_fwd_kernel(rot_ref, o_ref):
    n_pos = rot_ref.shape[0] * rot_ref.shape[2]
    rot = rot_ref[...].reshape(n_pos, 4 * HD)
    k, v_t = rot[:, 2 * HD:3 * HD], rot[:, 3 * HD:].T
    src_b = QB // rot_ref.shape[2]
    for qb in range(n_pos // QB):
        for head in range(2):
            q = rot[qb * QB:(qb + 1) * QB, head * HD:(head + 1) * HD]
            o_t = functools.reduce(jnp.add, [
                jnp.dot(v_t[:, at:at + p.shape[0]], p.astype(BF16), preferred_element_type=F32)
                for at, p in softmax_t(k, q, qb)])
            o_ref[pl.ds(qb * src_b, src_b), 0, :, pl.ds(head * HD, HD)] = o_t.T.astype(BF16).reshape(src_b, o_ref.shape[2], HD)


def attn_bwd_kernel(rot_ref, raw_ref, do_ref, gq_ref, gk_ref, cos_ref, sin_ref, oq_ref, ok_ref, ov_ref, dgq_ref, dgk_ref, dk_acc, dv_acc):
    n_src, _, tok, _ = rot_ref.shape
    n_pos = n_src * tok
    rot = rot_ref[...].reshape(n_pos, 4 * HD)
    raw = raw_ref[...].reshape(n_pos, 3 * HD)
    d_o = do_ref[...].reshape(n_pos, 2 * HD)
    k, v = rot[:, 2 * HD:3 * HD], rot[:, 3 * HD:]
    k_t = k.astype(F32).T.astype(BF16)
    src_b = QB // tok
    first = jnp.logical_and(pl.program_id(0) == 0, pl.program_id(1) == 0)

    @pl.when(first)
    def _():
        dgq_ref[...] = jnp.zeros_like(dgq_ref)
        dgk_ref[...] = jnp.zeros_like(dgk_ref)

    def post_back(d, x_raw, gain, lo, dg_ref):
        cnt = d.shape[0]
        d = d.astype(BF16).astype(F32)
        c, s = cos_ref[pl.ds(lo, cnt), :], sin_ref[pl.ds(lo, cnt), :]
        dn = d * c + pltpu.roll(d * s, HD // 2, 1)
        x = x_raw.astype(F32)
        r = lax.rsqrt(jnp.mean(x * x, axis=-1, keepdims=True) + NORM_EPS)
        xh = x * r
        t = dn * xh
        dg_ref[...] += jnp.sum(t.reshape(cnt // 8, 8, HD), axis=0)
        dng = dn * gain
        return (r * (dng - xh * jnp.mean(dng * xh, axis=-1, keepdims=True))).astype(BF16)

    for qb in reversed(range(n_pos // QB)):
        last = qb == n_pos // QB - 1
        sl = slice(qb * QB, (qb + 1) * QB)
        for head in range(2):
            hs = slice(head * HD, (head + 1) * HD)
            q, dob = rot[sl, hs], d_o[sl, hs]
            ps = softmax_t(k, q, qb)
            dps = [lax.dot_general(v[at:at + p.shape[0]], dob, NT, preferred_element_type=F32) for at, p in ps]
            delta = functools.reduce(jnp.add, [jnp.sum(p * dp, axis=0, keepdims=True) for (_, p), dp in zip(ps, dps)])
            dq_t = None
            for (at, p), dp in zip(ps, dps):
                ds = (p * (dp - delta) * HD ** -0.5).astype(BF16)
                dq_p = jnp.dot(k_t[:, at:at + p.shape[0]], ds, preferred_element_type=F32)
                dq_t = dq_p if dq_t is None else dq_t + dq_p
                dv = jnp.dot(p.astype(BF16), dob, preferred_element_type=F32)
                dk = jnp.dot(ds, q, preferred_element_type=F32)
                rows = pl.ds(at, dk.shape[0])
                if last and head == 0:
                    dk_acc[rows, :] = dk
                    dv_acc[rows, :] = dv
                else:
                    dk_acc[rows, :] += dk
                    dv_acc[rows, :] += dv
            dq_raw = post_back(dq_t.T, raw[sl, hs], gq_ref[...], qb * QB, dgq_ref)
            oq_ref[pl.ds(qb * src_b, src_b), 0, :, pl.ds(head * HD, HD)] = dq_raw.reshape(src_b, tok, HD)
    dk_raw = post_back(dk_acc[...], raw[:, 2 * HD:], gk_ref[...], 0, dgk_ref)
    ok_ref[:, 0] = dk_raw.reshape(n_src, tok, HD)
    ov_ref[:, 0] = dv_acc[...].astype(BF16).reshape(n_src, tok, HD)


def dx_kernel(dq_ref, dk_ref, dv_ref, wq_ref, wk_ref, wv_ref, x_ref, dy_ref, g_ref, dx_ref, dg_ref):
    n_src, rows, tok, dim = x_ref.shape
    n = n_src * rows * tok

    @pl.when(pl.program_id(0) == 0)
    def _():
        dg_ref[...] = jnp.zeros_like(dg_ref)

    dn = functools.reduce(jnp.add, [
        lax.dot_general(d[...].reshape(n, d.shape[-1]), w[...], NT, preferred_element_type=F32)
        for d, w in ((dq_ref, wq_ref), (dk_ref, wk_ref), (dv_ref, wv_ref))])
    x = x_ref[...].reshape(n, dim).astype(F32)
    r = lax.rsqrt(jnp.mean(x * x, axis=-1, keepdims=True) + NORM_EPS)
    xh = x * r
    dg_ref[...] += jnp.sum((dn * xh).reshape(n // 8, 8, dim), axis=0)
    dng = dn * g_ref[...]
    dx = r * (dng - xh * jnp.mean(dng * xh, axis=-1, keepdims=True))
    dx_ref[...] = (dy_ref[...].reshape(n, dim).astype(F32) + dx).astype(BF16).reshape(dx_ref.shape)


MESH = pl.DeviceIdType.MESH


def tail_kernel(n_dev, *refs):
    wq, wk, wv, dx, gains, oq, ok, ov, odx, ogains = refs[:10]
    chunks = [(wq, oq, 0, wq.shape[0] // 2), (wq, oq, wq.shape[0] // 2, wq.shape[0] // 2), (wk, ok, 0, wk.shape[0]), (wv, ov, 0, wv.shape[0])]
    nc = len(chunks)
    acc, r1, r2, r3 = (refs[10 + i * nc:10 + (i + 1) * nc] for i in range(4))
    gbuf, xbuf, send, recv, loc, xsend, xrecv, gsend, grecv, lsem = refs[10 + 4 * nc:]
    me = lax.axis_index('sp')
    c, x, y = me % 2, (me // 2) % 2, me // 4
    pn, xn, yn = me + 1 - 2 * c, me + 2 - 4 * x, me + 4 - 8 * y
    peers = [(me + d) % n_dev for d in range(1, n_dev)]

    barrier = pltpu.get_barrier_semaphore()
    for p in peers:
        pl.semaphore_signal(barrier, inc=1, device_id=(p,), device_id_type=MESH)
    pl.semaphore_wait(barrier, n_dev - 1)

    def rdma(src, dst, ci, slot, dev):
        return pltpu.make_async_remote_copy(src_ref=src, dst_ref=dst, send_sem=send.at[ci, slot], recv_sem=recv.at[ci, slot],
                                            device_id=(dev,), device_id_type=MESH)

    def add(dst, d0, src, s0, n):
        step = 8
        def body(i, _):
            dst[pl.ds(pl.multiple_of(d0 + i * step, 8), step), :] += src[pl.ds(pl.multiple_of(s0 + i * step, 8), step), :]
            return 0
        lax.fori_loop(0, n // step, body, 0, unroll=2)

    started = []

    def go(copies):
        for cp in copies:
            cp.start()
        started.extend(copies)
        return copies

    flight = {}

    def s1(i):
        src, out, row0, n = chunks[i]
        half = n // 2
        mine = pltpu.make_async_copy(src.at[pl.ds(pl.multiple_of(row0 + c * half, 8), half), :], acc[i], loc.at[i, 0])
        mine.start()
        flight[i, 1] = (mine, go([rdma(src.at[pl.ds(pl.multiple_of(row0 + (1 - c) * half, 8), half), :], r1[i], i, 0, pn)]))

    def s2(i):
        n = chunks[i][3]
        mine, cps = flight[i, 1]
        mine.wait()
        cps[0].wait_recv()
        add(acc[i], 0, r1[i], 0, n // 2)
        e = n // 8
        flight[i, 2] = go([rdma(acc[i].at[pl.ds(pl.multiple_of((1 - x) * e, 8), e), :], r2[i].at[0], i, 1, xn),
                           rdma(acc[i].at[pl.ds(pl.multiple_of(n // 4 + (1 - y) * e, 8), e), :], r2[i].at[1], i, 2, yn)])

    def s3(i):
        n = chunks[i][3]
        e, f = n // 8, n // 16
        for cp in flight[i, 2]:
            cp.wait_recv()
        p1, q1 = x * e, n // 4 + y * e
        add(acc[i], p1, r2[i].at[0], 0, e)
        add(acc[i], q1, r2[i].at[1], 0, e)
        flight[i, 3] = go([rdma(acc[i].at[pl.ds(pl.multiple_of(p1 + (1 - y) * f, 8), f), :], r3[i].at[0], i, 3, yn),
                           rdma(acc[i].at[pl.ds(pl.multiple_of(q1 + (1 - x) * f, 8), f), :], r3[i].at[1], i, 4, xn)])

    def s4(i):
        _, out, row0, n = chunks[i]
        e, f = n // 8, n // 16
        for cp in flight[i, 3]:
            cp.wait_recv()
        p, q = x * e + y * f, n // 4 + y * e + x * f
        add(acc[i], p, r3[i].at[0], 0, f)
        add(acc[i], q, r3[i].at[1], 0, f)
        base = row0 + c * (n // 2)
        ps, qs = acc[i].at[pl.ds(pl.multiple_of(p, 8), f), :], acc[i].at[pl.ds(pl.multiple_of(q, 8), f), :]
        po, qo = out.at[pl.ds(pl.multiple_of(base + p, 8), f), :], out.at[pl.ds(pl.multiple_of(base + q, 8), f), :]
        mine = [pltpu.make_async_copy(ps, po, loc.at[i, 1]), pltpu.make_async_copy(qs, qo, loc.at[i, 2])]
        for cp in mine:
            cp.start()
        flight[i, 4] = (mine, go([rdma(ps, po, i, 5, yn), rdma(qs, qo, i, 6, xn), rdma(ps, po, i, 7, xn), rdma(qs, qo, i, 8, yn)]))

    def s5(i):
        _, out, row0, n = chunks[i]
        e, f = n // 8, n // 16
        cps = flight[i, 4][1]
        cps[0].wait_recv()
        cps[1].wait_recv()
        base = row0 + c * (n // 2)
        po = out.at[pl.ds(pl.multiple_of(base + x * e + (1 - y) * f, 8), f), :]
        qo = out.at[pl.ds(pl.multiple_of(base + n // 4 + y * e + (1 - x) * f, 8), f), :]
        flight[i, 5] = go([rdma(po, po, i, 9, xn), rdma(qo, qo, i, 10, yn)])

    def s6(i):
        _, out, row0, n = chunks[i]
        mine, cps = flight[i, 4]
        for cp in mine:
            cp.wait()
        for cp in (cps[2], cps[3], *flight[i, 5]):
            cp.wait_recv()
        rows = out.at[pl.ds(pl.multiple_of(row0 + c * (n // 2), 8), n // 2), :]
        flight[i, 6] = go([rdma(rows, rows, i, 11, pn)])

    rows = dx.shape[1]

    def send_dx(d):
        to = me + (1 - 2 * c) * (d % 2) + (2 - 4 * x) * ((d // 2) % 2) + (4 - 8 * y) * (d // 4)
        cp = pltpu.make_async_remote_copy(src_ref=dx.at[to], dst_ref=odx.at[pl.ds(pl.multiple_of(me * rows, rows), rows)],
                                          send_sem=xsend.at[d], recv_sem=xrecv.at[d], device_id=(to,), device_id_type=MESH)
        cp.start()
        return cp

    for i in range(nc):
        s1(i)
    gcopies = []
    for d in range(1, n_dev):
        cp = pltpu.make_async_remote_copy(src_ref=gains, dst_ref=gbuf.at[d - 1], send_sem=gsend.at[d], recv_sem=grecv.at[d],
                                          device_id=(peers[d - 1],), device_id_type=MESH)
        cp.start()
        gcopies.append(cp)
    keep_in = pltpu.make_async_copy(dx.at[me], xbuf, lsem.at[0])
    keep_in.start()
    xcopies = [send_dx(d) for d in (2, 4, 1)]
    filler = [3, 5, 6, 7]
    stages = [s2, s3, s4, s5, s6]
    keep_out = None
    for t in range(nc + len(stages) - 1):
        for k in reversed(range(len(stages))):
            if 0 <= t - k < nc:
                stages[k](t - k)
        if t >= 2 and filler:
            xcopies.append(send_dx(filler.pop(0)))
        if t == 1:
            keep_in.wait()
            keep_out = pltpu.make_async_copy(xbuf, odx.at[pl.ds(pl.multiple_of(me * rows, rows), rows)], lsem.at[1])
            keep_out.start()
    for cp in gcopies:
        cp.wait()
    ogains[...] = gains[...] + functools.reduce(jnp.add, [gbuf[d] for d in range(n_dev - 1)])
    keep_out.wait()
    for i in range(nc):
        flight[i, 6][0].wait_recv()
    for cp in started:
        cp.wait_send()
    for cp in xcopies:
        cp.wait()


def finish(n_dev, dwq, dwk, dwv, dx, gains):
    nd, rows, tok, dim = dx.shape
    hbm, vmem = pl.BlockSpec(memory_space=pl.ANY), pl.BlockSpec(memory_space=pltpu.VMEM)
    sizes = [(dwq.shape[0] // 2, dwq.shape[1])] * 2 + [dwk.shape, dwv.shape]
    nc = len(sizes)
    dma = pltpu.SemaphoreType.DMA
    scratch = [pltpu.VMEM((r // 2, w), F32) for r, w in sizes] + [pltpu.VMEM((r // 2, w), F32) for r, w in sizes]
    scratch += [pltpu.VMEM((2, r // 8, w), F32) for r, w in sizes] + [pltpu.VMEM((2, r // 16, w), F32) for r, w in sizes]
    scratch += [pltpu.VMEM((n_dev - 1,) + gains.shape, F32), pltpu.VMEM((rows, tok, dim), BF16)]
    scratch += [dma((nc, 12)), dma((nc, 12)), dma((nc, 3)), dma((n_dev,)), dma((n_dev,)), dma((n_dev,)), dma((n_dev,)), dma((2,))]
    return pl.pallas_call(
        functools.partial(tail_kernel, n_dev), in_specs=[hbm] * 4 + [vmem], out_specs=[hbm] * 4 + [vmem],
        out_shape=[jax.ShapeDtypeStruct(a.shape, F32) for a in (dwq, dwk, dwv)] + [
            jax.ShapeDtypeStruct((nd * rows, tok, dim), BF16), jax.ShapeDtypeStruct(gains.shape, F32)],
        scratch_shapes=scratch, compiler_params=params(collective_id=0, has_side_effects=True), name='tail',
    )(dwq, dwk, dwv, dx, gains)


def params(**kw):
    return pltpu.CompilerParams(vmem_limit_bytes=VMEM_LIMIT, **kw)


def cost(flops, nbytes):
    return pl.CostEstimate(flops=int(flops), bytes_accessed=int(nbytes), transcendentals=0)


def solution(mesh):
    n_dev = mesh.shape['sp']
    seq_spec = P(None, 'sp', None)
    replicated = P()

    def local_step(hidden, norm_gain, w_q, w_k, w_v, q_gain, k_gain, w_o, d_out):
        n_batch, tok, dim = hidden.shape
        rows = n_batch // n_dev
        n_pos = tok * n_dev
        n_tok = n_pos * rows
        n_q, n_kv = w_q.shape[1] // HD, w_k.shape[1] // HD
        qw = n_q * HD
        cos_t, sin_t = rope_tables(n_pos)
        g2 = norm_gain.reshape(1, dim)
        gq2, gk2 = q_gain.reshape(1, HD), k_gain.reshape(1, HD)
        x = lax.all_to_all(hidden, 'sp', 0, 0, tiled=True).reshape(n_dev, rows, tok, dim)
        dy = lax.all_to_all(d_out, 'sp', 0, 0, tiled=True).reshape(n_dev, rows, tok, dim)

        sb = 2
        full = lambda *s: pl.BlockSpec(s, lambda *i: (0,) * len(s))
        tokspec = lambda c: pl.BlockSpec((sb, rows, tok, c), lambda i: (i, 0, 0, 0))
        shp = lambda c, d=BF16: jax.ShapeDtypeStruct((n_dev, rows, tok, c), d)
        h, raw, rot = pl.pallas_call(
            qkv_kernel, grid=(n_dev // sb,),
            in_specs=[tokspec(dim), full(1, dim), full(*w_q.shape), full(*w_k.shape), full(*w_v.shape), full(1, HD), full(1, HD),
                      pl.BlockSpec((sb * tok, HD), lambda i: (i, 0)), pl.BlockSpec((sb * tok, HD), lambda i: (i, 0))],
            out_specs=[tokspec(dim), tokspec(n_kv * 3 * HD), tokspec(n_kv * 4 * HD)],
            out_shape=[shp(dim), shp(n_kv * 3 * HD), shp(n_kv * 4 * HD)],
            compiler_params=params(), cost_estimate=cost(2 * n_tok * dim * 4 * HD * n_kv, 40e6), name='qkv',
        )(x, g2, w_q, w_k, w_v, gq2, gk2, cos_t, sin_t)

        head_spec = lambda c: pl.BlockSpec((n_dev, 1, tok, c), lambda r, j: (0, r, 0, j))
        o = pl.pallas_call(
            attn_fwd_kernel, grid=(rows, n_kv), in_specs=[head_spec(4 * HD)], out_specs=head_spec(2 * HD),
            out_shape=shp(qw), compiler_params=params(), cost_estimate=cost(4 * n_tok * n_pos * qw, 24e6), name='attn_fwd',
        )(rot)
        o2, dy2, x2 = o.reshape(n_tok, qw), dy.reshape(n_tok, dim), x.reshape(n_tok, dim)
        y = (x2.astype(F32) + jnp.dot(o2, w_o, preferred_element_type=F32)).astype(BF16)
        d_wo = lax.dot_general(o2, dy2, (((0,), (0,)), ((), ())), preferred_element_type=F32)
        d_o = lax.dot_general(dy2, w_o, (((1,), (1,)), ((), ())), preferred_element_type=F32).astype(BF16).reshape(n_dev, rows, tok, qw)
        y, d_wo, d_o = lax.optimization_barrier((y, d_wo, d_o))
        y_out = lax.all_to_all(y.reshape(n_batch, tok, dim), 'sp', 0, 0, tiled=True)

        dq, dk, dv, dgq, dgk = pl.pallas_call(
            attn_bwd_kernel, grid=(rows, n_kv),
            in_specs=[head_spec(4 * HD), head_spec(3 * HD), head_spec(2 * HD), full(1, HD), full(1, HD), full(n_pos, HD), full(n_pos, HD)],
            out_specs=[head_spec(2 * HD), head_spec(HD), head_spec(HD), full(8, HD), full(8, HD)],
            out_shape=[shp(qw), shp(n_kv * HD), shp(n_kv * HD), jax.ShapeDtypeStruct((8, HD), F32), jax.ShapeDtypeStruct((8, HD), F32)],
            scratch_shapes=[pltpu.VMEM((n_pos, HD), F32), pltpu.VMEM((n_pos, HD), F32)],
            compiler_params=params(), cost_estimate=cost(10 * n_tok * n_pos * qw, 60e6), name='attn_bwd',
        )(rot, raw, d_o, gq2, gk2, cos_t, sin_t)

        dq, y_out = lax.optimization_barrier((dq, y_out))
        h2 = h.reshape(n_tok, dim)
        d_wq, d_wk, d_wv = (lax.dot_general(h2, d.reshape(n_tok, -1), (((0,), (0,)), ((), ())), preferred_element_type=F32) for d in (dq, dk, dv))
        dx, dg = pl.pallas_call(
            dx_kernel, grid=(n_dev // sb,),
            in_specs=[tokspec(qw), tokspec(n_kv * HD), tokspec(n_kv * HD), full(*w_q.shape), full(*w_k.shape), full(*w_v.shape), tokspec(dim), tokspec(dim), full(1, dim)],
            out_specs=[tokspec(dim), full(8, dim)],
            out_shape=[shp(dim), jax.ShapeDtypeStruct((8, dim), F32)],
            compiler_params=params(), cost_estimate=cost(2 * n_tok * dim * 4 * HD * n_kv, 40e6), name='dx',
        )(dq, dk, dv, w_q, w_k, w_v, x, dy, g2)
        d_wo = lax.psum(d_wo, 'sp')
        gains = jnp.concatenate([jnp.sum(dg, 0), jnp.sum(dgq, 0), jnp.sum(dgk, 0)])
        gains = jnp.pad(gains, (0, -gains.size % 1024)).reshape(-1, 128)
        d_wq, d_wk, d_wv, d_hidden, gains = finish(n_dev, d_wq, d_wk, d_wv, dx, gains)
        gains = gains.reshape(-1)
        return (y_out, d_hidden, d_wq, d_wk, d_wv, d_wo, gains[:dim], gains[dim:dim + HD], gains[dim + HD:dim + 2 * HD])

    return jax.shard_map(local_step, mesh=mesh, in_specs=(seq_spec,) + (replicated,) * 7 + (seq_spec,),
                         out_specs=(seq_spec, seq_spec) + (replicated,) * 7, check_vma=False)
```

time: 1280 us -> 661 us (0.52)
  Pallas kernels: 0 us -> 417 us
  waiting for transfers between devices: 402 us -> 54.4 us
  matrix products: 308 us -> 72.6 us
  other arithmetic: 237 us -> 4.77 us
  local copies, waits for them, and re-layouts: 253 us -> 28.2 us
  blocking collectives: 24.3 us -> 53.3 us
  starting transfers between devices: 30.1 us -> 6.86 us
    pallas_call x0 -> x5, Pallas kernels: none -> 417 us  [the longest x1 192 us: finish(): pl.pallas_call(functools.partial(tail_kernel, n_dev), in_specs=[hbm] * 4...]
    dot_general x18 -> x6, matrix products: 308 us -> 72.6 us  [the longest x3 31.2 us: local_step(): lax.dot_general(h2, d.reshape(n_tok, -1), (((0,), (0,)), ((), ())), prefe...]
    psum x1, waiting for transfers between devices: 215 us -> 0.01 us  [local_step(): d_wo = lax.psum(d_wo, 'sp')]
    all_to_all x8 -> x2, waiting for transfers between devices: 186 us -> 54.4 us  [the longest x1 54.4 us: local_step(): y_out = lax.all_to_all(y.reshape(n_batch, tok, dim), 'sp', 0, 0, tiled=True)]
    all_to_all x9 -> x0, local copies, waits for them, and re-layouts: 87.5 us -> none  [the longest x2 32.7 us: local_step(): lax.all_to_all(o_here, 'sp', 1, 2, tiled=True)]
    reshape x4 -> x0, local copies, waits for them, and re-layouts: 66.4 us -> none  [the longest x1 21.6 us: core_forward(): out_heads.astype(jnp.bfloat16).reshape(n_batch, n_pos, q_heads, head_dim)]
    another operation x3 -> x0, other arithmetic: 63.9 us -> none
    reduce_sum x6 -> x3, other arithmetic: 65.7 us -> 2.16 us  [local_step(): gains = jnp.concatenate([jnp.sum(dg, 0), jnp.sum(dgq, 0), jnp.sum(dgk, 0)])]
  transfers between devices with their start and end apart: 9 -> 3, of which waited for: 7 -> 1; matrix products, arithmetic and copies ran while one was open for 39% -> 6% of each run, Pallas kernels for 0% -> 64%
where the time goes in v1:
time: 661 us; the launch traced here: 652 us
  Pallas kernels  417 us (63%)
  matrix products  72.6 us (11%)
  waiting for transfers between devices  54.4 us (8%)
  blocking collectives  53.3 us (8%)
  local copies, waits for them, and re-layouts  28.2 us (4%)
  between operations  14.6 us (2%)
  starting transfers between devices  6.86 us (1%)
    pallas_call x1, Pallas kernels, finish(): pl.pallas_call(functools.partial(tail_kernel, n_dev), in_specs=[hbm] * 4...  192 us
    pallas_call x1, Pallas kernels, local_step(): pl.pallas_call(attn_bwd_kernel, grid=(rows, n_kv), in_specs=[head_spec(4...  86 us
    pallas_call x1, Pallas kernels, local_step(): pl.pallas_call(qkv_kernel, grid=(n_dev // sb,), in_specs=[tokspec(dim), f...  56.5 us
    pallas_call x1, Pallas kernels, local_step(): pl.pallas_call(attn_fwd_kernel, grid=(rows, n_kv), in_specs=[head_spec(4...  54.7 us
    all_to_all x1, waiting for transfers between devices, local_step(): y_out = lax.all_to_all(y.reshape(n_batch, tok, dim), 'sp', 0, 0, tiled=True)  54.4 us
    all_to_all x1, blocking collectives, local_step(): lax.all_to_all(hidden, 'sp', 0, 0, tiled=True)  53.3 us
    dot_general x3, matrix products, local_step(): lax.dot_general(h2, d.reshape(n_tok, -1), (((0,), (0,)), ((), ())), prefe...  31.2 us
    pallas_call x1, Pallas kernels, local_step(): pl.pallas_call(dx_kernel, grid=(n_dev // sb,), in_specs=[tokspec(qw), tok...  27.7 us
  transfers between devices with their start and end apart: 3, of which 1 were waited for; matrix products, arithmetic and copies ran while one was open for 6% of the time, Pallas kernels for 64%

profile of v1, /device:TPU:0, one launch (start us, length us, event | category | flops | bytes accessed | tf_op | source)
XLA Modules:
  0.0 651.6 jit_solution(6601159909838500702)
XLA Ops:
  7.2 53.3 %all_to_all.15 = bf16[32,64,1024]{2,1,0:T(8,128)(2,1)} all-to-all(bf16[32,64,1024]{2,1,0:T(8,128)(2,1)} %param.9), channel_id=1, replica_groups=mesh['sp'=8] {'sp'}, dimensions={0} | all-to-all | bytes 8388608 | tf_op jit(solution)/shard_map/all_to_all | solution.py:366
  60.4 3.3 all-to-all-start.1
  65.8 56.5 %qkv.1 = (bf16[8,4,64,1024]{3,2,1,0:T(8,128)(2,1)}, bf16[8,4,64,3072]{3,2,1,0:T(8,128)(2,1)}, bf16[8,4,64,4096]{3,2,1,0:T(8,128)(2,1)}) custom-call(bf16[8,4,64,1024]{3,2,1,0:T(8,128)(2,1)} %bitcast.48, f32[1,1024]{1,0:T(1,128)} %bitcast.51, bf16[1024,2048]{1,0:T(8,128)(2,1)} %wq_ref.3, bf16[1024,1024]{1,0:T(8,128)(2,1)} %wk_ref.3, ...), custom_call_target="tpu_custom_call" | custom-call | flops 17179869184 | bytes 40000000 | tf_op jit(solution)/shard_map/qkv/pallas_call | solution.py:373
  122.3 54.7 %attn_fwd.1 = bf16[8,4,64,2048]{3,2,1,0:T(8,128)(2,1)} custom-call(bf16[8,4,64,4096]{3,2,1,0:T(8,128)(2,1)} %get-tuple-element.29.rot_ref), custom_call_target="tpu_custom_call" | custom-call | flops 8589934592 | bytes 24000000 | tf_op jit(solution)/shard_map/attn_fwd/pallas_call | solution.py:383
  177.0 14.1 %convolution_convert_fusion = bf16[2048,2048]{1,0:T(8,128)(2,1)} fusion(bf16[2048,1024]{1,0:T(8,128)(2,1)} %bitcast.6, bf16[2048,1024]{1,0:T(8,128)(2,1)} %param.16), kind=kOutput, calls=%fused_computation.2 | convolution fusion | flops 8594128896 | bytes 16777216 | tf_op jit(solution)/shard_map/dot_general | solution.py:390
  191.1 12.9 %fusion.3 = f32[2048,1024]{1,0:T(8,128)} fusion(bf16[2048,2048]{1,0:T(8,128)(2,1)S(1)} %bitcast.59, bf16[2048,1024]{1,0:T(8,128)(2,1)} %bitcast.6), kind=kOutput, calls=%fused_computation.20 | convolution fusion | flops 8589934592 | bytes 20971520 | tf_op jit(solution)/shard_map/dot_general | solution.py:389
  204.0 14.4 %fusion = bf16[2048,1024]{1,0:T(8,128)(2,1)} fusion(bf16[32,64,1024]{2,1,0:T(8,128)(2,1)} %all_to_all.15, bf16[2048,2048]{1,0:T(8,128)(2,1)} %bitcast.58, bf16[2048,1024]{1,0:T(8,128)(2,1)} %param.16), kind=kOutput, calls=%fused_computation.1 | convolution fusion | flops 8596226048 | bytes 20971520 | tf_op jit(solution)/shard_map/dot_general | solution.py:388
  218.4 86.0 %attn_bwd.1 = (bf16[8,4,64,2048]{3,2,1,0:T(8,128)(2,1)}, bf16[8,4,64,1024]{3,2,1,0:T(8,128)(2,1)}, bf16[8,4,64,1024]{3,2,1,0:T(8,128)(2,1)}, f32[8,128]{1,0:T(8,128)}, f32[8,128]{1,0:T(8,128)}) custom-call(bf16[8,4,64,4096]{3,2,1,0:T(8,128)(2,1)} %get-tuple-element.29.rot_ref, bf16[8,4,64,3072]{3,2,1,0:T(8,128)(2,1)} %get-tuple-element.30.raw_ref, ...), custom_call_target="tpu_custom_call" | custom-call | flops 21474836480 | bytes 60000000 | tf_op jit(solution)/shard_map/attn_bwd/pallas_call | solution.py:394
  305.8 3.5 all-to-all-start.2
  309.4 10.1 %convolution_bitcast_fusion.1.refs_2_ = f32[1024,1024]{1,0:T(8,128)} fusion(bf16[8,4,64,1024]{3,2,1,0:T(8,128)(2,1)} %get-tuple-element.35, bf16[8,4,64,1024]{3,2,1,0:T(8,128)(2,1)} %get-tuple-element.38.dv_ref), kind=kOutput, calls=%fused_computation.4 | convolution fusion | flops 4294967296 | bytes 12582912 | tf_op jit(solution)/shard_map/dot_general | solution.py:405
  319.5 6.2 convolution_bitcast_fusion.2.refs_1_
  325.7 54.4 %all-to-all-done.2 = bf16[32,64,1024]{2,1,0:T(8,128)(2,1)} async-done(((bf16[32,64,1024]{2,1,0:T(8,128)(2,1)}), bf16[32,64,1024]{2,1,0:T(8,128)(2,1)}, u32[]{:S(2)}, u32[]{:S(2)}) %all-to-all-start.2) | async-done | bytes 4194336 | tf_op jit(solution)/shard_map/all_to_all | solution.py:392
  380.1 27.7 %dx.1 = (bf16[8,4,64,1024]{3,2,1,0:T(8,128)(2,1)}, f32[8,1024]{1,0:T(8,128)}) custom-call(bf16[8,4,64,2048]{3,2,1,0:T(8,128)(2,1)} %get-tuple-element.36.dq_ref, bf16[8,4,64,1024]{3,2,1,0:T(8,128)(2,1)} %get-tuple-element.37.dk_ref, bf16[8,4,64,1024]{3,2,1,0:T(8,128)(2,1)} %get-tuple-element.38.dv_ref, bf16[1024,2048]{1,0:T(8,128)(2,1)} %wq_ref.3, ...), custom_call_target="tpu_custom_call" | custom-call | flops 17179869184 | bytes 40000000 | tf_op jit(solution)/shard_map/dx/pallas_call | solution.py:406
  409.2 14.9 %convolution_bitcast_fusion.refs_0_ = f32[1024,2048]{1,0:T(8,128)} fusion(bf16[8,4,64,1024]{3,2,1,0:T(8,128)(2,1)} %get-tuple-element.35, bf16[8,4,64,2048]{3,2,1,0:T(8,128)(2,1)} %get-tuple-element.36.dq_ref), kind=kOutput, calls=%fused_computation.3 | convolution fusion | flops 8589934592 | bytes 20971520 | tf_op jit(solution)/shard_map/dot_general | solution.py:405
  424.0 192.1 %tail.1 = (f32[1024,2048]{1,0:T(8,128)}, f32[1024,1024]{1,0:T(8,128)}, f32[1024,1024]{1,0:T(8,128)}, bf16[32,64,1024]{2,1,0:T(8,128)(2,1)}, f32[16,128]{1,0:T(8,128)}) custom-call(f32[1024,2048]{1,0:T(8,128)} %convolution_bitcast_fusion.refs_0_, f32[1024,1024]{1,0:T(8,128)} %convolution_bitcast_fusion.2.refs_1_, ...), custom_call_target="tpu_custom_call" | custom-call | tf_op jit(solution)/shard_map/tail/pallas_call | solution.py:335
  618.7 5.2 copy.27
  623.9 2.1 copy.28
  626.0 1.8 slice-done.3
  627.8 4.3 copy.29
  633.1 2.1 copy.30
  635.2 1.6 copy-done
  636.8 2.1 copy.31
  638.9 2.1 slice-done.1
  641.0 3.4 copy.32
  (33 shorter events, 8.4 us)
Async XLA Ops:
  60.4 116.6 %all-to-all-start.1 = ((bf16[32,64,1024]{2,1,0:T(8,128)(2,1)}), bf16[32,64,1024]{2,1,0:T(8,128)(2,1)}, u32[]{:S(2)}, u32[]{:S(2)}) async-start(bf16[32,64,1024]{2,1,0:T(8,128)(2,1)} %param.17), calls=%async_computation.1 | async-start | bytes 8388608 | tf_op jit(solution)/shard_map/all_to_all | solution.py:367
  63.7 554.9 %all-reduce.3.cloned.1.call-start = ((), (), s32[]{:S(2)}) async-start(), calls=%async_computation.3 | async-start | bytes 16777216 | tf_op jit(solution)/shard_map/psum | solution.py:413
  177.0 14.1 %copy-start.3 = (bf16[8,4,64,2048]{3,2,1,0:T(8,128)(2,1)S(1)}, bf16[8,4,64,2048]{3,2,1,0:T(8,128)(2,1)}, u32[]{:S(2)}) copy-start(bf16[8,4,64,2048]{3,2,1,0:T(8,128)(2,1)} %attn_fwd.1) | copy-start | bytes 25165828
  305.8 74.3 %all-to-all-start.2 = ((bf16[32,64,1024]{2,1,0:T(8,128)(2,1)}), bf16[32,64,1024]{2,1,0:T(8,128)(2,1)}, u32[]{:S(2)}, u32[]{:S(2)}) async-start(bf16[32,64,1024]{2,1,0:T(8,128)(2,1)} %bitcast.50), calls=%async_computation.2 | async-start | bytes 8388608 | tf_op jit(solution)/shard_map/all_to_all | solution.py:392
  309.4 10.2 %copy-start.4 = (bf16[8,4,64,1024]{3,2,1,0:T(8,128)(2,1)S(1)}, bf16[8,4,64,1024]{3,2,1,0:T(8,128)(2,1)}, u32[]{:S(2)}) copy-start(bf16[8,4,64,1024]{3,2,1,0:T(8,128)(2,1)} %get-tuple-element.35) | copy-start | bytes 12582916
  309.4 10.1 %copy-start.5 = (bf16[8,4,64,1024]{3,2,1,0:T(8,128)(2,1)S(1)}, bf16[8,4,64,1024]{3,2,1,0:T(8,128)(2,1)}, u32[]{:S(2)}) copy-start(bf16[8,4,64,1024]{3,2,1,0:T(8,128)(2,1)} %get-tuple-element.37.dk_ref) | copy-start | bytes 12582916
  618.7 5.2 copy-start.2
  618.7 7.3 %slice-start.2 = ((s8[8388608]{0:T(1024)(128)(4,1)}), s8[4194304]{0:T(1024)(128)(4,1)S(1)}, s32[]{:S(2)}) async-start(s8[8388608]{0:T(1024)(128)(4,1)} %bitcast.46), calls=%async_computation.6 | async-start | bytes 8388608
  623.9 4.0 slice-start.3
  627.8 5.2 copy-start.1
  633.1 3.7 copy-start
  633.1 5.8 slice-start
  636.8 4.2 slice-start.1
Sparse Core Ops, SparseCore 0:
  218.6 149.3 all-reduce.2

commit v2 on v1

--- a/solution.py
+++ b/solution.py
@@ -152,35 +152,16 @@
     ov_ref[:, 0] = dv_acc[...].astype(BF16).reshape(n_src, tok, HD)
 
 
-def dx_kernel(dq_ref, dk_ref, dv_ref, wq_ref, wk_ref, wv_ref, x_ref, dy_ref, g_ref, dx_ref, dg_ref):
-    n_src, rows, tok, dim = x_ref.shape
-    n = n_src * rows * tok
-
-    @pl.when(pl.program_id(0) == 0)
-    def _():
-        dg_ref[...] = jnp.zeros_like(dg_ref)
-
-    dn = functools.reduce(jnp.add, [
-        lax.dot_general(d[...].reshape(n, d.shape[-1]), w[...], NT, preferred_element_type=F32)
-        for d, w in ((dq_ref, wq_ref), (dk_ref, wk_ref), (dv_ref, wv_ref))])
-    x = x_ref[...].reshape(n, dim).astype(F32)
-    r = lax.rsqrt(jnp.mean(x * x, axis=-1, keepdims=True) + NORM_EPS)
-    xh = x * r
-    dg_ref[...] += jnp.sum((dn * xh).reshape(n // 8, 8, dim), axis=0)
-    dng = dn * g_ref[...]
-    dx = r * (dng - xh * jnp.mean(dng * xh, axis=-1, keepdims=True))
-    dx_ref[...] = (dy_ref[...].reshape(n, dim).astype(F32) + dx).astype(BF16).reshape(dx_ref.shape)
-
-
 MESH = pl.DeviceIdType.MESH
 
 
 def tail_kernel(n_dev, *refs):
-    wq, wk, wv, dx, gains, oq, ok, ov, odx, ogains = refs[:10]
-    chunks = [(wq, oq, 0, wq.shape[0] // 2), (wq, oq, wq.shape[0] // 2, wq.shape[0] // 2), (wk, ok, 0, wk.shape[0]), (wv, ov, 0, wv.shape[0])]
+    wq, wk, wv, dq, dk, dv, pq, pk, pv, x_hbm, dy_hbm, g_ref, dgq, dgk, oq, ok, ov, odx, ogains = refs[:19]
+    chunks = [(wk, ok, 0, wk.shape[0]), (wv, ov, 0, wv.shape[0]), (wq, oq, 0, wq.shape[0] // 2), (wq, oq, wq.shape[0] // 2, wq.shape[0] // 2)]
     nc = len(chunks)
-    acc, r1, r2, r3 = (refs[10 + i * nc:10 + (i + 1) * nc] for i in range(4))
-    gbuf, xbuf, send, recv, loc, xsend, xrecv, gsend, grecv, lsem = refs[10 + 4 * nc:]
+    acc, r1, r2, r3 = (refs[19 + i * nc:19 + (i + 1) * nc] for i in range(4))
+    (vq, vk, vv, bq, bk, bv, bx, by, dn, dxb, gpack, gbuf,
+     send, recv, loc, xsend, xrecv, gsend, grecv, lsem, wsem, bsem) = refs[19 + 4 * nc:]
     me = lax.axis_index('sp')
     c, x, y = me % 2, (me // 2) % 2, me // 4
     pn, xn, yn = me + 1 - 2 * c, me + 2 - 4 * x, me + 4 - 8 * y
@@ -197,9 +178,11 @@
 
     def add(dst, d0, src, s0, n):
         step = 8
+
         def body(i, _):
             dst[pl.ds(pl.multiple_of(d0 + i * step, 8), step), :] += src[pl.ds(pl.multiple_of(s0 + i * step, 8), step), :]
             return 0
+
         lax.fori_loop(0, n // step, body, 0, unroll=2)
 
     started = []
@@ -213,7 +196,7 @@
     flight = {}
 
     def s1(i):
-        src, out, row0, n = chunks[i]
+        src, _, row0, n = chunks[i]
         half = n // 2
         mine = pltpu.make_async_copy(src.at[pl.ds(pl.multiple_of(row0 + c * half, 8), half), :], acc[i], loc.at[i, 0])
         mine.start()
@@ -277,43 +260,112 @@
         rows = out.at[pl.ds(pl.multiple_of(row0 + c * (n // 2), 8), n // 2), :]
         flight[i, 6] = go([rdma(rows, rows, i, 11, pn)])
 
-    rows = dx.shape[1]
-
-    def send_dx(d):
-        to = me + (1 - 2 * c) * (d % 2) + (2 - 4 * x) * ((d // 2) % 2) + (4 - 8 * y) * (d // 4)
-        cp = pltpu.make_async_remote_copy(src_ref=dx.at[to], dst_ref=odx.at[pl.ds(pl.multiple_of(me * rows, rows), rows)],
-                                          send_sem=xsend.at[d], recv_sem=xrecv.at[d], device_id=(to,), device_id_type=MESH)
-        cp.start()
-        return cp
+    _, rows, tok, dim = x_hbm.shape
+    sb = bx.shape[1]
+    n_blk = n_dev // sb
+    ntok = sb * rows * tok
+    loads = [pltpu.make_async_copy(a, b, wsem.at[i]) for i, (a, b) in enumerate(((pq, vq), (pk, vk), (pv, vv)))]
+    order = [(2 - 4 * x) // sb, (4 - 8 * y) // sb, (2 - 4 * x + 4 - 8 * y) // sb, 0]
+    blocks = [me // sb + o for o in order]
+
+    def fetch(b):
+        src = pl.ds(pl.multiple_of(blocks[b] * sb, sb), sb)
+        cps = [pltpu.make_async_copy(a.at[src], v.at[b % 2], bsem.at[b % 2, i])
+               for i, (a, v) in enumerate(((dq, bq), (dk, bk), (dv, bv), (x_hbm, bx), (dy_hbm, by)))]
+        for cp in cps:
+            cp.start()
+        return cps
+
+    xcopies = []
+    local_out = []
+
+    def dx_block(b, fetched):
+        for cp in fetched:
+            cp.wait()
+
+        def col(j, _):
+            cols = pl.ds(pl.multiple_of(j * 256, 256), 256)
+            dn[:, cols] = functools.reduce(jnp.add, [
+                lax.dot_general(d[b % 2].reshape(ntok, d.shape[-1]), w[cols, :], NT, preferred_element_type=F32)
+                for d, w in ((bq, vq), (bk, vk), (bv, vv))])
+            return 0
+
+        lax.fori_loop(0, dim // 256, col, 0)
+
+        def tail_rows(j, _):
+            part = pl.ds(pl.multiple_of(j * tok, tok), tok)
+            si, ri = j // rows, j % rows
+            d = dn[part, :]
+            xv = bx[b % 2, si, ri].astype(F32)
+            r = lax.rsqrt(jnp.mean(xv * xv, axis=-1, keepdims=True) + NORM_EPS)
+            xh = xv * r
+            gpack[:, pl.ds(0, dim)] += jnp.sum((d * xh).reshape(tok // 8, 8, dim), axis=0)
+            dng = d * g_ref[...]
+            dx = r * (dng - xh * jnp.mean(dng * xh, axis=-1, keepdims=True))
+            dxb[b, si, ri] = (by[b % 2, si, ri].astype(F32) + dx).astype(BF16)
+            return 0
+
+        lax.fori_loop(0, sb * rows, tail_rows, 0)
+        home = odx.at[pl.ds(pl.multiple_of(me * rows, rows), rows)]
+        for si in range(sb):
+            core = (c + si) % 2
+            to = blocks[b] * sb + core
+            if b == n_blk - 1 and si == 0:
+                cp = pltpu.make_async_copy(dxb.at[b, core], home, lsem.at[0])
+                local_out.append(cp)
+            else:
+                cp = pltpu.make_async_remote_copy(src_ref=dxb.at[b, core], dst_ref=home, send_sem=xsend.at[b, si], recv_sem=xrecv.at[b, si],
+                                                  device_id=(to,), device_id_type=MESH)
+                xcopies.append(cp)
+            cp.start()
 
     for i in range(nc):
         s1(i)
+    for cp in loads:
+        cp.start()
+    fetched = {0: fetch(0)}
+    gpack[:, pl.ds(0, dim)] = jnp.zeros((8, dim), F32)
+    gpack[:, pl.ds(dim, HD)] = dgq[...]
+    gpack[:, pl.ds(dim + HD, HD)] = dgk[...]
+    fetched[1] = fetch(1)
+    for i in range(nc):
+        s2(i)
+    for cp in loads:
+        cp.wait()
+    dx_block(0, fetched[0])
+    fetched[2] = fetch(2)
+    s3(0)
+    s3(1)
+    dx_block(1, fetched[1])
+    fetched[3] = fetch(3)
+    s4(0)
+    s3(2)
+    s4(1)
+    s3(3)
+    dx_block(2, fetched[2])
+    s5(0)
+    s4(2)
+    s5(1)
+    s4(3)
+    dx_block(3, fetched[3])
     gcopies = []
     for d in range(1, n_dev):
-        cp = pltpu.make_async_remote_copy(src_ref=gains, dst_ref=gbuf.at[d - 1], send_sem=gsend.at[d], recv_sem=grecv.at[d],
+        cp = pltpu.make_async_remote_copy(src_ref=gpack, dst_ref=gbuf.at[d - 1], send_sem=gsend.at[d], recv_sem=grecv.at[d],
                                           device_id=(peers[d - 1],), device_id_type=MESH)
         cp.start()
         gcopies.append(cp)
-    keep_in = pltpu.make_async_copy(dx.at[me], xbuf, lsem.at[0])
-    keep_in.start()
-    xcopies = [send_dx(d) for d in (2, 4, 1)]
-    filler = [3, 5, 6, 7]
-    stages = [s2, s3, s4, s5, s6]
-    keep_out = None
-    for t in range(nc + len(stages) - 1):
-        for k in reversed(range(len(stages))):
-            if 0 <= t - k < nc:
-                stages[k](t - k)
-        if t >= 2 and filler:
-            xcopies.append(send_dx(filler.pop(0)))
-        if t == 1:
-            keep_in.wait()
-            keep_out = pltpu.make_async_copy(xbuf, odx.at[pl.ds(pl.multiple_of(me * rows, rows), rows)], lsem.at[1])
-            keep_out.start()
+    s6(0)
+    s5(2)
+    s6(1)
+    s5(3)
+    s6(2)
+    s6(3)
     for cp in gcopies:
         cp.wait()
-    ogains[...] = gains[...] + functools.reduce(jnp.add, [gbuf[d] for d in range(n_dev - 1)])
-    keep_out.wait()
+    total = gpack[...] + functools.reduce(jnp.add, [gbuf[d] for d in range(n_dev - 1)])
+    ogains[...] = jnp.sum(total, axis=0, keepdims=True)
+    for cp in local_out:
+        cp.wait()
     for i in range(nc):
         flight[i, 6][0].wait_recv()
     for cp in started:
@@ -322,22 +374,27 @@
         cp.wait()
 
 
-def finish(n_dev, dwq, dwk, dwv, dx, gains):
-    nd, rows, tok, dim = dx.shape
+def finish(n_dev, parts, d_parts, weights, x, dy, g2, dgq, dgk):
+    dwq, dwk, dwv = parts
+    nd, rows, tok, dim = x.shape
+    sb = 2
     hbm, vmem = pl.BlockSpec(memory_space=pl.ANY), pl.BlockSpec(memory_space=pltpu.VMEM)
-    sizes = [(dwq.shape[0] // 2, dwq.shape[1])] * 2 + [dwk.shape, dwv.shape]
+    sizes = [dwk.shape, dwv.shape] + [(dwq.shape[0] // 2, dwq.shape[1])] * 2
     nc = len(sizes)
     dma = pltpu.SemaphoreType.DMA
     scratch = [pltpu.VMEM((r // 2, w), F32) for r, w in sizes] + [pltpu.VMEM((r // 2, w), F32) for r, w in sizes]
     scratch += [pltpu.VMEM((2, r // 8, w), F32) for r, w in sizes] + [pltpu.VMEM((2, r // 16, w), F32) for r, w in sizes]
-    scratch += [pltpu.VMEM((n_dev - 1,) + gains.shape, F32), pltpu.VMEM((rows, tok, dim), BF16)]
-    scratch += [dma((nc, 12)), dma((nc, 12)), dma((nc, 3)), dma((n_dev,)), dma((n_dev,)), dma((n_dev,)), dma((n_dev,)), dma((2,))]
+    scratch += [pltpu.VMEM(w.shape, BF16) for w in weights]
+    scratch += [pltpu.VMEM((2, sb, rows, tok, d.shape[-1]), BF16) for d in (*d_parts, x, dy)]
+    scratch += [pltpu.VMEM((sb * rows * tok, dim), F32), pltpu.VMEM((nd // sb, sb, rows, tok, dim), BF16)]
+    scratch += [pltpu.VMEM((8, dim + 2 * HD), F32), pltpu.VMEM((n_dev - 1, 8, dim + 2 * HD), F32)]
+    scratch += [dma((nc, 12)), dma((nc, 12)), dma((nc, 3)), dma((nd // sb, sb)), dma((nd // sb, sb)), dma((n_dev,)), dma((n_dev,)), dma((1,)), dma((3,)), dma((2, 5))]
     return pl.pallas_call(
-        functools.partial(tail_kernel, n_dev), in_specs=[hbm] * 4 + [vmem], out_specs=[hbm] * 4 + [vmem],
-        out_shape=[jax.ShapeDtypeStruct(a.shape, F32) for a in (dwq, dwk, dwv)] + [
-            jax.ShapeDtypeStruct((nd * rows, tok, dim), BF16), jax.ShapeDtypeStruct(gains.shape, F32)],
+        functools.partial(tail_kernel, n_dev), in_specs=[hbm] * 11 + [vmem] * 3, out_specs=[hbm] * 4 + [vmem],
+        out_shape=[jax.ShapeDtypeStruct(a.shape, F32) for a in parts] + [
+            jax.ShapeDtypeStruct((nd * rows, tok, dim), BF16), jax.ShapeDtypeStruct((1, dim + 2 * HD), F32)],
         scratch_shapes=scratch, compiler_params=params(collective_id=0, has_side_effects=True), name='tail',
-    )(dwq, dwk, dwv, dx, gains)
+    )(*parts, *d_parts, *weights, x, dy, g2, dgq, dgk)
 
 
 def params(**kw):
@@ -400,20 +457,10 @@
             compiler_params=params(), cost_estimate=cost(10 * n_tok * n_pos * qw, 60e6), name='attn_bwd',
         )(rot, raw, d_o, gq2, gk2, cos_t, sin_t)
 
-        dq, y_out = lax.optimization_barrier((dq, y_out))
         h2 = h.reshape(n_tok, dim)
         d_wq, d_wk, d_wv = (lax.dot_general(h2, d.reshape(n_tok, -1), (((0,), (0,)), ((), ())), preferred_element_type=F32) for d in (dq, dk, dv))
-        dx, dg = pl.pallas_call(
-            dx_kernel, grid=(n_dev // sb,),
-            in_specs=[tokspec(qw), tokspec(n_kv * HD), tokspec(n_kv * HD), full(*w_q.shape), full(*w_k.shape), full(*w_v.shape), tokspec(dim), tokspec(dim), full(1, dim)],
-            out_specs=[tokspec(dim), full(8, dim)],
-            out_shape=[shp(dim), jax.ShapeDtypeStruct((8, dim), F32)],
-            compiler_params=params(), cost_estimate=cost(2 * n_tok * dim * 4 * HD * n_kv, 40e6), name='dx',
-        )(dq, dk, dv, w_q, w_k, w_v, x, dy, g2)
         d_wo = lax.psum(d_wo, 'sp')
-        gains = jnp.concatenate([jnp.sum(dg, 0), jnp.sum(dgq, 0), jnp.sum(dgk, 0)])
-        gains = jnp.pad(gains, (0, -gains.size % 1024)).reshape(-1, 128)
-        d_wq, d_wk, d_wv, d_hidden, gains = finish(n_dev, d_wq, d_wk, d_wv, dx, gains)
+        d_wq, d_wk, d_wv, d_hidden, gains = finish(n_dev, (d_wq, d_wk, d_wv), (dq, dk, dv), (w_q, w_k, w_v), x, dy, g2, dgq, dgk)
         gains = gains.reshape(-1)
         return (y_out, d_hidden, d_wq, d_wk, d_wv, d_wo, gains[:dim], gains[dim:dim + HD], gains[dim + HD:dim + 2 * HD])
 

time: 661 us -> 613 us (0.927)
  waiting for transfers between devices: 54.4 us -> 0.02 us
  Pallas kernels: 417 us -> 430 us
    all_to_all x1, waiting for transfers between devices: 54.4 us -> 0.01 us  [local_step(): y_out = lax.all_to_all(y.reshape(n_batch, tok, dim), 'sp', 0, 0, tiled=True)]
    pallas_call x2 -> x1, Pallas kernels: 220 us -> 232 us  [finish(): pl.pallas_call(functools.partial(tail_kernel, n_dev), in_specs=[hbm] * 11...]
    unnamed x26 -> x30, local copies, waits for them, and re-layouts: 25.7 us -> 25.7 us
  transfers between devices with their start and end apart: 3 -> 3, of which waited for: 1 -> 0; matrix products, arithmetic and copies ran while one was open for 6% -> 5% of each run, Pallas kernels for 64% -> 71%
where the time goes in v2:
time: 613 us; the launch traced here: 605 us
  Pallas kernels  430 us (70%)
  matrix products  69.8 us (11%)
  blocking collectives  53.4 us (9%)
  local copies, waits for them, and re-layouts  28.1 us (5%)
  between operations  14.4 us (2%)
  starting transfers between devices  6.81 us (1%)
    pallas_call x1, Pallas kernels, finish(): pl.pallas_call(functools.partial(tail_kernel, n_dev), in_specs=[hbm] * 11...  232 us
    pallas_call x1, Pallas kernels, local_step(): pl.pallas_call(attn_bwd_kernel, grid=(rows, n_kv), in_specs=[head_spec(4...  86.7 us
    pallas_call x1, Pallas kernels, local_step(): pl.pallas_call(qkv_kernel, grid=(n_dev // sb,), in_specs=[tokspec(dim), f...  56.5 us
    pallas_call x1, Pallas kernels, local_step(): pl.pallas_call(attn_fwd_kernel, grid=(rows, n_kv), in_specs=[head_spec(4...  54.7 us
    all_to_all x1, blocking collectives, local_step(): lax.all_to_all(hidden, 'sp', 0, 0, tiled=True)  53.4 us
    dot_general x3, matrix products, local_step(): lax.dot_general(h2, d.reshape(n_tok, -1), (((0,), (0,)), ((), ())), prefe...  28.1 us
    unnamed x30, local copies, waits for them, and re-layouts  25.7 us
    dot_general x1, matrix products, local_step(): jnp.dot(o2, w_o, preferred_element_type=F32)  14.4 us
  transfers between devices with their start and end apart: 3, of which 0 were waited for; matrix products, arithmetic and copies ran while one was open for 5% of the time, Pallas kernels for 71%

profile of v2, /device:TPU:0, one launch (start us, length us, event | category | flops | bytes accessed | tf_op | source)
XLA Modules:
  0.0 604.6 jit_solution(5291519372145222259)
XLA Ops:
  7.2 53.4 %all_to_all.15 = bf16[32,64,1024]{2,1,0:T(8,128)(2,1)} all-to-all(bf16[32,64,1024]{2,1,0:T(8,128)(2,1)} %param.9), channel_id=1, replica_groups=mesh['sp'=8] {'sp'}, dimensions={0} | all-to-all | bytes 8388608 | tf_op jit(solution)/shard_map/all_to_all | solution.py:423
  60.6 3.3 all-to-all-start.1
  66.0 56.5 %qkv.1 = (bf16[8,4,64,1024]{3,2,1,0:T(8,128)(2,1)}, bf16[8,4,64,3072]{3,2,1,0:T(8,128)(2,1)}, bf16[8,4,64,4096]{3,2,1,0:T(8,128)(2,1)}) custom-call(bf16[8,4,64,1024]{3,2,1,0:T(8,128)(2,1)} %bitcast.41, f32[1,1024]{1,0:T(1,128)} %bitcast.50, bf16[1024,2048]{1,0:T(8,128)(2,1)} %refs_6_.1, bf16[1024,1024]{1,0:T(8,128)(2,1)} %refs_7_.1, ...), custom_call_target="tpu_custom_call" | custom-call | flops 17179869184 | bytes 40000000 | tf_op jit(solution)/shard_map/qkv/pallas_call | solution.py:430
  122.5 54.7 %attn_fwd.1 = bf16[8,4,64,2048]{3,2,1,0:T(8,128)(2,1)} custom-call(bf16[8,4,64,4096]{3,2,1,0:T(8,128)(2,1)} %get-tuple-element.25.rot_ref), custom_call_target="tpu_custom_call" | custom-call | flops 8589934592 | bytes 24000000 | tf_op jit(solution)/shard_map/attn_fwd/pallas_call | solution.py:440
  177.2 14.1 %convolution_convert_fusion = bf16[2048,2048]{1,0:T(8,128)(2,1)} fusion(bf16[2048,1024]{1,0:T(8,128)(2,1)} %bitcast.6, bf16[2048,1024]{1,0:T(8,128)(2,1)} %param.16), kind=kOutput, calls=%fused_computation.2 | convolution fusion | flops 8594128896 | bytes 16777216 | tf_op jit(solution)/shard_map/dot_general | solution.py:447
  191.3 13.2 %fusion.2 = f32[2048,1024]{1,0:T(8,128)} fusion(bf16[2048,2048]{1,0:T(8,128)(2,1)S(1)} %bitcast.59, bf16[2048,1024]{1,0:T(8,128)(2,1)} %bitcast.6), kind=kOutput, calls=%fused_computation.15 | convolution fusion | flops 8589934592 | bytes 20971520 | tf_op jit(solution)/shard_map/dot_general | solution.py:446
  204.5 14.4 %fusion = bf16[2048,1024]{1,0:T(8,128)(2,1)} fusion(bf16[32,64,1024]{2,1,0:T(8,128)(2,1)} %all_to_all.15, bf16[2048,2048]{1,0:T(8,128)(2,1)} %bitcast.58, bf16[2048,1024]{1,0:T(8,128)(2,1)} %param.16), kind=kOutput, calls=%fused_computation.1 | convolution fusion | flops 8596226048 | bytes 20971520 | tf_op jit(solution)/shard_map/dot_general | solution.py:445
  218.9 3.5 all-to-all-start.2
  222.4 86.7 %attn_bwd.1 = (bf16[8,4,64,2048]{3,2,1,0:T(8,128)(2,1)}, bf16[8,4,64,1024]{3,2,1,0:T(8,128)(2,1)}, bf16[8,4,64,1024]{3,2,1,0:T(8,128)(2,1)}, f32[8,128]{1,0:T(8,128)}, f32[8,128]{1,0:T(8,128)}) custom-call(bf16[8,4,64,4096]{3,2,1,0:T(8,128)(2,1)} %get-tuple-element.25.rot_ref, bf16[8,4,64,3072]{3,2,1,0:T(8,128)(2,1)} %get-tuple-element.28.raw_ref, ...), custom_call_target="tpu_custom_call" | custom-call | flops 21474836480 | bytes 60000000 | tf_op jit(solution)/shard_map/attn_bwd/pallas_call | solution.py:451
  309.2 10.2 %convolution_bitcast_fusion.2.refs_1_ = f32[1024,1024]{1,0:T(8,128)} fusion(bf16[8,4,64,1024]{3,2,1,0:T(8,128)(2,1)} %get-tuple-element.27, bf16[8,4,64,1024]{3,2,1,0:T(8,128)(2,1)} %get-tuple-element.31.refs_4_), kind=kOutput, calls=%fused_computation.5 | convolution fusion | flops 4294967296 | bytes 12582912 | tf_op jit(solution)/shard_map/dot_general | solution.py:461
  319.4 6.1 %convolution_bitcast_fusion.1.refs_2_ = f32[1024,1024]{1,0:T(8,128)} fusion(bf16[8,4,64,1024]{3,2,1,0:T(8,128)(2,1)S(1)} %copy-done.5, bf16[8,4,64,1024]{3,2,1,0:T(8,128)(2,1)S(1)} %copy-done.3), kind=kOutput, calls=%fused_computation.4 | convolution fusion | flops 4294967296 | bytes 12582912 | tf_op jit(solution)/shard_map/dot_general | solution.py:461
  325.5 11.7 %convolution_bitcast_fusion.refs_0_ = f32[1024,2048]{1,0:T(8,128)} fusion(bf16[8,4,64,1024]{3,2,1,0:T(8,128)(2,1)S(1)} %copy-done.5, bf16[8,4,64,2048]{3,2,1,0:T(8,128)(2,1)S(1)} %bitcast.48), kind=kOutput, calls=%fused_computation.3 | convolution fusion | flops 8589934592 | bytes 20971520 | tf_op jit(solution)/shard_map/dot_general | solution.py:461
  337.2 232.2 %tail.1 = (f32[1024,2048]{1,0:T(8,128)}, f32[1024,1024]{1,0:T(8,128)}, f32[1024,1024]{1,0:T(8,128)}, bf16[32,64,1024]{2,1,0:T(8,128)(2,1)}, f32[1,1280]{1,0:T(1,128)}) custom-call(f32[1024,2048]{1,0:T(8,128)} %convolution_bitcast_fusion.refs_0_, f32[1024,1024]{1,0:T(8,128)} %convolution_bitcast_fusion.2.refs_1_, ...), custom_call_target="tpu_custom_call" | custom-call | tf_op jit(solution)/shard_map/tail/pallas_call | solution.py:392
  569.5 1.3 slice.18
  570.7 1.1 slice_bitcast_fusion
  571.9 5.2 copy.27
  577.1 2.1 copy.28
  579.2 1.8 slice-done.3
  581.0 4.3 copy.29
  586.3 2.1 copy.30
  588.4 1.6 copy-done
  590.0 2.1 copy.31
  592.1 2.1 slice-done.1
  594.2 3.4 copy.32
  (33 shorter events, 3.1 us)
Async XLA Ops:
  60.6 116.6 %all-to-all-start.1 = ((bf16[32,64,1024]{2,1,0:T(8,128)(2,1)}), bf16[32,64,1024]{2,1,0:T(8,128)(2,1)}, u32[]{:S(2)}, u32[]{:S(2)}) async-start(bf16[32,64,1024]{2,1,0:T(8,128)(2,1)} %param.17), calls=%async_computation.1 | async-start | bytes 8388608 | tf_op jit(solution)/shard_map/all_to_all | solution.py:424
  63.9 508.0 %all-reduce.2.cloned.1.call-start = ((), (), s32[]{:S(2)}) async-start(), calls=%async_computation.3 | async-start | bytes 16777216 | tf_op jit(solution)/shard_map/psum | solution.py:462
  177.2 14.1 %copy-start.4 = (bf16[8,4,64,2048]{3,2,1,0:T(8,128)(2,1)S(1)}, bf16[8,4,64,2048]{3,2,1,0:T(8,128)(2,1)}, u32[]{:S(2)}) copy-start(bf16[8,4,64,2048]{3,2,1,0:T(8,128)(2,1)} %attn_fwd.1) | copy-start | bytes 25165828
  218.9 352.9 %all-to-all-start.2 = ((bf16[32,64,1024]{2,1,0:T(8,128)(2,1)}), bf16[32,64,1024]{2,1,0:T(8,128)(2,1)}, u32[]{:S(2)}, u32[]{:S(2)}) async-start(bf16[32,64,1024]{2,1,0:T(8,128)(2,1)} %bitcast.49), calls=%async_computation.2 | async-start | bytes 8388608 | tf_op jit(solution)/shard_map/all_to_all | solution.py:449
  309.1 10.2 %copy-start.3 = (bf16[8,4,64,1024]{3,2,1,0:T(8,128)(2,1)S(1)}, bf16[8,4,64,1024]{3,2,1,0:T(8,128)(2,1)}, u32[]{:S(2)}) copy-start(bf16[8,4,64,1024]{3,2,1,0:T(8,128)(2,1)} %get-tuple-element.32.refs_5_) | copy-start | bytes 12582916
  309.1 10.2 %copy-start.5 = (bf16[8,4,64,1024]{3,2,1,0:T(8,128)(2,1)S(1)}, bf16[8,4,64,1024]{3,2,1,0:T(8,128)(2,1)}, u32[]{:S(2)}) copy-start(bf16[8,4,64,1024]{3,2,1,0:T(8,128)(2,1)} %get-tuple-element.27) | copy-start | bytes 12582916
  309.2 16.4 %slice-start.4 = ((s8[8388608]{0:T(1024)(128)(4,1)}), s8[4194304]{0:T(1024)(128)(4,1)S(1)}, s32[]{:S(2)}) async-start(s8[8388608]{0:T(1024)(128)(4,1)} %bitcast.47), calls=%async_computation.8 | async-start | bytes 8388608
  319.4 6.1 %slice-start.5 = ((s8[8388608]{0:T(1024)(128)(4,1)}), s8[4194304]{0:T(1024)(128)(4,1)S(1)}, s32[]{:S(2)}) async-start(s8[8388608]{0:T(1024)(128)(4,1)} %bitcast.47), calls=%async_computation.9 | async-start | bytes 8388608
  571.9 5.2 copy-start.2
  571.9 7.3 %slice-start.2 = ((s8[8388608]{0:T(1024)(128)(4,1)}), s8[4194304]{0:T(1024)(128)(4,1)S(1)}, s32[]{:S(2)}) async-start(s8[8388608]{0:T(1024)(128)(4,1)} %bitcast.45), calls=%async_computation.6 | async-start | bytes 8388608
  577.1 4.0 slice-start.3
  581.0 5.2 copy-start.1
  586.3 3.7 copy-start
  586.3 5.8 slice-start
  590.0 4.2 slice-start.1
Sparse Core Ops, SparseCore 0:
  219.0 194.7 all-reduce.1

commit v3 on v2

--- a/solution.py
+++ b/solution.py
@@ -93,7 +93,141 @@
             o_ref[pl.ds(qb * src_b, src_b), 0, :, pl.ds(head * HD, HD)] = o_t.T.astype(BF16).reshape(src_b, o_ref.shape[2], HD)
 
 
-def attn_bwd_kernel(rot_ref, raw_ref, do_ref, gq_ref, gk_ref, cos_ref, sin_ref, oq_ref, ok_ref, ov_ref, dgq_ref, dgk_ref, dk_acc, dv_acc):
+MESH = pl.DeviceIdType.MESH
+
+
+class Reducer:
+    def __init__(self, chunks, acc, r1, r2, r3, send, recv, loc):
+        self.chunks, self.acc, self.r1, self.r2, self.r3 = chunks, acc, r1, r2, r3
+        self.send, self.recv, self.loc = send, recv, loc
+        me = lax.axis_index('sp')
+        self.me, self.c, self.x, self.y = me, me % 2, (me // 2) % 2, me // 4
+        self.pn, self.xn, self.yn = me + 1 - 2 * self.c, me + 2 - 4 * self.x, me + 4 - 8 * self.y
+
+    def barrier(self, n_dev):
+        sem = pltpu.get_barrier_semaphore()
+        for d in range(1, n_dev):
+            pl.semaphore_signal(sem, inc=1, device_id=((self.me + d) % n_dev,), device_id_type=MESH)
+        pl.semaphore_wait(sem, n_dev - 1)
+
+    def rdma(self, src, dst, ci, slot, dev):
+        return pltpu.make_async_remote_copy(src_ref=src, dst_ref=dst, send_sem=self.send.at[ci, slot], recv_sem=self.recv.at[ci, slot],
+                                            device_id=(dev,), device_id_type=MESH)
+
+    @staticmethod
+    def rows(ref, at, n):
+        return ref.at[pl.ds(pl.multiple_of(at, 8), n), :]
+
+    def remote(self, i, k):
+        src, out, row0, n = self.chunks[i]
+        c, x, y, pn, xn, yn = self.c, self.x, self.y, self.pn, self.xn, self.yn
+        acc, rows = self.acc[i], self.rows
+        half, e, f = n // 2, n // 8, n // 16
+        base = row0 + c * half
+        p1, q1 = x * e, n // 4 + y * e
+        p, q = p1 + y * f, q1 + x * f
+        if k == 1:
+            return [self.rdma(rows(src, row0 + (1 - c) * half, half), self.r1[i], i, 0, pn)]
+        if k == 2:
+            return [self.rdma(rows(acc, (1 - x) * e, e), self.r2[i].at[0], i, 1, xn),
+                    self.rdma(rows(acc, n // 4 + (1 - y) * e, e), self.r2[i].at[1], i, 2, yn)]
+        if k == 3:
+            return [self.rdma(rows(acc, p1 + (1 - y) * f, f), self.r3[i].at[0], i, 3, yn),
+                    self.rdma(rows(acc, q1 + (1 - x) * f, f), self.r3[i].at[1], i, 4, xn)]
+        if k == 4:
+            ps, qs, po, qo = rows(acc, p, f), rows(acc, q, f), rows(out, base + p, f), rows(out, base + q, f)
+            return [self.rdma(ps, po, i, 5, yn), self.rdma(qs, qo, i, 6, xn), self.rdma(ps, po, i, 7, xn), self.rdma(qs, qo, i, 8, yn)]
+        if k == 5:
+            po, qo = rows(out, base + p1 + (1 - y) * f, f), rows(out, base + q1 + (1 - x) * f, f)
+            return [self.rdma(po, po, i, 9, xn), self.rdma(qo, qo, i, 10, yn)]
+        mine = rows(out, base, half)
+        return [self.rdma(mine, mine, i, 11, pn)]
+
+    def local(self, i, k):
+        src, out, row0, n = self.chunks[i]
+        c, half, rows = self.c, n // 2, self.rows
+        base = row0 + c * half
+        if k == 1:
+            return [pltpu.make_async_copy(rows(src, base, half), self.acc[i], self.loc.at[i, 0])]
+        p, q = self.x * (n // 8) + self.y * (n // 16), n // 4 + self.y * (n // 8) + self.x * (n // 16)
+        return [pltpu.make_async_copy(rows(self.acc[i], at, n // 16), rows(out, base + at, n // 16), self.loc.at[i, 1 + j]) for j, at in enumerate((p, q))]
+
+    def add(self, i, at, src, n):
+        dst = self.acc[i]
+
+        def body(j, _):
+            dst[pl.ds(pl.multiple_of(at + j * 8, 8), 8), :] += src[pl.ds(pl.multiple_of(j * 8, 8), 8), :]
+            return 0
+
+        lax.fori_loop(0, n // 8, body, 0, unroll=2)
+
+    def stage(self, i, k):
+        n = self.chunks[i][3]
+        e, f = n // 8, n // 16
+        p1, q1 = self.x * e, n // 4 + self.y * e
+        if k == 2:
+            self.local(i, 1)[0].wait()
+        if k == 6:
+            for cp in self.local(i, 4):
+                cp.wait()
+        before = self.remote(i, k - 1) if k > 1 else []
+        if k == 5:
+            before = before[:2]
+        if k == 6:
+            before = self.remote(i, 4)[2:] + before
+        for cp in before:
+            cp.wait_recv()
+        if k == 2:
+            self.add(i, 0, self.r1[i], n // 2)
+        elif k == 3:
+            self.add(i, p1, self.r2[i].at[0], e)
+            self.add(i, q1, self.r2[i].at[1], e)
+        elif k == 4:
+            self.add(i, p1 + self.y * f, self.r3[i].at[0], f)
+            self.add(i, q1 + self.x * f, self.r3[i].at[1], f)
+        if k in (1, 4):
+            for cp in self.local(i, k):
+                cp.start()
+        for cp in self.remote(i, k):
+            cp.start()
+
+    def drain(self):
+        for i in range(len(self.chunks)):
+            self.remote(i, 6)[0].wait_recv()
+            for k in range(1, 7):
+                for cp in self.remote(i, k):
+                    cp.wait_send()
+
+
+def reduce_scratch(sizes):
+    dma, nc = pltpu.SemaphoreType.DMA, len(sizes)
+    out = [pltpu.VMEM((r // 2, w), F32) for r, w in sizes] + [pltpu.VMEM((r // 2, w), F32) for r, w in sizes]
+    out += [pltpu.VMEM((2, r // 8, w), F32) for r, w in sizes] + [pltpu.VMEM((2, r // 16, w), F32) for r, w in sizes]
+    return out + [dma((nc, 12)), dma((nc, 12)), dma((nc, 3))]
+
+
+def reducer(chunks, refs):
+    nc = len(chunks)
+    return Reducer(chunks, *(refs[i * nc:(i + 1) * nc] for i in range(4)), *refs[4 * nc:4 * nc + 3])
+
+
+BWD_STAGES = {0: ((0, 1), (1, 1)), 3: ((0, 2), (1, 2)), 8: ((0, 3),), 12: ((1, 3),), 14: ((0, 4),), 16: ((1, 4),),
+              20: ((0, 5),), 24: ((1, 5),), 27: ((0, 6),), 29: ((1, 6),)}
+
+
+def attn_bwd_kernel(n_dev, rot_ref, raw_ref, do_ref, gq_ref, gk_ref, cos_ref, sin_ref, wo_part, oq_ref, ok_ref, ov_ref, dgq_ref, dgk_ref, wo_sum,
+                    dk_acc, dv_acc, *refs):
+    step = pl.program_id(0) * pl.num_programs(1) + pl.program_id(1)
+    n_half = wo_part.shape[0] // 2
+    red = reducer([(wo_part, wo_sum, 0, n_half), (wo_part, wo_sum, n_half, n_half)], refs)
+    for at, todo in BWD_STAGES.items():
+        @pl.when(step == at)
+        def _():
+            if at == 0:
+                red.barrier(n_dev)
+            for i, k in todo:
+                red.stage(i, k)
+
     n_src, _, tok, _ = rot_ref.shape
     n_pos = n_src * tok
     rot = rot_ref[...].reshape(n_pos, 4 * HD)
@@ -151,114 +285,20 @@
     ok_ref[:, 0] = dk_raw.reshape(n_src, tok, HD)
     ov_ref[:, 0] = dv_acc[...].astype(BF16).reshape(n_src, tok, HD)
 
-
-MESH = pl.DeviceIdType.MESH
+    @pl.when(step == pl.num_programs(0) * pl.num_programs(1) - 1)
+    def _():
+        red.drain()
 
 
 def tail_kernel(n_dev, *refs):
     wq, wk, wv, dq, dk, dv, pq, pk, pv, x_hbm, dy_hbm, g_ref, dgq, dgk, oq, ok, ov, odx, ogains = refs[:19]
     chunks = [(wk, ok, 0, wk.shape[0]), (wv, ov, 0, wv.shape[0]), (wq, oq, 0, wq.shape[0] // 2), (wq, oq, wq.shape[0] // 2, wq.shape[0] // 2)]
     nc = len(chunks)
-    acc, r1, r2, r3 = (refs[19 + i * nc:19 + (i + 1) * nc] for i in range(4))
+    red = reducer(chunks, refs[19:])
     (vq, vk, vv, bq, bk, bv, bx, by, dn, dxb, gpack, gbuf,
-     send, recv, loc, xsend, xrecv, gsend, grecv, lsem, wsem, bsem) = refs[19 + 4 * nc:]
-    me = lax.axis_index('sp')
-    c, x, y = me % 2, (me // 2) % 2, me // 4
-    pn, xn, yn = me + 1 - 2 * c, me + 2 - 4 * x, me + 4 - 8 * y
-    peers = [(me + d) % n_dev for d in range(1, n_dev)]
-
-    barrier = pltpu.get_barrier_semaphore()
-    for p in peers:
-        pl.semaphore_signal(barrier, inc=1, device_id=(p,), device_id_type=MESH)
-    pl.semaphore_wait(barrier, n_dev - 1)
-
-    def rdma(src, dst, ci, slot, dev):
-        return pltpu.make_async_remote_copy(src_ref=src, dst_ref=dst, send_sem=send.at[ci, slot], recv_sem=recv.at[ci, slot],
-                                            device_id=(dev,), device_id_type=MESH)
-
-    def add(dst, d0, src, s0, n):
-        step = 8
-
-        def body(i, _):
-            dst[pl.ds(pl.multiple_of(d0 + i * step, 8), step), :] += src[pl.ds(pl.multiple_of(s0 + i * step, 8), step), :]
-            return 0
-
-        lax.fori_loop(0, n // step, body, 0, unroll=2)
-
-    started = []
-
-    def go(copies):
-        for cp in copies:
-            cp.start()
-        started.extend(copies)
-        return copies
-
-    flight = {}
-
-    def s1(i):
-        src, _, row0, n = chunks[i]
-        half = n // 2
-        mine = pltpu.make_async_copy(src.at[pl.ds(pl.multiple_of(row0 + c * half, 8), half), :], acc[i], loc.at[i, 0])
-        mine.start()
-        flight[i, 1] = (mine, go([rdma(src.at[pl.ds(pl.multiple_of(row0 + (1 - c) * half, 8), half), :], r1[i], i, 0, pn)]))
-
-    def s2(i):
-        n = chunks[i][3]
-        mine, cps = flight[i, 1]
-        mine.wait()
-        cps[0].wait_recv()
-        add(acc[i], 0, r1[i], 0, n // 2)
-        e = n // 8
-        flight[i, 2] = go([rdma(acc[i].at[pl.ds(pl.multiple_of((1 - x) * e, 8), e), :], r2[i].at[0], i, 1, xn),
-                           rdma(acc[i].at[pl.ds(pl.multiple_of(n // 4 + (1 - y) * e, 8), e), :], r2[i].at[1], i, 2, yn)])
-
-    def s3(i):
-        n = chunks[i][3]
-        e, f = n // 8, n // 16
-        for cp in flight[i, 2]:
-            cp.wait_recv()
-        p1, q1 = x * e, n // 4 + y * e
-        add(acc[i], p1, r2[i].at[0], 0, e)
-        add(acc[i], q1, r2[i].at[1], 0, e)
-        flight[i, 3] = go([rdma(acc[i].at[pl.ds(pl.multiple_of(p1 + (1 - y) * f, 8), f), :], r3[i].at[0], i, 3, yn),
-                           rdma(acc[i].at[pl.ds(pl.multiple_of(q1 + (1 - x) * f, 8), f), :], r3[i].at[1], i, 4, xn)])
-
-    def s4(i):
-        _, out, row0, n = chunks[i]
-        e, f = n // 8, n // 16
-        for cp in flight[i, 3]:
-            cp.wait_recv()
-        p, q = x * e + y * f, n // 4 + y * e + x * f
-        add(acc[i], p, r3[i].at[0], 0, f)
-        add(acc[i], q, r3[i].at[1], 0, f)
-        base = row0 + c * (n // 2)
-        ps, qs = acc[i].at[pl.ds(pl.multiple_of(p, 8), f), :], acc[i].at[pl.ds(pl.multiple_of(q, 8), f), :]
-        po, qo = out.at[pl.ds(pl.multiple_of(base + p, 8), f), :], out.at[pl.ds(pl.multiple_of(base + q, 8), f), :]
-        mine = [pltpu.make_async_copy(ps, po, loc.at[i, 1]), pltpu.make_async_copy(qs, qo, loc.at[i, 2])]
-        for cp in mine:
-            cp.start()
-        flight[i, 4] = (mine, go([rdma(ps, po, i, 5, yn), rdma(qs, qo, i, 6, xn), rdma(ps, po, i, 7, xn), rdma(qs, qo, i, 8, yn)]))
-
-    def s5(i):
-        _, out, row0, n = chunks[i]
-        e, f = n // 8, n // 16
-        cps = flight[i, 4][1]
-        cps[0].wait_recv()
-        cps[1].wait_recv()
-        base = row0 + c * (n // 2)
-        po = out.at[pl.ds(pl.multiple_of(base + x * e + (1 - y) * f, 8), f), :]
-        qo = out.at[pl.ds(pl.multiple_of(base + n // 4 + y * e + (1 - x) * f, 8), f), :]
-        flight[i, 5] = go([rdma(po, po, i, 9, xn), rdma(qo, qo, i, 10, yn)])
-
-    def s6(i):
-        _, out, row0, n = chunks[i]
-        mine, cps = flight[i, 4]
-        for cp in mine:
-            cp.wait()
-        for cp in (cps[2], cps[3], *flight[i, 5]):
-            cp.wait_recv()
-        rows = out.at[pl.ds(pl.multiple_of(row0 + c * (n // 2), 8), n // 2), :]
-        flight[i, 6] = go([rdma(rows, rows, i, 11, pn)])
+     xsend, xrecv, gsend, grecv, lsem, wsem, bsem) = refs[19 + 4 * nc + 3:]
+    me, c, x, y = red.me, red.c, red.x, red.y
+    red.barrier(n_dev)
 
     _, rows, tok, dim = x_hbm.shape
     sb = bx.shape[1]
@@ -320,7 +360,7 @@
             cp.start()
 
     for i in range(nc):
-        s1(i)
+        red.stage(i, 1)
     for cp in loads:
         cp.start()
     fetched = {0: fetch(0)}
@@ -329,47 +369,44 @@
     gpack[:, pl.ds(dim + HD, HD)] = dgk[...]
     fetched[1] = fetch(1)
     for i in range(nc):
-        s2(i)
+        red.stage(i, 2)
     for cp in loads:
         cp.wait()
     dx_block(0, fetched[0])
     fetched[2] = fetch(2)
-    s3(0)
-    s3(1)
+    red.stage(0, 3)
+    red.stage(1, 3)
     dx_block(1, fetched[1])
     fetched[3] = fetch(3)
-    s4(0)
-    s3(2)
-    s4(1)
-    s3(3)
+    red.stage(0, 4)
+    red.stage(2, 3)
+    red.stage(1, 4)
+    red.stage(3, 3)
     dx_block(2, fetched[2])
-    s5(0)
-    s4(2)
-    s5(1)
-    s4(3)
+    red.stage(0, 5)
+    red.stage(2, 4)
+    red.stage(1, 5)
+    red.stage(3, 4)
     dx_block(3, fetched[3])
     gcopies = []
     for d in range(1, n_dev):
         cp = pltpu.make_async_remote_copy(src_ref=gpack, dst_ref=gbuf.at[d - 1], send_sem=gsend.at[d], recv_sem=grecv.at[d],
-                                          device_id=(peers[d - 1],), device_id_type=MESH)
+                                          device_id=((me + d) % n_dev,), device_id_type=MESH)
         cp.start()
         gcopies.append(cp)
-    s6(0)
-    s5(2)
-    s6(1)
-    s5(3)
-    s6(2)
-    s6(3)
+    red.stage(0, 6)
+    red.stage(2, 5)
+    red.stage(1, 6)
+    red.stage(3, 5)
+    red.stage(2, 6)
+    red.stage(3, 6)
     for cp in gcopies:
         cp.wait()
     total = gpack[...] + functools.reduce(jnp.add, [gbuf[d] for d in range(n_dev - 1)])
     ogains[...] = jnp.sum(total, axis=0, keepdims=True)
     for cp in local_out:
         cp.wait()
-    for i in range(nc):
-        flight[i, 6][0].wait_recv()
-    for cp in started:
-        cp.wait_send()
+    red.drain()
     for cp in xcopies:
         cp.wait()
 
@@ -380,15 +417,13 @@
     sb = 2
     hbm, vmem = pl.BlockSpec(memory_space=pl.ANY), pl.BlockSpec(memory_space=pltpu.VMEM)
     sizes = [dwk.shape, dwv.shape] + [(dwq.shape[0] // 2, dwq.shape[1])] * 2
-    nc = len(sizes)
     dma = pltpu.SemaphoreType.DMA
-    scratch = [pltpu.VMEM((r // 2, w), F32) for r, w in sizes] + [pltpu.VMEM((r // 2, w), F32) for r, w in sizes]
-    scratch += [pltpu.VMEM((2, r // 8, w), F32) for r, w in sizes] + [pltpu.VMEM((2, r // 16, w), F32) for r, w in sizes]
+    scratch = reduce_scratch(sizes)
     scratch += [pltpu.VMEM(w.shape, BF16) for w in weights]
     scratch += [pltpu.VMEM((2, sb, rows, tok, d.shape[-1]), BF16) for d in (*d_parts, x, dy)]
     scratch += [pltpu.VMEM((sb * rows * tok, dim), F32), pltpu.VMEM((nd // sb, sb, rows, tok, dim), BF16)]
     scratch += [pltpu.VMEM((8, dim + 2 * HD), F32), pltpu.VMEM((n_dev - 1, 8, dim + 2 * HD), F32)]
-    scratch += [dma((nc, 12)), dma((nc, 12)), dma((nc, 3)), dma((nd // sb, sb)), dma((nd // sb, sb)), dma((n_dev,)), dma((n_dev,)), dma((1,)), dma((3,)), dma((2, 5))]
+    scratch += [dma((nd // sb, sb)), dma((nd // sb, sb)), dma((n_dev,)), dma((n_dev,)), dma((1,)), dma((3,)), dma((2, 5))]
     return pl.pallas_call(
         functools.partial(tail_kernel, n_dev), in_specs=[hbm] * 11 + [vmem] * 3, out_specs=[hbm] * 4 + [vmem],
         out_shape=[jax.ShapeDtypeStruct(a.shape, F32) for a in parts] + [
@@ -446,20 +481,20 @@
         d_wo = lax.dot_general(o2, dy2, (((0,), (0,)), ((), ())), preferred_element_type=F32)
         d_o = lax.dot_general(dy2, w_o, (((1,), (1,)), ((), ())), preferred_element_type=F32).astype(BF16).reshape(n_dev, rows, tok, qw)
         y, d_wo, d_o = lax.optimization_barrier((y, d_wo, d_o))
+        dq, dk, dv, dgq, dgk, d_wo = pl.pallas_call(
+            functools.partial(attn_bwd_kernel, n_dev), grid=(rows, n_kv),
+            in_specs=[head_spec(4 * HD), head_spec(3 * HD), head_spec(2 * HD), full(1, HD), full(1, HD), full(n_pos, HD), full(n_pos, HD),
+                      pl.BlockSpec(memory_space=pl.ANY)],
+            out_specs=[head_spec(2 * HD), head_spec(HD), head_spec(HD), full(8, HD), full(8, HD), pl.BlockSpec(memory_space=pl.ANY)],
+            out_shape=[shp(qw), shp(n_kv * HD), shp(n_kv * HD), jax.ShapeDtypeStruct((8, HD), F32), jax.ShapeDtypeStruct((8, HD), F32),
+                       jax.ShapeDtypeStruct(d_wo.shape, F32)],
+            scratch_shapes=[pltpu.VMEM((n_pos, HD), F32), pltpu.VMEM((n_pos, HD), F32)] + reduce_scratch([(qw // 2, dim)] * 2),
+            compiler_params=params(collective_id=1, has_side_effects=True), cost_estimate=cost(10 * n_tok * n_pos * qw, 60e6), name='attn_bwd',
+        )(rot, raw, d_o, gq2, gk2, cos_t, sin_t, d_wo)
+        y, dq = lax.optimization_barrier((y, dq))
         y_out = lax.all_to_all(y.reshape(n_batch, tok, dim), 'sp', 0, 0, tiled=True)
-
-        dq, dk, dv, dgq, dgk = pl.pallas_call(
-            attn_bwd_kernel, grid=(rows, n_kv),
-            in_specs=[head_spec(4 * HD), head_spec(3 * HD), head_spec(2 * HD), full(1, HD), full(1, HD), full(n_pos, HD), full(n_pos, HD)],
-            out_specs=[head_spec(2 * HD), head_spec(HD), head_spec(HD), full(8, HD), full(8, HD)],
-            out_shape=[shp(qw), shp(n_kv * HD), shp(n_kv * HD), jax.ShapeDtypeStruct((8, HD), F32), jax.ShapeDtypeStruct((8, HD), F32)],
-            scratch_shapes=[pltpu.VMEM((n_pos, HD), F32), pltpu.VMEM((n_pos, HD), F32)],
-            compiler_params=params(), cost_estimate=cost(10 * n_tok * n_pos * qw, 60e6), name='attn_bwd',
-        )(rot, raw, d_o, gq2, gk2, cos_t, sin_t)
-
         h2 = h.reshape(n_tok, dim)
         d_wq, d_wk, d_wv = (lax.dot_general(h2, d.reshape(n_tok, -1), (((0,), (0,)), ((), ())), preferred_element_type=F32) for d in (dq, dk, dv))
-        d_wo = lax.psum(d_wo, 'sp')
         d_wq, d_wk, d_wv, d_hidden, gains = finish(n_dev, (d_wq, d_wk, d_wv), (dq, dk, dv), (w_q, w_k, w_v), x, dy, g2, dgq, dgk)
         gains = gains.reshape(-1)
         return (y_out, d_hidden, d_wq, d_wk, d_wv, d_wo, gains[:dim], gains[dim:dim + HD], gains[dim + HD:dim + 2 * HD])

time: 613 us -> 583 us (0.951)
  between operations: 14.4 us -> 0.98 us
  Pallas kernels: 430 us -> 417 us
    pallas_call x1, Pallas kernels: 232 us -> 210 us  [finish(): pl.pallas_call(functools.partial(tail_kernel, n_dev), in_specs=[hbm] * 11...]
    pallas_call x1, Pallas kernels: 86.7 us -> 95.3 us  [local_step(): pl.pallas_call(functools.partial(attn_bwd_kernel, n_dev), grid=(rows, n_k...]
    unnamed x30 -> x34, local copies, waits for them, and re-layouts: 25.7 us -> 25.7 us
  transfers between devices with their start and end apart: 3 -> 2, of which waited for: 0 -> 0; matrix products, arithmetic and copies ran while one was open for 5% -> 6% of each run, Pallas kernels for 71% -> 56%
where the time goes in v3:
time: 583 us; the launch traced here: 575 us
  Pallas kernels  417 us (72%)
  matrix products  66.6 us (11%)
  blocking collectives  53.4 us (9%)
  local copies, waits for them, and re-layouts  28.2 us (5%)
  starting transfers between devices  6.84 us (1%)
    pallas_call x1, Pallas kernels, finish(): pl.pallas_call(functools.partial(tail_kernel, n_dev), in_specs=[hbm] * 11...  210 us
    pallas_call x1, Pallas kernels, local_step(): pl.pallas_call(functools.partial(attn_bwd_kernel, n_dev), grid=(rows, n_k...  95.3 us
    pallas_call x1, Pallas kernels, local_step(): pl.pallas_call(qkv_kernel, grid=(n_dev // sb,), in_specs=[tokspec(dim), f...  56.5 us
    pallas_call x1, Pallas kernels, local_step(): pl.pallas_call(attn_fwd_kernel, grid=(rows, n_kv), in_specs=[head_spec(4...  54.7 us
    all_to_all x1, blocking collectives, local_step(): lax.all_to_all(hidden, 'sp', 0, 0, tiled=True)  53.4 us
    dot_general x3, matrix products, local_step(): lax.dot_general(h2, d.reshape(n_tok, -1), (((0,), (0,)), ((), ())), prefe...  27.8 us
    unnamed x34, local copies, waits for them, and re-layouts  25.7 us
    dot_general x1, matrix products, local_step(): lax.dot_general(dy2, w_o, (((1,), (1,)), ((), ())), preferred_element_typ...  14.1 us
  transfers between devices with their start and end apart: 2, of which 0 were waited for; matrix products, arithmetic and copies ran while one was open for 6% of the time, Pallas kernels for 56%

profile of v3, /device:TPU:0, one launch (start us, length us, event | category | flops | bytes accessed | tf_op | source)
XLA Modules:
  0.0 574.8 jit_solution(15968854492226756289)
XLA Ops:
  0.6 53.4 %all_to_all.15 = bf16[32,64,1024]{2,1,0:T(8,128)(2,1)} all-to-all(bf16[32,64,1024]{2,1,0:T(8,128)(2,1)} %param.9), channel_id=1, replica_groups=mesh['sp'=8] {'sp'}, dimensions={0} | all-to-all | bytes 8388608 | tf_op jit(solution)/shard_map/all_to_all | solution.py:458
  54.1 3.3 all-to-all-start.1
  59.4 56.5 %qkv.1 = (bf16[8,4,64,1024]{3,2,1,0:T(8,128)(2,1)}, bf16[8,4,64,3072]{3,2,1,0:T(8,128)(2,1)}, bf16[8,4,64,4096]{3,2,1,0:T(8,128)(2,1)}) custom-call(bf16[8,4,64,1024]{3,2,1,0:T(8,128)(2,1)} %bitcast.41, f32[1,1024]{1,0:T(1,128)} %bitcast.50, bf16[1024,2048]{1,0:T(8,128)(2,1)} %refs_6_.1, bf16[1024,1024]{1,0:T(8,128)(2,1)} %refs_7_.1, ...), custom_call_target="tpu_custom_call" | custom-call | flops 17179869184 | bytes 40000000 | tf_op jit(solution)/shard_map/qkv/pallas_call | solution.py:465
  115.9 54.7 %attn_fwd.1 = bf16[8,4,64,2048]{3,2,1,0:T(8,128)(2,1)} custom-call(bf16[8,4,64,4096]{3,2,1,0:T(8,128)(2,1)} %get-tuple-element.28.rot_ref), custom_call_target="tpu_custom_call" | custom-call | flops 8589934592 | bytes 24000000 | tf_op jit(solution)/shard_map/attn_fwd/pallas_call | solution.py:475
  170.6 14.1 %convolution_convert_fusion = bf16[2048,2048]{1,0:T(8,128)(2,1)} fusion(bf16[2048,1024]{1,0:T(8,128)(2,1)} %bitcast.6, bf16[2048,1024]{1,0:T(8,128)(2,1)} %param.16), kind=kOutput, calls=%fused_computation.2 | convolution fusion | flops 8594128896 | bytes 16777216 | tf_op jit(solution)/shard_map/dot_general | solution.py:482
  184.7 13.9 %fusion.2.wo_part = f32[2048,1024]{1,0:T(8,128)} fusion(bf16[2048,2048]{1,0:T(8,128)(2,1)S(1)} %bitcast.58, bf16[2048,1024]{1,0:T(8,128)(2,1)} %bitcast.6), kind=kOutput, calls=%fused_computation.15 | convolution fusion | flops 8589934592 | bytes 20971520 | tf_op jit(solution)/shard_map/dot_general | solution.py:481
  198.7 10.7 %fusion = bf16[2048,1024]{1,0:T(8,128)(2,1)} fusion(bf16[32,64,1024]{2,1,0:T(8,128)(2,1)S(1)} %copy-done, bf16[2048,2048]{1,0:T(8,128)(2,1)S(1)} %bitcast.59, bf16[2048,1024]{1,0:T(8,128)(2,1)S(1)} %copy-done.5), kind=kOutput, calls=%fused_computation.1 | convolution fusion | flops 8596226048 | bytes 20971520 | tf_op jit(solution)/shard_map/dot_general | solution.py:480
  209.3 95.3 %attn_bwd.1 = (bf16[8,4,64,2048]{3,2,1,0:T(8,128)(2,1)}, bf16[8,4,64,1024]{3,2,1,0:T(8,128)(2,1)}, bf16[8,4,64,1024]{3,2,1,0:T(8,128)(2,1)}, f32[8,128]{1,0:T(8,...) custom-call(bf16[8,4,64,4096]{3,2,1,0:T(8,128)(2,1)} %get-tuple-element.28.rot_ref, ...), custom_call_target="tpu_custom_call" | custom-call | flops 21474836480 | bytes 60000000 | tf_op jit(solution)/shard_map/attn_bwd/pallas_call | solution.py:484
  304.6 3.5 all-to-all-start.2
  308.2 10.2 %convolution_bitcast_fusion.2.refs_1_ = f32[1024,1024]{1,0:T(8,128)} fusion(bf16[8,4,64,1024]{3,2,1,0:T(8,128)(2,1)} %get-tuple-element.35, bf16[8,4,64,1024]{3,2,1,0:T(8,128)(2,1)} %get-tuple-element.37.refs_4_), kind=kOutput, calls=%fused_computation.5 | convolution fusion | flops 4294967296 | bytes 12582912 | tf_op jit(solution)/shard_map/dot_general | solution.py:497
  318.4 6.1 %convolution_bitcast_fusion.1.refs_2_ = f32[1024,1024]{1,0:T(8,128)} fusion(bf16[8,4,64,1024]{3,2,1,0:T(8,128)(2,1)S(1)} %copy-done.7, bf16[8,4,64,1024]{3,2,1,0:T(8,128)(2,1)S(1)} %copy-done.4), kind=kOutput, calls=%fused_computation.4 | convolution fusion | flops 4294967296 | bytes 12582912 | tf_op jit(solution)/shard_map/dot_general | solution.py:497
  324.5 11.5 %convolution_bitcast_fusion.refs_0_ = f32[1024,2048]{1,0:T(8,128)} fusion(bf16[8,4,64,1024]{3,2,1,0:T(8,128)(2,1)S(1)} %copy-done.7, bf16[8,4,64,2048]{3,2,1,0:T(8,128)(2,1)S(1)} %bitcast.48), kind=kOutput, calls=%fused_computation.3 | convolution fusion | flops 8589934592 | bytes 20971520 | tf_op jit(solution)/shard_map/dot_general | solution.py:497
  336.0 210.3 %tail.1 = (f32[1024,2048]{1,0:T(8,128)}, f32[1024,1024]{1,0:T(8,128)}, f32[1024,1024]{1,0:T(8,128)}, bf16[32,64,1024]{2,1,0:T(8,128)(2,1)}, f32[1,1280]{1,0:T(1,128)}) custom-call(f32[1024,2048]{1,0:T(8,128)} %convolution_bitcast_fusion.refs_0_, f32[1024,1024]{1,0:T(8,128)} %convolution_bitcast_fusion.2.refs_1_, ...), custom_call_target="tpu_custom_call" | custom-call | tf_op jit(solution)/shard_map/tail/pallas_call | solution.py:427
  546.4 1.3 slice.18
  547.6 1.2 slice_bitcast_fusion
  548.8 5.2 copy.27
  554.0 2.1 copy.28
  556.2 1.8 slice-done.3
  558.0 4.3 copy.29
  563.2 2.1 copy.30
  565.4 1.6 copy-done.1
  566.9 2.1 copy.31
  569.1 2.1 slice-done.1
  571.1 3.4 copy.32
  (34 shorter events, 3.0 us)
Async XLA Ops:
  54.1 116.5 %all-to-all-start.1 = ((bf16[32,64,1024]{2,1,0:T(8,128)(2,1)}), bf16[32,64,1024]{2,1,0:T(8,128)(2,1)}, u32[]{:S(2)}, u32[]{:S(2)}) async-start(bf16[32,64,1024]{2,1,0:T(8,128)(2,1)} %param.17), calls=%async_computation.1 | async-start | bytes 8388608 | tf_op jit(solution)/shard_map/all_to_all | solution.py:459
  170.6 14.1 %copy-start.6 = (bf16[8,4,64,2048]{3,2,1,0:T(8,128)(2,1)S(1)}, bf16[8,4,64,2048]{3,2,1,0:T(8,128)(2,1)}, u32[]{:S(2)}) copy-start(bf16[8,4,64,2048]{3,2,1,0:T(8,128)(2,1)} %attn_fwd.1) | copy-start | bytes 25165828
  184.7 14.0 %copy-start = (bf16[32,64,1024]{2,1,0:T(8,128)(2,1)S(1)}, bf16[32,64,1024]{2,1,0:T(8,128)(2,1)}, u32[]{:S(2)}) copy-start(bf16[32,64,1024]{2,1,0:T(8,128)(2,1)} %all_to_all.15) | copy-start | bytes 12582916
  184.7 14.0 %copy-start.5 = (bf16[2048,1024]{1,0:T(8,128)(2,1)S(1)}, bf16[2048,1024]{1,0:T(8,128)(2,1)}, u32[]{:S(2)}) copy-start(bf16[2048,1024]{1,0:T(8,128)(2,1)} %param.16) | copy-start | bytes 12582916
  304.6 244.2 %all-to-all-start.2 = ((bf16[32,64,1024]{2,1,0:T(8,128)(2,1)}), bf16[32,64,1024]{2,1,0:T(8,128)(2,1)}, u32[]{:S(2)}, u32[]{:S(2)}) async-start(bf16[32,64,1024]{2,1,0:T(8,128)(2,1)} %bitcast.49), calls=%async_computation.2 | async-start | bytes 8388608 | tf_op jit(solution)/shard_map/all_to_all | solution.py:495
  308.2 10.2 %copy-start.4 = (bf16[8,4,64,1024]{3,2,1,0:T(8,128)(2,1)S(1)}, bf16[8,4,64,1024]{3,2,1,0:T(8,128)(2,1)}, u32[]{:S(2)}) copy-start(bf16[8,4,64,1024]{3,2,1,0:T(8,128)(2,1)} %get-tuple-element.38.refs_5_) | copy-start | bytes 12582916
  308.2 10.2 %copy-start.7 = (bf16[8,4,64,1024]{3,2,1,0:T(8,128)(2,1)S(1)}, bf16[8,4,64,1024]{3,2,1,0:T(8,128)(2,1)}, u32[]{:S(2)}) copy-start(bf16[8,4,64,1024]{3,2,1,0:T(8,128)(2,1)} %get-tuple-element.35) | copy-start | bytes 12582916
  308.2 16.3 %slice-start.4 = ((s8[8388608]{0:T(1024)(128)(4,1)}), s8[4194304]{0:T(1024)(128)(4,1)S(1)}, s32[]{:S(2)}) async-start(s8[8388608]{0:T(1024)(128)(4,1)} %bitcast.47), calls=%async_computation.7 | async-start | bytes 8388608
  318.4 6.2 %slice-start.5 = ((s8[8388608]{0:T(1024)(128)(4,1)}), s8[4194304]{0:T(1024)(128)(4,1)S(1)}, s32[]{:S(2)}) async-start(s8[8388608]{0:T(1024)(128)(4,1)} %bitcast.47), calls=%async_computation.8 | async-start | bytes 8388608
  548.8 5.2 copy-start.3
  548.8 7.3 %slice-start.2 = ((s8[8388608]{0:T(1024)(128)(4,1)}), s8[4194304]{0:T(1024)(128)(4,1)S(1)}, s32[]{:S(2)}) async-start(s8[8388608]{0:T(1024)(128)(4,1)} %bitcast.45), calls=%async_computation.5 | async-start | bytes 8388608
  554.0 4.0 slice-start.3
  558.0 5.2 copy-start.2
  563.2 3.7 copy-start.1
  563.2 5.8 %slice-start = ((s8[8388608]{0:T(1024)(128)(4,1)}), s8[4194304]{0:T(1024)(128)(4,1)S(1)}, s32[]{:S(2)}) async-start(s8[8388608]{0:T(1024)(128)(4,1)} %bitcast.43), calls=%async_computation.3 | async-start | bytes 8388608
  566.9 4.2 slice-start.1

commit v4 on v3

--- a/solution.py
+++ b/solution.py
@@ -23,14 +23,69 @@
     return jnp.concatenate([cos, cos], axis=-1), jnp.concatenate([-sin, sin], axis=-1)
 
 
-def qkv_kernel(x_ref, g_ref, wq_ref, wk_ref, wv_ref, gq_ref, gk_ref, cos_ref, sin_ref, h_ref, raw_ref, rot_ref):
+def block_of(i):
+    chip = lax.axis_index('sp') // 2
+    return 2 * ((chip // 2 + i // 2) % 2) + (chip % 2 + i % 2) % 2
+
+
+def qkv_kernel(n_dev, hid, dyl, g_ref, wq_ref, wk_ref, wv_ref, gq_ref, gk_ref, cos_ref, sin_ref, x_ref, h_ref, raw_ref, rot_ref, dy_hbm, xbuf, send, recv, dsend, drecv, lsem):
     n_src, rows, tok, dim = x_ref.shape
     n = n_src * rows * tok
+    i = pl.program_id(0)
+    me = lax.axis_index('sp')
+    c = me % 2
+
+    def piece(rel, si):
+        core = (c + si) % 2
+        to = block_of(rel) * 2 + core
+        return pltpu.make_async_remote_copy(src_ref=hid.at[pl.ds(pl.multiple_of(to * rows, rows), rows)], dst_ref=xbuf.at[me],
+                                            send_sem=send.at[rel, si], recv_sem=recv.at[rel, si], device_id=(to,), device_id_type=MESH)
+
+    def dy_piece(si):
+        to = block_of(3) * 2 + (c + si) % 2
+        return pltpu.make_async_remote_copy(src_ref=dyl.at[pl.ds(pl.multiple_of(to * rows, rows), rows)], dst_ref=dy_hbm.at[me],
+                                            send_sem=dsend.at[si], recv_sem=drecv.at[si], device_id=(to,), device_id_type=MESH)
+
+    own = pltpu.make_async_copy(hid.at[pl.ds(pl.multiple_of(me * rows, rows), rows)], xbuf.at[me], lsem.at[0])
+    n_rel = n_dev // 2
+
+    @pl.when(i == 0)
+    def _():
+        own.start()
+        sem = pltpu.get_barrier_semaphore()
+        for d in range(1, n_dev):
+            pl.semaphore_signal(sem, inc=1, device_id=((me + d) % n_dev,), device_id_type=MESH)
+        pl.semaphore_wait(sem, n_dev - 1)
+        for rel in range(n_rel):
+            for si in range(2):
+                if rel or si:
+                    piece(rel, si).start()
+        for si in range(2):
+            dy_piece(si).start()
+        own.wait()
+
+    for rel in range(n_rel):
+        @pl.when(i == rel)
+        def _():
+            for si in range(2):
+                if rel or si:
+                    piece(rel, si).wait_recv()
+
+    @pl.when(i == n_rel - 1)
+    def _():
+        for rel in range(n_rel):
+            for si in range(2):
+                if rel or si:
+                    piece(rel, si).wait_send()
+
+    blk = block_of(i)
+    x_ref[...] = xbuf[pl.ds(pl.multiple_of(blk * n_src, n_src), n_src)]
     x = x_ref[...].reshape(n, dim).astype(F32)
     r = lax.rsqrt(jnp.mean(x * x, axis=-1, keepdims=True) + NORM_EPS)
     h_ref[...] = (x * r * g_ref[...]).astype(BF16).reshape(h_ref.shape)
-    cos = cos_ref[...].reshape(n_src, 1, tok, HD)
-    sin = sin_ref[...].reshape(n_src, 1, tok, HD)
+    at = pl.ds(pl.multiple_of(blk * n_src * tok, n_src * tok), n_src * tok)
+    cos = cos_ref[at, :].reshape(n_src, 1, tok, HD)
+    sin = sin_ref[at, :].reshape(n_src, 1, tok, HD)
 
     def post(raw, gain):
         v = raw.astype(F32)
@@ -59,13 +114,19 @@
 
     lax.fori_loop(0, wk_ref.shape[1] // (2 * HD), body, 0, unroll=2)
 
-
-QB = 256
+    @pl.when(i == n_rel - 1)
+    def _():
+        for si in range(2):
+            dy_piece(si).wait()
+
+
+QB_FWD, QB_BWD, KV_STEP = 512, 256, 2
 NT = (((1,), (1,)), ((), ()))
 EXP_SCALE = HD ** -0.5 * math.log2(math.e)
 
 
 def softmax_t(k, q, qb):
+    QB = q.shape[0]
     lo = qb * QB
     parts = [(lo, lax.dot_general(k[lo:lo + QB], q, NT, preferred_element_type=F32))]
     keys = lax.broadcasted_iota(jnp.int32, (QB, QB), 0)
@@ -79,18 +140,90 @@
     return [(at, e * inv) for at, e in exps]
 
 
-def attn_fwd_kernel(rot_ref, o_ref):
-    n_pos = rot_ref.shape[0] * rot_ref.shape[2]
+def attn_fwd_kernel(n_dev, rot_ref, x_ref, wo_ref, dyl, dy_part, o_ref, y_hbm, dy_hbm, o_all, yb, send, recv, lsem, dyb, dsend, drecv, dloc):
+    n_src, _, tok, dim = x_ref.shape
+    n_pos = n_src * tok
+    r, j = pl.program_id(0), pl.program_id(1)
+    n_rows, n_kv = dyl.shape[0] // n_dev, pl.num_programs(1)
+    me = lax.axis_index('sp')
+
+    c = me % 2
+
+    def mine(dev):
+        return dyl.at[pl.ds(pl.multiple_of(dev * n_rows, n_rows), n_rows)]
+
+    def dy_piece(rel, si):
+        to = block_of(rel) * 2 + (c + si) % 2
+        return pltpu.make_async_remote_copy(src_ref=mine(to), dst_ref=dy_hbm.at[me], send_sem=dsend.at[rel, si], recv_sem=drecv.at[rel, si],
+                                            device_id=(to,), device_id_type=MESH)
+
+    dy_rest = ((0, 1), (1, 0), (2, 0), (1, 1), (2, 1))
+    keep_in = pltpu.make_async_copy(mine(me), dyb, dloc.at[0])
+    keep_out = pltpu.make_async_copy(dyb, dy_hbm.at[me], dloc.at[1])
+
+    @pl.when(jnp.logical_and(r == 0, j == 0))
+    def _():
+        sem = pltpu.get_barrier_semaphore()
+        for d in range(1, n_dev):
+            pl.semaphore_signal(sem, inc=1, device_id=((me + d) % n_dev,), device_id_type=MESH)
+        pl.semaphore_wait(sem, n_dev - 1)
+        keep_in.start()
+        for rel, si in dy_rest:
+            dy_piece(rel, si).start()
+
+    @pl.when(jnp.logical_and(r == 0, j == 1))
+    def _():
+        keep_in.wait()
+        keep_out.start()
+
     rot = rot_ref[...].reshape(n_pos, 4 * HD)
     k, v_t = rot[:, 2 * HD:3 * HD], rot[:, 3 * HD:].T
-    src_b = QB // rot_ref.shape[2]
-    for qb in range(n_pos // QB):
+    src_b = QB_FWD // tok
+    for qb in range(n_pos // QB_FWD):
         for head in range(2):
-            q = rot[qb * QB:(qb + 1) * QB, head * HD:(head + 1) * HD]
+            q = rot[qb * QB_FWD:(qb + 1) * QB_FWD, head * HD:(head + 1) * HD]
             o_t = functools.reduce(jnp.add, [
                 jnp.dot(v_t[:, at:at + p.shape[0]], p.astype(BF16), preferred_element_type=F32)
                 for at, p in softmax_t(k, q, qb)])
-            o_ref[pl.ds(qb * src_b, src_b), 0, :, pl.ds(head * HD, HD)] = o_t.T.astype(BF16).reshape(src_b, o_ref.shape[2], HD)
+            o = o_t.T.astype(BF16)
+            o_ref[pl.ds(qb * src_b, src_b), 0, :, pl.ds(head * HD, HD)] = o.reshape(src_b, tok, HD)
+    o_all[j] = o_ref[...].reshape(n_pos, 2 * HD)
+
+    def to_home(row, d):
+        to = (me + d) % n_dev
+        dst = y_hbm.at[me * n_rows + row]
+        if d == 0:
+            return pltpu.make_async_copy(yb.at[row, me], dst, lsem.at[row])
+        return pltpu.make_async_remote_copy(src_ref=yb.at[row, to], dst_ref=dst, send_sem=send.at[row, d], recv_sem=recv.at[row, d],
+                                            device_id=(to,), device_id_type=MESH)
+
+    @pl.when(j == n_kv - 1)
+    def _():
+        width = 256
+
+        def cols(t, _):
+            at = pl.ds(pl.multiple_of(t * width, width), width)
+            y = functools.reduce(jnp.add, [
+                jnp.dot(o_all[kv], wo_ref[pl.ds(kv * 2 * HD, 2 * HD), at], preferred_element_type=F32) for kv in range(o_all.shape[0])])
+            y = x_ref[:, 0, :, at].reshape(n_pos, width).astype(F32) + y
+            yb[r, :, :, at] = y.astype(BF16).reshape(n_src, tok, width)
+            return 0
+
+        lax.fori_loop(0, dim // width, cols, 0)
+        for d in range(n_dev):
+            to_home(r, d).start()
+
+    @pl.when(jnp.logical_and(r == n_rows - 1, j == n_kv - 1))
+    def _():
+        def finish_row(row, _):
+            for d in range(n_dev):
+                to_home(row, d).wait()
+            return 0
+
+        lax.fori_loop(0, n_rows, finish_row, 0)
+        keep_out.wait()
+        for rel, si in dy_rest:
+            dy_piece(rel, si).wait()
 
 
 MESH = pl.DeviceIdType.MESH
@@ -211,8 +344,8 @@
     return Reducer(chunks, *(refs[i * nc:(i + 1) * nc] for i in range(4)), *refs[4 * nc:4 * nc + 3])
 
 
-BWD_STAGES = {0: ((0, 1), (1, 1)), 3: ((0, 2), (1, 2)), 8: ((0, 3),), 12: ((1, 3),), 14: ((0, 4),), 16: ((1, 4),),
-              20: ((0, 5),), 24: ((1, 5),), 27: ((0, 6),), 29: ((1, 6),)}
+BWD_STAGES = {0: ((0, 1), (1, 1)), 1: ((0, 2), (1, 2)), 4: ((0, 3),), 6: ((1, 3), (0, 4)), 8: ((1, 4),),
+              10: ((0, 5),), 12: ((1, 5), (0, 6)), 14: ((1, 6),)}
 
 
 def attn_bwd_kernel(n_dev, rot_ref, raw_ref, do_ref, gq_ref, gk_ref, cos_ref, sin_ref, wo_part, oq_ref, ok_ref, ov_ref, dgq_ref, dgk_ref, wo_sum,
@@ -230,12 +363,7 @@
 
     n_src, _, tok, _ = rot_ref.shape
     n_pos = n_src * tok
-    rot = rot_ref[...].reshape(n_pos, 4 * HD)
-    raw = raw_ref[...].reshape(n_pos, 3 * HD)
-    d_o = do_ref[...].reshape(n_pos, 2 * HD)
-    k, v = rot[:, 2 * HD:3 * HD], rot[:, 3 * HD:]
-    k_t = k.astype(F32).T.astype(BF16)
-    src_b = QB // tok
+    src_b = QB_BWD // tok
     first = jnp.logical_and(pl.program_id(0) == 0, pl.program_id(1) == 0)
 
     @pl.when(first)
@@ -256,34 +384,40 @@
         dng = dn * gain
         return (r * (dng - xh * jnp.mean(dng * xh, axis=-1, keepdims=True))).astype(BF16)
 
-    for qb in reversed(range(n_pos // QB)):
-        last = qb == n_pos // QB - 1
-        sl = slice(qb * QB, (qb + 1) * QB)
-        for head in range(2):
-            hs = slice(head * HD, (head + 1) * HD)
-            q, dob = rot[sl, hs], d_o[sl, hs]
-            ps = softmax_t(k, q, qb)
-            dps = [lax.dot_general(v[at:at + p.shape[0]], dob, NT, preferred_element_type=F32) for at, p in ps]
-            delta = functools.reduce(jnp.add, [jnp.sum(p * dp, axis=0, keepdims=True) for (_, p), dp in zip(ps, dps)])
-            dq_t = None
-            for (at, p), dp in zip(ps, dps):
-                ds = (p * (dp - delta) * HD ** -0.5).astype(BF16)
-                dq_p = jnp.dot(k_t[:, at:at + p.shape[0]], ds, preferred_element_type=F32)
-                dq_t = dq_p if dq_t is None else dq_t + dq_p
-                dv = jnp.dot(p.astype(BF16), dob, preferred_element_type=F32)
-                dk = jnp.dot(ds, q, preferred_element_type=F32)
-                rows = pl.ds(at, dk.shape[0])
-                if last and head == 0:
-                    dk_acc[rows, :] = dk
-                    dv_acc[rows, :] = dv
-                else:
-                    dk_acc[rows, :] += dk
-                    dv_acc[rows, :] += dv
-            dq_raw = post_back(dq_t.T, raw[sl, hs], gq_ref[...], qb * QB, dgq_ref)
-            oq_ref[pl.ds(qb * src_b, src_b), 0, :, pl.ds(head * HD, HD)] = dq_raw.reshape(src_b, tok, HD)
-    dk_raw = post_back(dk_acc[...], raw[:, 2 * HD:], gk_ref[...], 0, dgk_ref)
-    ok_ref[:, 0] = dk_raw.reshape(n_src, tok, HD)
-    ov_ref[:, 0] = dv_acc[...].astype(BF16).reshape(n_src, tok, HD)
+    for kv in range(KV_STEP):
+        rot = rot_ref[:, 0, :, pl.ds(kv * 4 * HD, 4 * HD)].reshape(n_pos, 4 * HD)
+        raw = raw_ref[:, 0, :, pl.ds(kv * 3 * HD, 3 * HD)].reshape(n_pos, 3 * HD)
+        d_o = do_ref[:, 0, :, pl.ds(kv * 2 * HD, 2 * HD)].reshape(n_pos, 2 * HD)
+        k, v = rot[:, 2 * HD:3 * HD], rot[:, 3 * HD:]
+        k_t = k.astype(F32).T.astype(BF16)
+        for qb in reversed(range(n_pos // QB_BWD)):
+            last = qb == n_pos // QB_BWD - 1
+            sl = slice(qb * QB_BWD, (qb + 1) * QB_BWD)
+            for head in range(2):
+                hs = slice(head * HD, (head + 1) * HD)
+                q, dob = rot[sl, hs], d_o[sl, hs]
+                ps = softmax_t(k, q, qb)
+                dps = [lax.dot_general(v[at:at + p.shape[0]], dob, NT, preferred_element_type=F32) for at, p in ps]
+                delta = functools.reduce(jnp.add, [jnp.sum(p * dp, axis=0, keepdims=True) for (_, p), dp in zip(ps, dps)])
+                dq_t = None
+                for (at, p), dp in zip(ps, dps):
+                    ds = (p * (dp - delta) * HD ** -0.5).astype(BF16)
+                    dq_p = jnp.dot(k_t[:, at:at + p.shape[0]], ds, preferred_element_type=F32)
+                    dq_t = dq_p if dq_t is None else dq_t + dq_p
+                    dv = jnp.dot(p.astype(BF16), dob, preferred_element_type=F32)
+                    dk = jnp.dot(ds, q, preferred_element_type=F32)
+                    rows = pl.ds(at, dk.shape[0])
+                    if last and head == 0:
+                        dk_acc[kv, rows, :] = dk
+                        dv_acc[kv, rows, :] = dv
+                    else:
+                        dk_acc[kv, rows, :] += dk
+                        dv_acc[kv, rows, :] += dv
+                dq_raw = post_back(dq_t.T, raw[sl, hs], gq_ref[...], qb * QB_BWD, dgq_ref)
+                oq_ref[pl.ds(qb * src_b, src_b), 0, :, pl.ds((2 * kv + head) * HD, HD)] = dq_raw.reshape(src_b, tok, HD)
+        dk_raw = post_back(dk_acc[kv], raw[:, 2 * HD:], gk_ref[...], 0, dgk_ref)
+        ok_ref[:, 0, :, pl.ds(kv * HD, HD)] = dk_raw.reshape(n_src, tok, HD)
+        ov_ref[:, 0, :, pl.ds(kv * HD, HD)] = dv_acc[kv].astype(BF16).reshape(n_src, tok, HD)
 
     @pl.when(step == pl.num_programs(0) * pl.num_programs(1) - 1)
     def _():
@@ -331,6 +465,7 @@
             return 0
 
         lax.fori_loop(0, dim // 256, col, 0)
+        per = rows * tok
 
         def tail_rows(j, _):
             part = pl.ds(pl.multiple_of(j * tok, tok), tok)
@@ -346,6 +481,8 @@
             return 0
 
         lax.fori_loop(0, sb * rows, tail_rows, 0)
+
+    def dx_send(b):
         home = odx.at[pl.ds(pl.multiple_of(me * rows, rows), rows)]
         for si in range(sb):
             core = (c + si) % 2
@@ -373,30 +510,34 @@
     for cp in loads:
         cp.wait()
     dx_block(0, fetched[0])
+    dx_send(0)
     fetched[2] = fetch(2)
     red.stage(0, 3)
+    dx_block(1, fetched[1])
+    dx_send(1)
+    fetched[3] = fetch(3)
     red.stage(1, 3)
-    dx_block(1, fetched[1])
-    fetched[3] = fetch(3)
     red.stage(0, 4)
+    dx_block(2, fetched[2])
     red.stage(2, 3)
     red.stage(1, 4)
-    red.stage(3, 3)
-    dx_block(2, fetched[2])
-    red.stage(0, 5)
-    red.stage(2, 4)
-    red.stage(1, 5)
-    red.stage(3, 4)
     dx_block(3, fetched[3])
+    dx_send(3)
     gcopies = []
     for d in range(1, n_dev):
         cp = pltpu.make_async_remote_copy(src_ref=gpack, dst_ref=gbuf.at[d - 1], send_sem=gsend.at[d], recv_sem=grecv.at[d],
                                           device_id=((me + d) % n_dev,), device_id_type=MESH)
         cp.start()
         gcopies.append(cp)
+    red.stage(3, 3)
+    red.stage(2, 4)
+    red.stage(0, 5)
+    red.stage(1, 5)
+    red.stage(3, 4)
+    dx_send(2)
     red.stage(0, 6)
+    red.stage(1, 6)
     red.stage(2, 5)
-    red.stage(1, 6)
     red.stage(3, 5)
     red.stage(2, 6)
     red.stage(3, 6)
@@ -455,44 +596,45 @@
         cos_t, sin_t = rope_tables(n_pos)
         g2 = norm_gain.reshape(1, dim)
         gq2, gk2 = q_gain.reshape(1, HD), k_gain.reshape(1, HD)
-        x = lax.all_to_all(hidden, 'sp', 0, 0, tiled=True).reshape(n_dev, rows, tok, dim)
-        dy = lax.all_to_all(d_out, 'sp', 0, 0, tiled=True).reshape(n_dev, rows, tok, dim)
-
         sb = 2
         full = lambda *s: pl.BlockSpec(s, lambda *i: (0,) * len(s))
         tokspec = lambda c: pl.BlockSpec((sb, rows, tok, c), lambda i: (i, 0, 0, 0))
         shp = lambda c, d=BF16: jax.ShapeDtypeStruct((n_dev, rows, tok, c), d)
-        h, raw, rot = pl.pallas_call(
-            qkv_kernel, grid=(n_dev // sb,),
-            in_specs=[tokspec(dim), full(1, dim), full(*w_q.shape), full(*w_k.shape), full(*w_v.shape), full(1, HD), full(1, HD),
-                      pl.BlockSpec((sb * tok, HD), lambda i: (i, 0)), pl.BlockSpec((sb * tok, HD), lambda i: (i, 0))],
-            out_specs=[tokspec(dim), tokspec(n_kv * 3 * HD), tokspec(n_kv * 4 * HD)],
-            out_shape=[shp(dim), shp(n_kv * 3 * HD), shp(n_kv * 4 * HD)],
-            compiler_params=params(), cost_estimate=cost(2 * n_tok * dim * 4 * HD * n_kv, 40e6), name='qkv',
-        )(x, g2, w_q, w_k, w_v, gq2, gk2, cos_t, sin_t)
+        outspec = lambda c: pl.BlockSpec((sb, rows, tok, c), lambda i: (block_of(i), 0, 0, 0))
+        hbm = pl.BlockSpec(memory_space=pl.ANY)
+        dma = pltpu.SemaphoreType.DMA
+        x, h, raw, rot, dy = pl.pallas_call(
+            functools.partial(qkv_kernel, n_dev), grid=(n_dev // sb,),
+            in_specs=[hbm, hbm, full(1, dim), full(*w_q.shape), full(*w_k.shape), full(*w_v.shape), full(1, HD), full(1, HD), full(n_pos, HD), full(n_pos, HD)],
+            out_specs=[outspec(dim), outspec(dim), outspec(n_kv * 3 * HD), outspec(n_kv * 4 * HD), hbm],
+            out_shape=[shp(dim), shp(dim), shp(n_kv * 3 * HD), shp(n_kv * 4 * HD), shp(dim)],
+            scratch_shapes=[pltpu.VMEM((n_dev, rows, tok, dim), BF16), dma((n_dev // 2, 2)), dma((n_dev // 2, 2)), dma((2,)), dma((2,)), dma((1,))],
+            compiler_params=params(collective_id=2, has_side_effects=True), cost_estimate=cost(2 * n_tok * dim * 4 * HD * n_kv, 40e6), name='qkv',
+        )(hidden, d_out, g2, w_q, w_k, w_v, gq2, gk2, cos_t, sin_t)
 
         head_spec = lambda c: pl.BlockSpec((n_dev, 1, tok, c), lambda r, j: (0, r, 0, j))
-        o = pl.pallas_call(
-            attn_fwd_kernel, grid=(rows, n_kv), in_specs=[head_spec(4 * HD)], out_specs=head_spec(2 * HD),
-            out_shape=shp(qw), compiler_params=params(), cost_estimate=cost(4 * n_tok * n_pos * qw, 24e6), name='attn_fwd',
-        )(rot)
-        o2, dy2, x2 = o.reshape(n_tok, qw), dy.reshape(n_tok, dim), x.reshape(n_tok, dim)
-        y = (x2.astype(F32) + jnp.dot(o2, w_o, preferred_element_type=F32)).astype(BF16)
+        o, y_out, dy = pl.pallas_call(
+            functools.partial(attn_fwd_kernel, n_dev), grid=(rows, n_kv),
+            in_specs=[head_spec(4 * HD), pl.BlockSpec((n_dev, 1, tok, dim), lambda r, j: (0, r, 0, 0)), full(*w_o.shape), hbm, hbm],
+            out_specs=[head_spec(2 * HD), hbm, hbm],
+            out_shape=[shp(qw), jax.ShapeDtypeStruct((n_batch, tok, dim), BF16), shp(dim)], input_output_aliases={4: 2},
+            scratch_shapes=[pltpu.VMEM((n_kv, n_pos, 2 * HD), BF16), pltpu.VMEM((rows, n_dev, tok, dim), BF16), dma((rows, n_dev)), dma((rows, n_dev)), dma((rows,)),
+                            pltpu.VMEM((rows, tok, dim), BF16), dma((3, 2)), dma((3, 2)), dma((2,))],
+            compiler_params=params(collective_id=3, has_side_effects=True), cost_estimate=cost(4 * n_tok * n_pos * qw, 24e6), name='attn_fwd',
+        )(rot, x, w_o, d_out, dy)
+        o2, dy2 = o.reshape(n_tok, qw), dy.reshape(n_tok, dim)
         d_wo = lax.dot_general(o2, dy2, (((0,), (0,)), ((), ())), preferred_element_type=F32)
         d_o = lax.dot_general(dy2, w_o, (((1,), (1,)), ((), ())), preferred_element_type=F32).astype(BF16).reshape(n_dev, rows, tok, qw)
-        y, d_wo, d_o = lax.optimization_barrier((y, d_wo, d_o))
         dq, dk, dv, dgq, dgk, d_wo = pl.pallas_call(
-            functools.partial(attn_bwd_kernel, n_dev), grid=(rows, n_kv),
-            in_specs=[head_spec(4 * HD), head_spec(3 * HD), head_spec(2 * HD), full(1, HD), full(1, HD), full(n_pos, HD), full(n_pos, HD),
+            functools.partial(attn_bwd_kernel, n_dev), grid=(rows, n_kv // KV_STEP),
+            in_specs=[head_spec(KV_STEP * 4 * HD), head_spec(KV_STEP * 3 * HD), head_spec(KV_STEP * 2 * HD), full(1, HD), full(1, HD), full(n_pos, HD), full(n_pos, HD),
                       pl.BlockSpec(memory_space=pl.ANY)],
-            out_specs=[head_spec(2 * HD), head_spec(HD), head_spec(HD), full(8, HD), full(8, HD), pl.BlockSpec(memory_space=pl.ANY)],
+            out_specs=[head_spec(KV_STEP * 2 * HD), head_spec(KV_STEP * HD), head_spec(KV_STEP * HD), full(8, HD), full(8, HD), pl.BlockSpec(memory_space=pl.ANY)],
             out_shape=[shp(qw), shp(n_kv * HD), shp(n_kv * HD), jax.ShapeDtypeStruct((8, HD), F32), jax.ShapeDtypeStruct((8, HD), F32),
                        jax.ShapeDtypeStruct(d_wo.shape, F32)],
-            scratch_shapes=[pltpu.VMEM((n_pos, HD), F32), pltpu.VMEM((n_pos, HD), F32)] + reduce_scratch([(qw // 2, dim)] * 2),
+            scratch_shapes=[pltpu.VMEM((KV_STEP, n_pos, HD), F32), pltpu.VMEM((KV_STEP, n_pos, HD), F32)] + reduce_scratch([(qw // 2, dim)] * 2),
             compiler_params=params(collective_id=1, has_side_effects=True), cost_estimate=cost(10 * n_tok * n_pos * qw, 60e6), name='attn_bwd',
         )(rot, raw, d_o, gq2, gk2, cos_t, sin_t, d_wo)
-        y, dq = lax.optimization_barrier((y, dq))
-        y_out = lax.all_to_all(y.reshape(n_batch, tok, dim), 'sp', 0, 0, tiled=True)
         h2 = h.reshape(n_tok, dim)
         d_wq, d_wk, d_wv = (lax.dot_general(h2, d.reshape(n_tok, -1), (((0,), (0,)), ((), ())), preferred_element_type=F32) for d in (dq, dk, dv))
         d_wq, d_wk, d_wv, d_hidden, gains = finish(n_dev, (d_wq, d_wk, d_wv), (dq, dk, dv), (w_q, w_k, w_v), x, dy, g2, dgq, dgk)

time: 583 us -> 542 us (0.930)
  blocking collectives: 53.4 us -> 0 us
  Pallas kernels: 417 us -> 447 us
  matrix products: 66.6 us -> 54.8 us
  starting transfers between devices: 6.84 us -> 0 us
    all_to_all x1 -> x0, blocking collectives: 53.4 us -> none  [local_step(): lax.all_to_all(hidden, 'sp', 0, 0, tiled=True)]
    pallas_call x2, Pallas kernels: 111 us -> 155 us  [the longest x1 79.9 us: local_step(): pl.pallas_call(functools.partial(qkv_kernel, n_dev), grid=(n_dev // sb,),...]
    pallas_call x1, Pallas kernels: 210 us -> 198 us  [finish(): pl.pallas_call(functools.partial(tail_kernel, n_dev), in_specs=[hbm] * 11...]
    dot_general x1 -> x0, matrix products: 10.7 us -> none  [local_step(): jnp.dot(o2, w_o, preferred_element_type=F32)]
    all_to_all x2 -> x0, starting transfers between devices: 6.84 us -> none  [the longest x1 3.55 us: local_step(): y_out = lax.all_to_all(y.reshape(n_batch, tok, dim), 'sp', 0, 0, tiled=True)]
    unnamed x34 -> x32, local copies, waits for them, and re-layouts: 25.7 us -> 25.7 us
  transfers between devices with their start and end apart: 2 -> 0, of which waited for: 0 -> 0; matrix products, arithmetic and copies ran while one was open for 6% -> 0% of each run, Pallas kernels for 56% -> 0%
where the time goes in v4:
time: 542 us; the launch traced here: 533 us
  Pallas kernels  447 us (82%)
  matrix products  54.8 us (10%)
  local copies, waits for them, and re-layouts  28.2 us (5%)
    pallas_call x1, Pallas kernels, finish(): pl.pallas_call(functools.partial(tail_kernel, n_dev), in_specs=[hbm] * 11...  198 us
    pallas_call x1, Pallas kernels, local_step(): pl.pallas_call(functools.partial(attn_bwd_kernel, n_dev), grid=(rows, n_k...  94 us
    pallas_call x1, Pallas kernels, local_step(): pl.pallas_call(functools.partial(qkv_kernel, n_dev), grid=(n_dev // sb,),...  79.9 us
    pallas_call x1, Pallas kernels, local_step(): pl.pallas_call(functools.partial(attn_fwd_kernel, n_dev), grid=(rows, n_k...  75 us
    dot_general x3, matrix products, local_step(): lax.dot_general(h2, d.reshape(n_tok, -1), (((0,), (0,)), ((), ())), prefe...  28 us
    unnamed x32, local copies, waits for them, and re-layouts  25.7 us
    dot_general x1, matrix products, local_step(): lax.dot_general(o2, dy2, (((0,), (0,)), ((), ())), preferred_element_type...  15.7 us
    dot_general x1, matrix products, local_step(): lax.dot_general(dy2, w_o, (((1,), (1,)), ((), ())), preferred_element_typ...  11.1 us

profile of v4, /device:TPU:0, one launch (start us, length us, event | category | flops | bytes accessed | tf_op | source)
XLA Modules:
  0.0 533.2 jit_solution(966966382344558626)
XLA Ops:
  0.7 1.0 fusion
  1.7 1.0 pad_maximum_fusion
  2.7 79.9 %qkv.1 = (bf16[8,4,64,1024]{3,2,1,0:T(8,128)(2,1)}, bf16[8,4,64,1024]{3,2,1,0:T(8,128)(2,1)}, bf16[8,4,64,3072]{3,2,1,0:T(8,128)(2,1)}, bf16[8,4,64,4096]{3,2,1,0:T(8,128)(2,1)}, bf16[8,4,64,1024]{3,2,1,0:T(8,128)(2,1)}) custom-call(bf16[32,64,1024]{2,1,0:T(8,128)(2,1)} %hid.1, bf16[32,64,1024]{2,1,0:T(8,128)(2,1)} %dyl.3, f32[1,1024]{1,0:T(1,128)} %bitcast.43, ...), custom_call_target="tpu_custom_call" | custom-call | flops 17179869184 | bytes 40000000 | tf_op jit(solution)/shard_map/qkv/pallas_call | solution.py:606
  82.6 75.0 %attn_fwd.1 = (bf16[8,4,64,2048]{3,2,1,0:T(8,128)(2,1)}, bf16[32,64,1024]{2,1,0:T(8,128)(2,1)}, bf16[8,4,64,1024]{3,2,1,0:T(8,128)(2,1)}) custom-call(bf16[8,4,64,4096]{3,2,1,0:T(8,128)(2,1)} %get-tuple-element.28.rot_ref, bf16[8,4,64,1024]{3,2,1,0:T(8,128)(2,1)} %get-tuple-element.29.x_ref.refs_9_, ...), custom_call_target="tpu_custom_call", output_to_operand_aliasing={{2}: (4, {})} | custom-call | flops 8589934592 | bytes 24000000 | tf_op jit(solution)/shard_map/attn_fwd/pallas_call | solution.py:616
  157.6 0.0 copy-start.4
  157.6 15.7 %convolution_bitcast_fusion.1.wo_part = f32[2048,1024]{1,0:T(8,128)} fusion(bf16[8,4,64,2048]{3,2,1,0:T(8,128)(2,1)} %get-tuple-element.35, bf16[8,4,64,1024]{3,2,1,0:T(8,128)(2,1)} %get-tuple-element.34.refs_10_), kind=kOutput, calls=%fused_computation.2 | convolution fusion | flops 8589934592 | bytes 20971520 | tf_op jit(solution)/shard_map/dot_general | solution.py:626
  173.4 11.1 %convolution_convert_fusion = bf16[2048,2048]{1,0:T(8,128)(2,1)} fusion(bf16[2048,1024]{1,0:T(8,128)(2,1)S(1)} %bitcast.36, bf16[2048,1024]{1,0:T(8,128)(2,1)S(1)} %copy-done.4), kind=kOutput, calls=%fused_computation | convolution fusion | flops 8594128896 | bytes 16777216 | tf_op jit(solution)/shard_map/dot_general | solution.py:627
  184.4 94.0 %attn_bwd.1 = (bf16[8,4,64,2048]{3,2,1,0:T(8,128)(2,1)}, bf16[8,4,64,1024]{3,2,1,0:T(8,128)(2,1)}, bf16[8,4,64,1024]{3,2,1,0:T(8,128)(2,1)}, f32[8,128]{1,0:T(8,...) custom-call(bf16[8,4,64,4096]{3,2,1,0:T(8,128)(2,1)} %get-tuple-element.28.rot_ref, ...), custom_call_target="tpu_custom_call" | custom-call | flops 21474836480 | bytes 60000000 | tf_op jit(solution)/shard_map/attn_bwd/pallas_call | solution.py:628
  278.5 10.2 %convolution_bitcast_fusion.3.refs_1_ = f32[1024,1024]{1,0:T(8,128)} fusion(bf16[8,4,64,1024]{3,2,1,0:T(8,128)(2,1)} %get-tuple-element.32, bf16[8,4,64,1024]{3,2,1,0:T(8,128)(2,1)} %get-tuple-element.37.refs_4_), kind=kOutput, calls=%fused_computation.4 | convolution fusion | flops 4294967296 | bytes 12582912 | tf_op jit(solution)/shard_map/dot_general | solution.py:639
  288.7 6.3 %convolution_bitcast_fusion.2.refs_2_ = f32[1024,1024]{1,0:T(8,128)} fusion(bf16[8,4,64,1024]{3,2,1,0:T(8,128)(2,1)S(1)} %copy-done.6, bf16[8,4,64,1024]{3,2,1,0:T(8,128)(2,1)S(1)} %copy-done.5), kind=kOutput, calls=%fused_computation.3 | convolution fusion | flops 4294967296 | bytes 12582912 | tf_op jit(solution)/shard_map/dot_general | solution.py:639
  295.0 11.5 %convolution_bitcast_fusion.refs_0_ = f32[1024,2048]{1,0:T(8,128)} fusion(bf16[8,4,64,1024]{3,2,1,0:T(8,128)(2,1)S(1)} %copy-done.6, bf16[8,4,64,2048]{3,2,1,0:T(8,128)(2,1)S(1)} %bitcast.42), kind=kOutput, calls=%fused_computation.1 | convolution fusion | flops 8589934592 | bytes 20971520 | tf_op jit(solution)/shard_map/dot_general | solution.py:639
  306.5 198.1 %tail.1 = (f32[1024,2048]{1,0:T(8,128)}, f32[1024,1024]{1,0:T(8,128)}, f32[1024,1024]{1,0:T(8,128)}, bf16[32,64,1024]{2,1,0:T(8,128)(2,1)}, f32[1,1280]{1,0:T(1,128)}) custom-call(f32[1024,2048]{1,0:T(8,128)} %convolution_bitcast_fusion.refs_0_, f32[1024,1024]{1,0:T(8,128)} %convolution_bitcast_fusion.3.refs_1_, ...), custom_call_target="tpu_custom_call" | custom-call | tf_op jit(solution)/shard_map/tail/pallas_call | solution.py:568
  504.7 1.2 slice_bitcast_fusion
  505.9 1.3 slice.18
  507.2 5.2 copy.30
  512.4 2.1 copy.31
  514.5 1.8 slice-done.3
  516.3 4.3 copy.32
  520.6 1.0 copy-done.2
  521.6 2.1 copy.33
  523.7 1.6 copy-done.1
  525.3 2.1 copy.34
  527.4 2.1 slice-done.1
  529.5 3.4 copy.35
  (26 shorter events, 0.1 us)
Async XLA Ops:
  157.6 15.7 %copy-start = (bf16[8,4,64,1024]{3,2,1,0:T(8,128)(2,1)S(1)}, bf16[8,4,64,1024]{3,2,1,0:T(8,128)(2,1)}, u32[]{:S(2)}) copy-start(bf16[8,4,64,1024]{3,2,1,0:T(8,128)(2,1)} %get-tuple-element.34.refs_10_) | copy-start | bytes 12582916
  157.6 15.7 %copy-start.4 = (bf16[2048,1024]{1,0:T(8,128)(2,1)S(1)}, bf16[2048,1024]{1,0:T(8,128)(2,1)}, u32[]{:S(2)}) copy-start(bf16[2048,1024]{1,0:T(8,128)(2,1)} %wo_ref.1) | copy-start | bytes 12582916
  278.5 10.2 %copy-start.5 = (bf16[8,4,64,1024]{3,2,1,0:T(8,128)(2,1)S(1)}, bf16[8,4,64,1024]{3,2,1,0:T(8,128)(2,1)}, u32[]{:S(2)}) copy-start(bf16[8,4,64,1024]{3,2,1,0:T(8,128)(2,1)} %get-tuple-element.38.refs_5_) | copy-start | bytes 12582916
  278.5 10.2 %copy-start.6 = (bf16[8,4,64,1024]{3,2,1,0:T(8,128)(2,1)S(1)}, bf16[8,4,64,1024]{3,2,1,0:T(8,128)(2,1)}, u32[]{:S(2)}) copy-start(bf16[8,4,64,1024]{3,2,1,0:T(8,128)(2,1)} %get-tuple-element.32) | copy-start | bytes 12582916
  278.5 16.6 %slice-start.4 = ((s8[8388608]{0:T(1024)(128)(4,1)}), s8[4194304]{0:T(1024)(128)(4,1)S(1)}, s32[]{:S(2)}) async-start(s8[8388608]{0:T(1024)(128)(4,1)} %bitcast.41), calls=%async_computation.4 | async-start | bytes 8388608
  288.7 6.4 %slice-start.5 = ((s8[8388608]{0:T(1024)(128)(4,1)}), s8[4194304]{0:T(1024)(128)(4,1)S(1)}, s32[]{:S(2)}) async-start(s8[8388608]{0:T(1024)(128)(4,1)} %bitcast.41), calls=%async_computation.5 | async-start | bytes 8388608
  507.2 5.2 copy-start.3
  507.2 7.3 %slice-start.2 = ((s8[8388608]{0:T(1024)(128)(4,1)}), s8[4194304]{0:T(1024)(128)(4,1)S(1)}, s32[]{:S(2)}) async-start(s8[8388608]{0:T(1024)(128)(4,1)} %bitcast.39), calls=%async_computation.2 | async-start | bytes 8388608
  512.3 4.0 slice-start.3
  516.3 5.2 copy-start.2
  521.6 3.7 copy-start.1
  521.6 5.8 %slice-start = ((s8[8388608]{0:T(1024)(128)(4,1)}), s8[4194304]{0:T(1024)(128)(4,1)S(1)}, s32[]{:S(2)}) async-start(s8[8388608]{0:T(1024)(128)(4,1)} %bitcast.37), calls=%async_computation | async-start | bytes 8388608
  525.3 4.2 slice-start.1

commit v5 on v4

--- a/solution.py
+++ b/solution.py
@@ -12,6 +12,7 @@
 F32 = jnp.float32
 BF16 = jnp.bfloat16
 HD = 128
+H2, H3, H4 = 2 * HD, 3 * HD, 4 * HD
 VMEM_LIMIT = 60 * 1024 * 1024
 
 
@@ -103,16 +104,16 @@
             cols = pl.ds(pl.multiple_of(j * width, width), width)
             return jnp.dot(hh, w_ref[:, cols], preferred_element_type=F32).astype(BF16)
 
-        q, k, v = proj(wq_ref, 4 * HD), proj(wk_ref, 2 * HD), proj(wv_ref, 2 * HD)
+        q, k, v = proj(wq_ref, H4), proj(wk_ref, H2), proj(wv_ref, H2)
         for i in range(2):
             heads = [q[:, 2 * i * HD:(2 * i + 1) * HD], q[:, (2 * i + 1) * HD:(2 * i + 2) * HD], k[:, i * HD:(i + 1) * HD]]
             for part, (val, gain) in enumerate(zip(heads, (gq, gq, gk))):
-                raw_ref[:, :, :, pl.ds(pl.multiple_of((2 * j + i) * 3 * HD + part * HD, HD), HD)] = val.reshape(shape)
-                rot_ref[:, :, :, pl.ds(pl.multiple_of((2 * j + i) * 4 * HD + part * HD, HD), HD)] = post(val, gain)
-            rot_ref[:, :, :, pl.ds(pl.multiple_of((2 * j + i) * 4 * HD + 3 * HD, HD), HD)] = v[:, i * HD:(i + 1) * HD].reshape(shape)
+                raw_ref[:, :, :, pl.ds(pl.multiple_of((2 * j + i) * H3 + part * HD, HD), HD)] = val.reshape(shape)
+                rot_ref[:, :, :, pl.ds(pl.multiple_of((2 * j + i) * H4 + part * HD, HD), HD)] = post(val, gain)
+            rot_ref[:, :, :, pl.ds(pl.multiple_of((2 * j + i) * H4 + H3, HD), HD)] = v[:, i * HD:(i + 1) * HD].reshape(shape)
         return 0
 
-    lax.fori_loop(0, wk_ref.shape[1] // (2 * HD), body, 0, unroll=2)
+    lax.fori_loop(0, wk_ref.shape[1] // (H2), body, 0, unroll=2)
 
     @pl.when(i == n_rel - 1)
     def _():
@@ -122,6 +123,7 @@
 
 QB_FWD, QB_BWD, KV_STEP = 512, 256, 2
 NT = (((1,), (1,)), ((), ()))
+TN = (((0,), (0,)), ((), ()))
 EXP_SCALE = HD ** -0.5 * math.log2(math.e)
 
 
@@ -176,8 +178,8 @@
         keep_in.wait()
         keep_out.start()
 
-    rot = rot_ref[...].reshape(n_pos, 4 * HD)
-    k, v_t = rot[:, 2 * HD:3 * HD], rot[:, 3 * HD:].T
+    rot = rot_ref[...].reshape(n_pos, H4)
+    k, v_t = rot[:, H2:H3], rot[:, H3:].T
     src_b = QB_FWD // tok
     for qb in range(n_pos // QB_FWD):
         for head in range(2):
@@ -187,7 +189,7 @@
                 for at, p in softmax_t(k, q, qb)])
             o = o_t.T.astype(BF16)
             o_ref[pl.ds(qb * src_b, src_b), 0, :, pl.ds(head * HD, HD)] = o.reshape(src_b, tok, HD)
-    o_all[j] = o_ref[...].reshape(n_pos, 2 * HD)
+    o_all[j] = o_ref[...].reshape(n_pos, H2)
 
     def to_home(row, d):
         to = (me + d) % n_dev
@@ -204,7 +206,7 @@
         def cols(t, _):
             at = pl.ds(pl.multiple_of(t * width, width), width)
             y = functools.reduce(jnp.add, [
-                jnp.dot(o_all[kv], wo_ref[pl.ds(kv * 2 * HD, 2 * HD), at], preferred_element_type=F32) for kv in range(o_all.shape[0])])
+                jnp.dot(o_all[kv], wo_ref[pl.ds(kv * H2, H2), at], preferred_element_type=F32) for kv in range(o_all.shape[0])])
             y = x_ref[:, 0, :, at].reshape(n_pos, width).astype(F32) + y
             yb[r, :, :, at] = y.astype(BF16).reshape(n_src, tok, width)
             return 0
@@ -344,8 +346,7 @@
     return Reducer(chunks, *(refs[i * nc:(i + 1) * nc] for i in range(4)), *refs[4 * nc:4 * nc + 3])
 
 
-BWD_STAGES = {0: ((0, 1), (1, 1)), 1: ((0, 2), (1, 2)), 4: ((0, 3),), 6: ((1, 3), (0, 4)), 8: ((1, 4),),
-              10: ((0, 5),), 12: ((1, 5), (0, 6)), 14: ((1, 6),)}
+BWD_STAGES = ((0, 1, 4, 6, 10, 12), (0, 1, 6, 8, 12, 14))
 
 
 def attn_bwd_kernel(n_dev, rot_ref, raw_ref, do_ref, gq_ref, gk_ref, cos_ref, sin_ref, wo_part, oq_ref, ok_ref, ov_ref, dgq_ref, dgk_ref, wo_sum,
@@ -353,13 +354,13 @@
     step = pl.program_id(0) * pl.num_programs(1) + pl.program_id(1)
     n_half = wo_part.shape[0] // 2
     red = reducer([(wo_part, wo_sum, 0, n_half), (wo_part, wo_sum, n_half, n_half)], refs)
-    for at, todo in BWD_STAGES.items():
-        @pl.when(step == at)
-        def _():
-            if at == 0:
-                red.barrier(n_dev)
-            for i, k in todo:
-                red.stage(i, k)
+    for i, steps in enumerate(BWD_STAGES):
+        for k, at in enumerate(steps):
+            @pl.when(step == at)
+            def _():
+                if i + k == 0:
+                    red.barrier(n_dev)
+                red.stage(i, k + 1)
 
     n_src, _, tok, _ = rot_ref.shape
     n_pos = n_src * tok
@@ -385,10 +386,10 @@
         return (r * (dng - xh * jnp.mean(dng * xh, axis=-1, keepdims=True))).astype(BF16)
 
     for kv in range(KV_STEP):
-        rot = rot_ref[:, 0, :, pl.ds(kv * 4 * HD, 4 * HD)].reshape(n_pos, 4 * HD)
-        raw = raw_ref[:, 0, :, pl.ds(kv * 3 * HD, 3 * HD)].reshape(n_pos, 3 * HD)
-        d_o = do_ref[:, 0, :, pl.ds(kv * 2 * HD, 2 * HD)].reshape(n_pos, 2 * HD)
-        k, v = rot[:, 2 * HD:3 * HD], rot[:, 3 * HD:]
+        rot = rot_ref[:, 0, :, pl.ds(kv * H4, H4)].reshape(n_pos, H4)
+        raw = raw_ref[:, 0, :, pl.ds(kv * H3, H3)].reshape(n_pos, H3)
+        d_o = do_ref[:, 0, :, pl.ds(kv * H2, H2)].reshape(n_pos, H2)
+        k, v = rot[:, H2:H3], rot[:, H3:]
         k_t = k.astype(F32).T.astype(BF16)
         for qb in reversed(range(n_pos // QB_BWD)):
             last = qb == n_pos // QB_BWD - 1
@@ -415,7 +416,7 @@
                         dv_acc[kv, rows, :] += dv
                 dq_raw = post_back(dq_t.T, raw[sl, hs], gq_ref[...], qb * QB_BWD, dgq_ref)
                 oq_ref[pl.ds(qb * src_b, src_b), 0, :, pl.ds((2 * kv + head) * HD, HD)] = dq_raw.reshape(src_b, tok, HD)
-        dk_raw = post_back(dk_acc[kv], raw[:, 2 * HD:], gk_ref[...], 0, dgk_ref)
+        dk_raw = post_back(dk_acc[kv], raw[:, H2:], gk_ref[...], 0, dgk_ref)
         ok_ref[:, 0, :, pl.ds(kv * HD, HD)] = dk_raw.reshape(n_src, tok, HD)
         ov_ref[:, 0, :, pl.ds(kv * HD, HD)] = dv_acc[kv].astype(BF16).reshape(n_src, tok, HD)
 
@@ -509,38 +510,32 @@
         red.stage(i, 2)
     for cp in loads:
         cp.wait()
-    dx_block(0, fetched[0])
-    dx_send(0)
-    fetched[2] = fetch(2)
-    red.stage(0, 3)
-    dx_block(1, fetched[1])
-    dx_send(1)
-    fetched[3] = fetch(3)
-    red.stage(1, 3)
-    red.stage(0, 4)
-    dx_block(2, fetched[2])
-    red.stage(2, 3)
-    red.stage(1, 4)
-    dx_block(3, fetched[3])
-    dx_send(3)
+    late = n_blk - 2
+    for b in range(n_blk):
+        dx_block(b, fetched[b])
+        if b != late:
+            dx_send(b)
+        if b + 2 < n_blk:
+            fetched[b + 2] = fetch(b + 2)
+        red.stage(b, 3)
+        if b:
+            red.stage(b - 1, 4)
     gcopies = []
     for d in range(1, n_dev):
         cp = pltpu.make_async_remote_copy(src_ref=gpack, dst_ref=gbuf.at[d - 1], send_sem=gsend.at[d], recv_sem=grecv.at[d],
                                           device_id=((me + d) % n_dev,), device_id_type=MESH)
         cp.start()
         gcopies.append(cp)
-    red.stage(3, 3)
-    red.stage(2, 4)
-    red.stage(0, 5)
-    red.stage(1, 5)
-    red.stage(3, 4)
-    dx_send(2)
-    red.stage(0, 6)
-    red.stage(1, 6)
-    red.stage(2, 5)
-    red.stage(3, 5)
-    red.stage(2, 6)
-    red.stage(3, 6)
+    first, last = range(nc // 2), range(nc // 2, nc)
+    for i in first:
+        red.stage(i, 5)
+    red.stage(nc - 1, 4)
+    dx_send(late)
+    for i in first:
+        red.stage(i, 6)
+    for k in (5, 6):
+        for i in last:
+            red.stage(i, k)
     for cp in gcopies:
         cp.wait()
     total = gpack[...] + functools.reduce(jnp.add, [gbuf[d] for d in range(n_dev - 1)])
@@ -563,22 +558,18 @@
     scratch += [pltpu.VMEM(w.shape, BF16) for w in weights]
     scratch += [pltpu.VMEM((2, sb, rows, tok, d.shape[-1]), BF16) for d in (*d_parts, x, dy)]
     scratch += [pltpu.VMEM((sb * rows * tok, dim), F32), pltpu.VMEM((nd // sb, sb, rows, tok, dim), BF16)]
-    scratch += [pltpu.VMEM((8, dim + 2 * HD), F32), pltpu.VMEM((n_dev - 1, 8, dim + 2 * HD), F32)]
+    scratch += [pltpu.VMEM((8, dim + H2), F32), pltpu.VMEM((n_dev - 1, 8, dim + H2), F32)]
     scratch += [dma((nd // sb, sb)), dma((nd // sb, sb)), dma((n_dev,)), dma((n_dev,)), dma((1,)), dma((3,)), dma((2, 5))]
     return pl.pallas_call(
         functools.partial(tail_kernel, n_dev), in_specs=[hbm] * 11 + [vmem] * 3, out_specs=[hbm] * 4 + [vmem],
         out_shape=[jax.ShapeDtypeStruct(a.shape, F32) for a in parts] + [
-            jax.ShapeDtypeStruct((nd * rows, tok, dim), BF16), jax.ShapeDtypeStruct((1, dim + 2 * HD), F32)],
+            jax.ShapeDtypeStruct((nd * rows, tok, dim), BF16), jax.ShapeDtypeStruct((1, dim + H2), F32)],
         scratch_shapes=scratch, compiler_params=params(collective_id=0, has_side_effects=True), name='tail',
     )(*parts, *d_parts, *weights, x, dy, g2, dgq, dgk)
 
 
 def params(**kw):
     return pltpu.CompilerParams(vmem_limit_bytes=VMEM_LIMIT, **kw)
-
-
-def cost(flops, nbytes):
-    return pl.CostEstimate(flops=int(flops), bytes_accessed=int(nbytes), transcendentals=0)
 
 
 def solution(mesh):
@@ -606,40 +597,40 @@
         x, h, raw, rot, dy = pl.pallas_call(
             functools.partial(qkv_kernel, n_dev), grid=(n_dev // sb,),
             in_specs=[hbm, hbm, full(1, dim), full(*w_q.shape), full(*w_k.shape), full(*w_v.shape), full(1, HD), full(1, HD), full(n_pos, HD), full(n_pos, HD)],
-            out_specs=[outspec(dim), outspec(dim), outspec(n_kv * 3 * HD), outspec(n_kv * 4 * HD), hbm],
-            out_shape=[shp(dim), shp(dim), shp(n_kv * 3 * HD), shp(n_kv * 4 * HD), shp(dim)],
+            out_specs=[outspec(dim), outspec(dim), outspec(n_kv * H3), outspec(n_kv * H4), hbm],
+            out_shape=[shp(dim), shp(dim), shp(n_kv * H3), shp(n_kv * H4), shp(dim)],
             scratch_shapes=[pltpu.VMEM((n_dev, rows, tok, dim), BF16), dma((n_dev // 2, 2)), dma((n_dev // 2, 2)), dma((2,)), dma((2,)), dma((1,))],
-            compiler_params=params(collective_id=2, has_side_effects=True), cost_estimate=cost(2 * n_tok * dim * 4 * HD * n_kv, 40e6), name='qkv',
+            compiler_params=params(collective_id=2, has_side_effects=True), name='qkv',
         )(hidden, d_out, g2, w_q, w_k, w_v, gq2, gk2, cos_t, sin_t)
 
         head_spec = lambda c: pl.BlockSpec((n_dev, 1, tok, c), lambda r, j: (0, r, 0, j))
         o, y_out, dy = pl.pallas_call(
             functools.partial(attn_fwd_kernel, n_dev), grid=(rows, n_kv),
-            in_specs=[head_spec(4 * HD), pl.BlockSpec((n_dev, 1, tok, dim), lambda r, j: (0, r, 0, 0)), full(*w_o.shape), hbm, hbm],
-            out_specs=[head_spec(2 * HD), hbm, hbm],
+            in_specs=[head_spec(H4), pl.BlockSpec((n_dev, 1, tok, dim), lambda r, j: (0, r, 0, 0)), full(*w_o.shape), hbm, hbm],
+            out_specs=[head_spec(H2), hbm, hbm],
             out_shape=[shp(qw), jax.ShapeDtypeStruct((n_batch, tok, dim), BF16), shp(dim)], input_output_aliases={4: 2},
-            scratch_shapes=[pltpu.VMEM((n_kv, n_pos, 2 * HD), BF16), pltpu.VMEM((rows, n_dev, tok, dim), BF16), dma((rows, n_dev)), dma((rows, n_dev)), dma((rows,)),
+            scratch_shapes=[pltpu.VMEM((n_kv, n_pos, H2), BF16), pltpu.VMEM((rows, n_dev, tok, dim), BF16), dma((rows, n_dev)), dma((rows, n_dev)), dma((rows,)),
                             pltpu.VMEM((rows, tok, dim), BF16), dma((3, 2)), dma((3, 2)), dma((2,))],
-            compiler_params=params(collective_id=3, has_side_effects=True), cost_estimate=cost(4 * n_tok * n_pos * qw, 24e6), name='attn_fwd',
+            compiler_params=params(collective_id=3, has_side_effects=True), name='attn_fwd',
         )(rot, x, w_o, d_out, dy)
         o2, dy2 = o.reshape(n_tok, qw), dy.reshape(n_tok, dim)
-        d_wo = lax.dot_general(o2, dy2, (((0,), (0,)), ((), ())), preferred_element_type=F32)
-        d_o = lax.dot_general(dy2, w_o, (((1,), (1,)), ((), ())), preferred_element_type=F32).astype(BF16).reshape(n_dev, rows, tok, qw)
+        d_wo = lax.dot_general(o2, dy2, TN, preferred_element_type=F32)
+        d_o = lax.dot_general(dy2, w_o, NT, preferred_element_type=F32).astype(BF16).reshape(n_dev, rows, tok, qw)
         dq, dk, dv, dgq, dgk, d_wo = pl.pallas_call(
             functools.partial(attn_bwd_kernel, n_dev), grid=(rows, n_kv // KV_STEP),
-            in_specs=[head_spec(KV_STEP * 4 * HD), head_spec(KV_STEP * 3 * HD), head_spec(KV_STEP * 2 * HD), full(1, HD), full(1, HD), full(n_pos, HD), full(n_pos, HD),
+            in_specs=[head_spec(KV_STEP * H4), head_spec(KV_STEP * H3), head_spec(KV_STEP * H2), full(1, HD), full(1, HD), full(n_pos, HD), full(n_pos, HD),
                       pl.BlockSpec(memory_space=pl.ANY)],
-            out_specs=[head_spec(KV_STEP * 2 * HD), head_spec(KV_STEP * HD), head_spec(KV_STEP * HD), full(8, HD), full(8, HD), pl.BlockSpec(memory_space=pl.ANY)],
+            out_specs=[head_spec(KV_STEP * H2), head_spec(KV_STEP * HD), head_spec(KV_STEP * HD), full(8, HD), full(8, HD), pl.BlockSpec(memory_space=pl.ANY)],
             out_shape=[shp(qw), shp(n_kv * HD), shp(n_kv * HD), jax.ShapeDtypeStruct((8, HD), F32), jax.ShapeDtypeStruct((8, HD), F32),
                        jax.ShapeDtypeStruct(d_wo.shape, F32)],
             scratch_shapes=[pltpu.VMEM((KV_STEP, n_pos, HD), F32), pltpu.VMEM((KV_STEP, n_pos, HD), F32)] + reduce_scratch([(qw // 2, dim)] * 2),
-            compiler_params=params(collective_id=1, has_side_effects=True), cost_estimate=cost(10 * n_tok * n_pos * qw, 60e6), name='attn_bwd',
+            compiler_params=params(collective_id=1, has_side_effects=True), name='attn_bwd',
         )(rot, raw, d_o, gq2, gk2, cos_t, sin_t, d_wo)
         h2 = h.reshape(n_tok, dim)
-        d_wq, d_wk, d_wv = (lax.dot_general(h2, d.reshape(n_tok, -1), (((0,), (0,)), ((), ())), preferred_element_type=F32) for d in (dq, dk, dv))
+        d_wq, d_wk, d_wv = (lax.dot_general(h2, d.reshape(n_tok, -1), TN, preferred_element_type=F32) for d in (dq, dk, dv))
         d_wq, d_wk, d_wv, d_hidden, gains = finish(n_dev, (d_wq, d_wk, d_wv), (dq, dk, dv), (w_q, w_k, w_v), x, dy, g2, dgq, dgk)
         gains = gains.reshape(-1)
-        return (y_out, d_hidden, d_wq, d_wk, d_wv, d_wo, gains[:dim], gains[dim:dim + HD], gains[dim + HD:dim + 2 * HD])
+        return (y_out, d_hidden, d_wq, d_wk, d_wv, d_wo, gains[:dim], gains[dim:dim + HD], gains[dim + HD:dim + H2])
 
     return jax.shard_map(local_step, mesh=mesh, in_specs=(seq_spec,) + (replicated,) * 7 + (seq_spec,),
                          out_specs=(seq_spec, seq_spec) + (replicated,) * 7, check_vma=False)

time: 542 us -> 544 us (level)
    unnamed x32 -> x28, local copies, waits for them, and re-layouts: 25.7 us -> 24.9 us
where the time goes in v5:
time: 544 us; the launch traced here: 535 us
  Pallas kernels  450 us (83%)
  matrix products  54.8 us (10%)
  local copies, waits for them, and re-layouts  27.4 us (5%)
    pallas_call x1, Pallas kernels, finish(): pl.pallas_call(functools.partial(tail_kernel, n_dev), in_specs=[hbm] * 11...  197 us
    pallas_call x1, Pallas kernels, local_step(): pl.pallas_call(functools.partial(attn_bwd_kernel, n_dev), grid=(rows, n_k...  97.7 us
    pallas_call x1, Pallas kernels, local_step(): pl.pallas_call(functools.partial(qkv_kernel, n_dev), grid=(n_dev // sb,),...  79.9 us
    pallas_call x1, Pallas kernels, local_step(): pl.pallas_call(functools.partial(attn_fwd_kernel, n_dev), grid=(rows, n_k...  75 us
    dot_general x3, matrix products, local_step(): lax.dot_general(h2, d.reshape(n_tok, -1), TN, preferred_element_type=F32)  28 us
    unnamed x28, local copies, waits for them, and re-layouts  24.9 us
    dot_general x1, matrix products, local_step(): d_wo = lax.dot_general(o2, dy2, TN, preferred_element_type=F32)  15.7 us
    dot_general x1, matrix products, local_step(): lax.dot_general(dy2, w_o, NT, preferred_element_type=F32).astype(BF16)  11.1 us

profile of v5, /device:TPU:0, one launch (start us, length us, event | category | flops | bytes accessed | tf_op | source)
XLA Modules:
  0.0 535.4 jit_solution(17771069855045938673)
XLA Ops:
  0.7 1.0 fusion
  1.7 1.0 pad_maximum_fusion
  2.7 79.9 %qkv.1 = (bf16[8,4,64,1024]{3,2,1,0:T(8,128)(2,1)}, bf16[8,4,64,1024]{3,2,1,0:T(8,128)(2,1)}, bf16[8,4,64,3072]{3,2,1,0:T(8,128)(2,1)}, bf16[8,4,64,4096]{3,2,1,0:T(8,128)(2,1)}, bf16[8,4,64,1024]{3,2,1,0:T(8,128)(2,1)}) custom-call(bf16[32,64,1024]{2,1,0:T(8,128)(2,1)} %hid.1, bf16[32,64,1024]{2,1,0:T(8,128)(2,1)} %dyl.3, f32[1,1024]{1,0:T(1,128)} %bitcast.42, ...), custom_call_target="tpu_custom_call" | custom-call | tf_op jit(solution)/shard_map/qkv/pallas_call | solution.py:597
  82.6 75.0 %attn_fwd.1 = (bf16[8,4,64,2048]{3,2,1,0:T(8,128)(2,1)}, bf16[32,64,1024]{2,1,0:T(8,128)(2,1)}, bf16[8,4,64,1024]{3,2,1,0:T(8,128)(2,1)}) custom-call(bf16[8,4,64,4096]{3,2,1,0:T(8,128)(2,1)} %get-tuple-element.28.rot_ref, bf16[8,4,64,1024]{3,2,1,0:T(8,128)(2,1)} %get-tuple-element.29.x_ref.refs_9_, ...), custom_call_target="tpu_custom_call", output_to_operand_aliasing={{2}: (4, {})} | custom-call | tf_op jit(solution)/shard_map/attn_fwd/pallas_call | solution.py:607
  157.6 0.0 copy-start
  157.6 0.0 copy-start.4
  157.6 15.7 %convolution_bitcast_fusion.1.wo_part = f32[2048,1024]{1,0:T(8,128)} fusion(bf16[8,4,64,2048]{3,2,1,0:T(8,128)(2,1)} %get-tuple-element.35, bf16[8,4,64,1024]{3,2,1,0:T(8,128)(2,1)} %get-tuple-element.34.refs_10_), kind=kOutput, calls=%fused_computation.2 | convolution fusion | flops 8589934592 | bytes 20971520 | tf_op jit(solution)/shard_map/dot_general | solution.py:617
  173.4 11.1 %convolution_convert_fusion = bf16[2048,2048]{1,0:T(8,128)(2,1)} fusion(bf16[2048,1024]{1,0:T(8,128)(2,1)S(1)} %bitcast.36, bf16[2048,1024]{1,0:T(8,128)(2,1)S(1)} %copy-done.4), kind=kOutput, calls=%fused_computation | convolution fusion | flops 8594128896 | bytes 16777216 | tf_op jit(solution)/shard_map/dot_general | solution.py:618
  184.4 97.7 %attn_bwd.1 = (bf16[8,4,64,2048]{3,2,1,0:T(8,128)(2,1)}, bf16[8,4,64,1024]{3,2,1,0:T(8,128)(2,1)}, bf16[8,4,64,1024]{3,2,1,0:T(8,128)(2,1)}, f32[8,128]{1,0:T(8,...) custom-call(bf16[8,4,64,4096]{3,2,1,0:T(8,128)(2,1)} %get-tuple-element.28.rot_ref, ...), custom_call_target="tpu_custom_call" | custom-call | tf_op jit(solution)/shard_map/attn_bwd/pallas_call | solution.py:619
  282.1 0.0 slice-start.2
  282.2 10.2 %convolution_bitcast_fusion.3.refs_1_ = f32[1024,1024]{1,0:T(8,128)} fusion(bf16[8,4,64,1024]{3,2,1,0:T(8,128)(2,1)} %get-tuple-element.32, bf16[8,4,64,1024]{3,2,1,0:T(8,128)(2,1)} %get-tuple-element.37.refs_4_), kind=kOutput, calls=%fused_computation.4 | convolution fusion | flops 4294967296 | bytes 12582912 | tf_op jit(solution)/shard_map/dot_general | solution.py:630
  292.4 6.3 %convolution_bitcast_fusion.2.refs_2_ = f32[1024,1024]{1,0:T(8,128)} fusion(bf16[8,4,64,1024]{3,2,1,0:T(8,128)(2,1)S(1)} %copy-done.6, bf16[8,4,64,1024]{3,2,1,0:T(8,128)(2,1)S(1)} %copy-done.5), kind=kOutput, calls=%fused_computation.3 | convolution fusion | flops 4294967296 | bytes 12582912 | tf_op jit(solution)/shard_map/dot_general | solution.py:630
  298.7 11.5 %convolution_bitcast_fusion.refs_0_ = f32[1024,2048]{1,0:T(8,128)} fusion(bf16[8,4,64,1024]{3,2,1,0:T(8,128)(2,1)S(1)} %copy-done.6, bf16[8,4,64,2048]{3,2,1,0:T(8,128)(2,1)S(1)} %bitcast.41), kind=kOutput, calls=%fused_computation.1 | convolution fusion | flops 8589934592 | bytes 20971520 | tf_op jit(solution)/shard_map/dot_general | solution.py:630
  310.2 197.4 %tail.1 = (f32[1024,2048]{1,0:T(8,128)}, f32[1024,1024]{1,0:T(8,128)}, f32[1024,1024]{1,0:T(8,128)}, bf16[32,64,1024]{2,1,0:T(8,128)(2,1)}, f32[1,1280]{1,0:T(1,128)}) custom-call(f32[1024,2048]{1,0:T(8,128)} %convolution_bitcast_fusion.refs_0_, f32[1024,1024]{1,0:T(8,128)} %convolution_bitcast_fusion.3.refs_1_, ...), custom_call_target="tpu_custom_call" | custom-call | tf_op jit(solution)/shard_map/tail/pallas_call | solution.py:563
  507.6 1.2 slice_bitcast_fusion
  508.8 1.3 slice.18
  510.1 5.2 copy.30
  515.2 5.1 copy.31
  520.3 4.3 copy.32
  524.6 1.0 copy-done.3
  525.5 2.1 copy.33
  527.7 1.9 copy-done.2
  529.6 2.0 copy.34
  531.6 3.4 copy.35
  (21 shorter events, 0.0 us)
Async XLA Ops:
  157.6 15.8 %copy-start = (bf16[8,4,64,1024]{3,2,1,0:T(8,128)(2,1)S(1)}, bf16[8,4,64,1024]{3,2,1,0:T(8,128)(2,1)}, u32[]{:S(2)}) copy-start(bf16[8,4,64,1024]{3,2,1,0:T(8,128)(2,1)} %get-tuple-element.34.refs_10_) | copy-start | bytes 12582916
  157.6 15.8 %copy-start.4 = (bf16[2048,1024]{1,0:T(8,128)(2,1)S(1)}, bf16[2048,1024]{1,0:T(8,128)(2,1)}, u32[]{:S(2)}) copy-start(bf16[2048,1024]{1,0:T(8,128)(2,1)} %wo_ref.1) | copy-start | bytes 12582916
  282.1 10.2 %copy-start.5 = (bf16[8,4,64,1024]{3,2,1,0:T(8,128)(2,1)S(1)}, bf16[8,4,64,1024]{3,2,1,0:T(8,128)(2,1)}, u32[]{:S(2)}) copy-start(bf16[8,4,64,1024]{3,2,1,0:T(8,128)(2,1)} %get-tuple-element.38.refs_5_) | copy-start | bytes 12582916
  282.1 10.2 %copy-start.6 = (bf16[8,4,64,1024]{3,2,1,0:T(8,128)(2,1)S(1)}, bf16[8,4,64,1024]{3,2,1,0:T(8,128)(2,1)}, u32[]{:S(2)}) copy-start(bf16[8,4,64,1024]{3,2,1,0:T(8,128)(2,1)} %get-tuple-element.32) | copy-start | bytes 12582916
  282.1 16.6 %slice-start.2 = ((s8[8388608]{0:T(1024)(128)(4,1)}), s8[4194304]{0:T(1024)(128)(4,1)S(1)}, s32[]{:S(2)}) async-start(s8[8388608]{0:T(1024)(128)(4,1)} %bitcast.40), calls=%async_computation.2 | async-start | bytes 8388608
  292.3 6.4 %slice-start.3 = ((s8[8388608]{0:T(1024)(128)(4,1)}), s8[4194304]{0:T(1024)(128)(4,1)S(1)}, s32[]{:S(2)}) async-start(s8[8388608]{0:T(1024)(128)(4,1)} %bitcast.40), calls=%async_computation.3 | async-start | bytes 8388608
  510.1 10.2 %copy-start.1 = (f32[1024,2048]{1,0:T(8,128)S(1)}, f32[1024,2048]{1,0:T(8,128)}, u32[]{:S(2)}) copy-start(f32[1024,2048]{1,0:T(8,128)} %get-tuple-element.65) | copy-start | bytes 25165828
  515.2 16.3 %slice-start = ((s8[8388608]{0:T(1024)(128)(4,1)}), s8[4194304]{0:T(1024)(128)(4,1)S(1)}, s32[]{:S(2)}) async-start(s8[8388608]{0:T(1024)(128)(4,1)} %bitcast.38), calls=%async_computation | async-start | bytes 8388608
  520.3 5.2 copy-start.3
  520.3 11.3 %slice-start.1 = ((s8[8388608]{0:T(1024)(128)(4,1)}), s8[4194304]{0:T(1024)(128)(4,1)S(1)}, s32[]{:S(2)}) async-start(s8[8388608]{0:T(1024)(128)(4,1)} %bitcast.38), calls=%async_computation.1 | async-start | bytes 8388608
  525.5 4.0 copy-start.2
